TPU v7x, 32 devices: a whole 2x2x4 slice. The times are simulated.
32 devices in a mesh: tensor: 4 (over y, x), dp: 8 (over z, core).
Axes of the slice: x: 2, y: 2, z: 4, core: 2. Of those that a mesh axis runs over, the one named last changes fastest.
Arguments:
- images: bfloat16 [32, 729, 1152], P('dp'), may hold values from -16 to 16
- counts: int32 [8], P('dp'), may hold values from 3 to 4, as said below
- ln1_gain: bfloat16 [1152], replicated, may hold values from 0.099609375 to 1.8984375
- ln1_bias: bfloat16 [1152], replicated, may hold values from -3 to 3
- qkv_weight: bfloat16 [3, 1152, 1152], P(None, None, 'tensor'), may hold values from -1 to 1
- qv_bias: bfloat16 [2, 1152], P(None, 'tensor'), may hold values from -3 to 3
- out_weight: bfloat16 [1152, 1152], P('tensor'), may hold values from -1.5 to 1.5
- out_bias: bfloat16 [1152], replicated, may hold values from -3 to 3
- ln2_gain: bfloat16 [1152], replicated, may hold values from 0.099609375 to 1.8984375
- ln2_bias: bfloat16 [1152], replicated, may hold values from -3 to 3
- fc1_weight: bfloat16 [1152, 4304], P(None, 'tensor'), may hold values from -0.1875 to 0.1875
- fc1_bias: bfloat16 [4304], P('tensor'), may hold values from -3 to 3
- fc2_weight: bfloat16 [4304, 1152], P('tensor'), may hold values from -0.25 to 0.25
- fc2_bias: bfloat16 [1152], replicated, may hold values from -3 to 3
- grad_out: bfloat16 [32, 729, 1152], P('dp'), may hold values from -6 to 6
Outputs:
- block_out: float32 [32, 729, 1152], P('dp', None, 'tensor')
- grad_in: float32 [32, 729, 1152], P('dp', None, 'tensor')
- grad_ln1_gain: float32 [1152], P('tensor')
- grad_ln1_bias: float32 [1152], P('tensor')
- grad_qkv_weight: float32 [3, 1152, 1152], P(None, None, 'tensor')
- grad_qv_bias: float32 [2, 1152], P(None, 'tensor')
- grad_out_weight: float32 [1152, 1152], P('tensor')
- grad_out_bias: float32 [1152], P('tensor')
- grad_ln2_gain: float32 [1152], P('tensor')
- grad_ln2_bias: float32 [1152], P('tensor')
- grad_fc1_weight: float32 [1152, 4304], P(None, 'tensor')
- grad_fc1_bias: float32 [4304], P('tensor')
- grad_fc2_weight: float32 [4304, 1152], P('tensor')
- grad_fc2_bias: float32 [1152], P('tensor')
Inputs may be any that keep to these rules, and one draw needn't show every extreme that they name: `counts`: exactly 6 of the 8 replicas hold 4 live images, the others 4 - 1; a replica's live images fill its first slots.
All inputs are finite; a program needn't handle non-finite values.
Results may differ from a plain program's by a relative error of at most 0.02.
Values may be sent and summed in bfloat16 or wider, within the bound.
A program may use at most 192 MiB of HBM per device.

v0:
```python
import math

import jax
import jax.numpy as jnp
from jax import lax
from jax.sharding import PartitionSpec as P

HD = 72


EPS = 1e-06


def own_columns(values, share_width):
    start = lax.axis_index("tensor") * share_width
    return lax.dynamic_slice_in_dim(values, start, share_width, values.ndim - 1)


def row_mean(values):
    return jnp.mean(values, axis=-1, keepdims=True)


def group_stats(first, second):
    return lax.psum((first, second), "tensor")


def contract_rows(left, right):
    return lax.dot_general(
        left, right, (((0,), (0,)), ((), ())), preferred_element_type=jnp.float32
    )


def contract_cols(left, right):
    return lax.dot_general(
        left, right, (((1,), (1,)), ((), ())), preferred_element_type=jnp.float32
    )


def gelu_tanh(values):
    return jax.nn.gelu(values, approximate=True)


def local(
    images,
    counts,
    ln1_gain,
    ln1_bias,
    qkv_weight,
    qv_bias,
    out_weight,
    out_bias,
    ln2_gain,
    ln2_bias,
    fc1_weight,
    fc1_bias,
    fc2_weight,
    fc2_bias,
    grad_out,
):
    slot_count, length, full_width = images.shape
    share_width = full_width // lax.axis_size("tensor")
    local_width = qkv_weight.shape[2]
    local_heads = local_width // HD
    hidden_width = fc1_weight.shape[1]
    score_scale = 1.0 / math.sqrt(HD)
    gain_one = ln1_gain.astype(jnp.float32)
    shift_one = ln1_bias.astype(jnp.float32)
    gain_two = ln2_gain.astype(jnp.float32)
    shift_two = ln2_bias.astype(jnp.float32)
    bias_out = out_bias.astype(jnp.float32)
    bias_fc1 = fc1_bias.astype(jnp.float32)
    bias_fc2 = fc2_bias.astype(jnp.float32)
    bias_query = qv_bias[0].astype(jnp.float32)
    bias_value = qv_bias[1].astype(jnp.float32)
    live_count = counts[0]

    def to_heads(values):
        return values.reshape(length, local_heads, HD)

    def head_scores(query_heads, key_heads):
        return (
            jnp.einsum("qhd,khd->hqk", query_heads, key_heads, preferred_element_type=jnp.float32)
            * score_scale
        )

    def layer_step(slot_index, loop_state):
        block_acc, input_acc, grads = loop_state
        (
            grad_gain_one,
            grad_shift_one,
            grad_qkv,
            grad_qv,
            grad_out_w,
            grad_out_b,
            grad_gain_two,
            grad_shift_two,
            grad_fc1_w,
            grad_fc1_b,
            grad_fc2_w,
            grad_fc2_b,
        ) = grads
        live_flag = (slot_index < live_count).astype(jnp.float32)
        picture = lax.dynamic_index_in_dim(images, slot_index, 0, keepdims=False).astype(
            jnp.float32
        )
        upstream = (
            lax.dynamic_index_in_dim(grad_out, slot_index, 0, keepdims=False).astype(jnp.float32)
            * live_flag
        )
        upstream_low = upstream.astype(jnp.bfloat16)
        centered = picture - row_mean(picture)
        inv_one = lax.rsqrt(row_mean(centered * centered) + EPS)
        unit_one = centered * inv_one
        normed_one = (unit_one * gain_one + shift_one).astype(jnp.bfloat16)
        query_rows = (
            jnp.dot(normed_one, qkv_weight[0], preferred_element_type=jnp.float32) + bias_query
        ).astype(jnp.bfloat16)
        key_rows = jnp.dot(normed_one, qkv_weight[1], preferred_element_type=jnp.float32).astype(
            jnp.bfloat16
        )
        value_rows = (
            jnp.dot(normed_one, qkv_weight[2], preferred_element_type=jnp.float32) + bias_value
        ).astype(jnp.bfloat16)
        query_heads = to_heads(query_rows)
        key_heads = to_heads(key_rows)
        value_heads = to_heads(value_rows)
        scores = head_scores(query_heads, key_heads)
        row_top = jnp.max(scores, axis=-1, keepdims=True)
        logsum = row_top + jnp.log(jnp.sum(jnp.exp(scores - row_top), axis=-1, keepdims=True))
        probs_low = jnp.exp(scores - logsum).astype(jnp.bfloat16)
        mixed = jnp.einsum(
            "hqk,khd->qhd", probs_low, value_heads, preferred_element_type=jnp.float32
        )
        mixed = mixed.reshape(length, local_width).astype(jnp.bfloat16)
        partial_out = jnp.dot(mixed, out_weight, preferred_element_type=jnp.float32).astype(
            jnp.bfloat16
        )
        residual = (
            own_columns(picture, share_width)
            + lax.psum_scatter(partial_out, "tensor", scatter_dimension=1, tiled=True).astype(
                jnp.float32
            )
            + own_columns(bias_out, share_width)
        )
        row_sum, row_square = group_stats(
            jnp.sum(residual, axis=-1), jnp.sum(residual * residual, axis=-1)
        )
        average = row_sum[:, None] / full_width
        inv_two = lax.rsqrt(row_square[:, None] / full_width - average * average + EPS)
        unit_two = (residual - average) * inv_two
        own_normed = (
            unit_two * own_columns(gain_two, share_width) + own_columns(shift_two, share_width)
        ).astype(jnp.bfloat16)
        normed_two = lax.all_gather(own_normed, "tensor", axis=1, tiled=True)
        preact = jnp.dot(normed_two, fc1_weight, preferred_element_type=jnp.float32) + bias_fc1
        activated = gelu_tanh(preact).astype(jnp.bfloat16)
        partial_mlp = jnp.dot(activated, fc2_weight, preferred_element_type=jnp.float32).astype(
            jnp.bfloat16
        )
        block_rows = (
            residual
            + lax.psum_scatter(partial_mlp, "tensor", scatter_dimension=1, tiled=True).astype(
                jnp.float32
            )
            + own_columns(bias_fc2, share_width)
        )
        block_rows = block_rows * live_flag
        grad_fc2_b = grad_fc2_b + own_columns(jnp.sum(upstream, axis=0), share_width)
        grad_fc2_w = grad_fc2_w + contract_rows(activated, upstream_low)
        d_act = contract_cols(upstream_low, fc2_weight)
        gelu_pull = jax.vjp(gelu_tanh, preact)[1]
        d_pre = gelu_pull(d_act)[0].astype(jnp.bfloat16)
        grad_fc1_b = grad_fc1_b + jnp.sum(d_pre.astype(jnp.float32), axis=0)
        grad_fc1_w = grad_fc1_w + contract_rows(normed_two, d_pre)
        back_mlp = contract_cols(d_pre, fc1_weight)
        d_norm_two = lax.psum_scatter(
            back_mlp.astype(jnp.bfloat16), "tensor", scatter_dimension=1, tiled=True
        ).astype(jnp.float32)
        scaled_two = d_norm_two * own_columns(gain_two, share_width)
        sum_plain, sum_cross = group_stats(
            jnp.sum(scaled_two, axis=-1), jnp.sum(scaled_two * unit_two, axis=-1)
        )
        d_residual = own_columns(upstream, share_width) + inv_two * (
            scaled_two
            - sum_plain[:, None] / full_width
            - unit_two * (sum_cross[:, None] / full_width)
        )
        grad_gain_two = grad_gain_two + jnp.sum(d_norm_two * unit_two, axis=0)
        grad_shift_two = grad_shift_two + jnp.sum(d_norm_two, axis=0)
        grad_out_b = grad_out_b + jnp.sum(d_residual, axis=0)
        d_residual_low = lax.all_gather(
            d_residual.astype(jnp.bfloat16), "tensor", axis=1, tiled=True
        )
        grad_out_w = grad_out_w + contract_rows(mixed, d_residual_low)
        d_mixed_heads = to_heads(contract_cols(d_residual_low, out_weight).astype(jnp.bfloat16))
        probs = jnp.exp(head_scores(query_heads, key_heads) - logsum)
        probs_again = probs.astype(jnp.bfloat16)
        d_value = jnp.einsum(
            "hqk,qhd->khd", probs_again, d_mixed_heads, preferred_element_type=jnp.float32
        )
        d_probs = jnp.einsum(
            "qhd,khd->hqk", d_mixed_heads, value_heads, preferred_element_type=jnp.float32
        )
        inner = jnp.sum(probs * d_probs, axis=-1, keepdims=True)
        d_scores = (probs * (d_probs - inner)).astype(jnp.bfloat16)
        d_query = (
            jnp.einsum("hqk,khd->qhd", d_scores, key_heads, preferred_element_type=jnp.float32)
            * score_scale
        )
        d_key = (
            jnp.einsum("hqk,qhd->khd", d_scores, query_heads, preferred_element_type=jnp.float32)
            * score_scale
        )
        d_stack = (
            jnp.stack([d_query, d_key, d_value], axis=1)
            .reshape(length, 3, local_width)
            .astype(jnp.bfloat16)
        )
        grad_qkv = grad_qkv + jnp.einsum(
            "ld,lje->jde", normed_one, d_stack, preferred_element_type=jnp.float32
        )
        bias_sums = jnp.sum(d_stack.astype(jnp.float32), axis=0)
        grad_qv = grad_qv + jnp.stack([bias_sums[0], bias_sums[2]])
        back_attn = jnp.einsum(
            "lje,jde->ld", d_stack, qkv_weight, preferred_element_type=jnp.float32
        )
        d_norm_one = lax.psum_scatter(
            back_attn.astype(jnp.bfloat16), "tensor", scatter_dimension=1, tiled=True
        ).astype(jnp.float32)
        own_unit = own_columns(unit_one, share_width)
        scaled_one = d_norm_one * own_columns(gain_one, share_width)
        plain_one, cross_one = group_stats(
            jnp.sum(scaled_one, axis=-1), jnp.sum(scaled_one * own_unit, axis=-1)
        )
        d_input = d_residual + inv_one * (
            scaled_one
            - plain_one[:, None] / full_width
            - own_unit * (cross_one[:, None] / full_width)
        )
        grad_gain_one = grad_gain_one + jnp.sum(d_norm_one * own_unit, axis=0)
        grad_shift_one = grad_shift_one + jnp.sum(d_norm_one, axis=0)
        block_acc = lax.dynamic_update_index_in_dim(block_acc, block_rows, slot_index, 0)
        input_acc = lax.dynamic_update_index_in_dim(input_acc, d_input, slot_index, 0)
        new_grads = (
            grad_gain_one,
            grad_shift_one,
            grad_qkv,
            grad_qv,
            grad_out_w,
            grad_out_b,
            grad_gain_two,
            grad_shift_two,
            grad_fc1_w,
            grad_fc1_b,
            grad_fc2_w,
            grad_fc2_b,
        )
        return (block_acc, input_acc, new_grads)

    share_zeros = jnp.zeros((share_width,), jnp.float32)
    start_grads = (
        share_zeros,
        share_zeros,
        jnp.zeros((3, full_width, local_width), jnp.float32),
        jnp.zeros((2, local_width), jnp.float32),
        jnp.zeros((local_width, full_width), jnp.float32),
        share_zeros,
        share_zeros,
        share_zeros,
        jnp.zeros((full_width, hidden_width), jnp.float32),
        jnp.zeros((hidden_width,), jnp.float32),
        jnp.zeros((hidden_width, full_width), jnp.float32),
        share_zeros,
    )
    start_rows = jnp.zeros((slot_count, length, share_width), jnp.float32)
    block_acc, input_acc, grads = lax.fori_loop(
        0, slot_count, layer_step, (start_rows, start_rows, start_grads)
    )
    (
        grad_gain_one,
        grad_shift_one,
        grad_qkv,
        grad_qv,
        grad_out_w,
        grad_out_b,
        grad_gain_two,
        grad_shift_two,
        grad_fc1_w,
        grad_fc1_b,
        grad_fc2_w,
        grad_fc2_b,
    ) = grads
    summed = (
        lax.psum(grad_gain_one.astype(jnp.bfloat16), "dp").astype(jnp.float32),
        lax.psum(grad_shift_one.astype(jnp.bfloat16), "dp").astype(jnp.float32),
        lax.psum(grad_qkv.astype(jnp.bfloat16), "dp").astype(jnp.float32),
        lax.psum(grad_qv.astype(jnp.bfloat16), "dp").astype(jnp.float32),
        lax.psum(grad_out_w.astype(jnp.bfloat16), "dp").astype(jnp.float32),
        lax.psum(grad_out_b.astype(jnp.bfloat16), "dp").astype(jnp.float32),
        lax.psum(grad_gain_two.astype(jnp.bfloat16), "dp").astype(jnp.float32),
        lax.psum(grad_shift_two.astype(jnp.bfloat16), "dp").astype(jnp.float32),
        lax.psum(grad_fc1_w.astype(jnp.bfloat16), "dp").astype(jnp.float32),
        lax.psum(grad_fc1_b.astype(jnp.bfloat16), "dp").astype(jnp.float32),
        lax.psum(grad_fc2_w.astype(jnp.bfloat16), "dp").astype(jnp.float32),
        lax.psum(grad_fc2_b.astype(jnp.bfloat16), "dp").astype(jnp.float32),
    )
    return (
        block_acc,
        input_acc,
        summed[0],
        summed[1],
        summed[2],
        summed[3],
        summed[4],
        summed[5],
        summed[6],
        summed[7],
        summed[8],
        summed[9],
        summed[10],
        summed[11],
    )


def solution(mesh):
    return jax.shard_map(
        local,
        mesh=mesh,
        in_specs=(
            P("dp", None, None),
            P("dp"),
            P(),
            P(),
            P(None, None, "tensor"),
            P(None, "tensor"),
            P("tensor", None),
            P(),
            P(),
            P(),
            P(None, "tensor"),
            P("tensor"),
            P("tensor", None),
            P(),
            P("dp", None, None),
        ),
        out_specs=(
            P("dp", None, "tensor"),
            P("dp", None, "tensor"),
            P("tensor"),
            P("tensor"),
            P(None, None, "tensor"),
            P(None, "tensor"),
            P("tensor", None),
            P("tensor"),
            P("tensor"),
            P("tensor"),
            P(None, "tensor"),
            P("tensor"),
            P("tensor", None),
            P("tensor"),
        ),
        check_vma=False,
    )
```

profile of v0, /device:TPU:0, one launch (start us, length us, event | category | flops | bytes accessed | tf_op | source)
XLA Modules:
  0.0 1362.5 jit_solution(6711157673283328373)
XLA Ops:
  16.7 12.7 copy.34
  29.4 12.7 copy.35
  42.1 1129.5 %while.42 = (s32[]{:T(128)}, f32[4,729,288]{1,2,0:T(8,128)}, f32[4,729,288]{1,2,0:T(8,128)}, f32[288]{0:T(512)}, f32[288]{0:T(512)}, /*index=5*/f32[3,1152,288]{...) while((s32[]{:T(128)}, f32[4,729,288]{1,2,0:T(8,128)}, ...), condition=%wide.region_30.31_spmd.clone, body=%wide.region_0.30_spmd.clone.sunk | while | flops 18614964224 | bytes 394633504 | solution.py:276
  70.5 29.5 %reduce-scatter.5.cloned.1.call-done = bf16[729,288]{0,1:T(8,128)(2,1)} async-done(((bf16[729,1152]{0,1:T(8,128)(2,1)}), bf16[729,288]{0,1:T(8,128)(2,1)}) %reduce-scatter.5.cloned.1.call-update) | async-done | bytes 419920 | tf_op jit(solution)/shard_map/while/body/eval_jaxpr/reduce_scatter | solution.py:140
  101.5 9.1 all-reduce.8
  112.9 31.3 %all-gather.3.cloned.1.call-done = bf16[729,1152]{0,1:T(8,128)(2,1)} async-done(((bf16[729,288]{0,1:T(8,128)(2,1)}), bf16[729,1152]{0,1:T(8,128)(2,1)}) %all-gather.3.cloned.1.call-update) | async-done | bytes 1679632 | tf_op jit(solution)/shard_map/while/body/eval_jaxpr/all_gather | solution.py:154
  149.0 7.7 convert_reduce_fusion.11
  165.4 29.0 %reduce-scatter.9.cloned.1.call-done = bf16[729,288]{0,1:T(8,128)(2,1)} async-done(((bf16[729,1152]{0,1:T(8,128)(2,1)}), bf16[729,288]{0,1:T(8,128)(2,1)}) %reduce-scatter.9.cloned.1.call-update) | async-done | bytes 419920 | tf_op jit(solution)/shard_map/while/body/eval_jaxpr/reduce_scatter | solution.py:176
  196.4 9.1 all-reduce.9
  215.2 6.1 convolution_convert_fusion.17
  221.4 19.9 %all-gather.5.cloned.1.call-done = bf16[729,1152]{0,1:T(8,128)(2,1)} async-done(((bf16[729,288]{0,1:T(8,128)(2,1)}), bf16[729,1152]{0,1:T(8,128)(2,1)}) %all-gather.5.cloned.1.call-update) | async-done | bytes 1679632 | tf_op jit(solution)/shard_map/while/body/eval_jaxpr/all_gather | solution.py:191
  243.7 7.6 multiply_reduce_fusion.9
  251.3 10.4 multiply_convert_fusion.9
  266.8 5.7 convolution_convert_fusion.20
  278.1 6.8 convolution_add_fusion.12
  285.5 6.9 convolution_add_fusion.13
  299.2 6.0 bitcast_add_fusion.3
  305.2 6.9 reduce-scatter.11.cloned.1.call-done
  313.8 9.1 all-reduce.10
  354.3 26.8 %reduce-scatter.5.cloned.1.call-done = bf16[729,288]{0,1:T(8,128)(2,1)} async-done(((bf16[729,1152]{0,1:T(8,128)(2,1)}), bf16[729,288]{0,1:T(8,128)(2,1)}) %reduce-scatter.5.cloned.1.call-update) | async-done | bytes 419920 | tf_op jit(solution)/shard_map/while/body/eval_jaxpr/reduce_scatter | solution.py:140
  382.6 9.1 all-reduce.8
  393.6 31.7 %all-gather.3.cloned.1.call-done = bf16[729,1152]{0,1:T(8,128)(2,1)} async-done(((bf16[729,288]{0,1:T(8,128)(2,1)}), bf16[729,1152]{0,1:T(8,128)(2,1)}) %all-gather.3.cloned.1.call-update) | async-done | bytes 1679632 | tf_op jit(solution)/shard_map/while/body/eval_jaxpr/all_gather | solution.py:154
  430.1 7.7 convert_reduce_fusion.11
  446.5 29.0 %reduce-scatter.9.cloned.1.call-done = bf16[729,288]{0,1:T(8,128)(2,1)} async-done(((bf16[729,1152]{0,1:T(8,128)(2,1)}), bf16[729,288]{0,1:T(8,128)(2,1)}) %reduce-scatter.9.cloned.1.call-update) | async-done | bytes 419920 | tf_op jit(solution)/shard_map/while/body/eval_jaxpr/reduce_scatter | solution.py:176
  477.4 9.1 all-reduce.9
  496.9 6.1 convolution_convert_fusion.17
  503.1 19.2 %all-gather.5.cloned.1.call-done = bf16[729,1152]{0,1:T(8,128)(2,1)} async-done(((bf16[729,288]{0,1:T(8,128)(2,1)}), bf16[729,1152]{0,1:T(8,128)(2,1)}) %all-gather.5.cloned.1.call-update) | async-done | bytes 1679632 | tf_op jit(solution)/shard_map/while/body/eval_jaxpr/all_gather | solution.py:191
  524.8 7.6 multiply_reduce_fusion.9
  532.4 10.3 multiply_convert_fusion.9
  559.2 8.2 convolution_add_fusion.12
  568.1 8.4 convolution_add_fusion.13
  584.7 7.2 bitcast_add_fusion.3
  595.1 9.1 all-reduce.10
  635.3 26.8 %reduce-scatter.5.cloned.1.call-done = bf16[729,288]{0,1:T(8,128)(2,1)} async-done(((bf16[729,1152]{0,1:T(8,128)(2,1)}), bf16[729,288]{0,1:T(8,128)(2,1)}) %reduce-scatter.5.cloned.1.call-update) | async-done | bytes 419920 | tf_op jit(solution)/shard_map/while/body/eval_jaxpr/reduce_scatter | solution.py:140
  663.6 9.1 all-reduce.8
  674.9 31.5 %all-gather.3.cloned.1.call-done = bf16[729,1152]{0,1:T(8,128)(2,1)} async-done(((bf16[729,288]{0,1:T(8,128)(2,1)}), bf16[729,1152]{0,1:T(8,128)(2,1)}) %all-gather.3.cloned.1.call-update) | async-done | bytes 1679632 | tf_op jit(solution)/shard_map/while/body/eval_jaxpr/all_gather | solution.py:154
  711.1 7.7 convert_reduce_fusion.11
  727.5 29.0 %reduce-scatter.9.cloned.1.call-done = bf16[729,288]{0,1:T(8,128)(2,1)} async-done(((bf16[729,1152]{0,1:T(8,128)(2,1)}), bf16[729,288]{0,1:T(8,128)(2,1)}) %reduce-scatter.9.cloned.1.call-update) | async-done | bytes 419920 | tf_op jit(solution)/shard_map/while/body/eval_jaxpr/reduce_scatter | solution.py:176
  758.5 9.1 all-reduce.9
  778.0 6.1 convolution_convert_fusion.17
  784.2 19.2 %all-gather.5.cloned.1.call-done = bf16[729,1152]{0,1:T(8,128)(2,1)} async-done(((bf16[729,288]{0,1:T(8,128)(2,1)}), bf16[729,1152]{0,1:T(8,128)(2,1)}) %all-gather.5.cloned.1.call-update) | async-done | bytes 1679632 | tf_op jit(solution)/shard_map/while/body/eval_jaxpr/all_gather | solution.py:191
  805.8 7.6 multiply_reduce_fusion.9
  813.4 10.4 multiply_convert_fusion.9
  828.9 5.7 convolution_convert_fusion.20
  840.3 8.2 convolution_add_fusion.12
  849.1 8.2 convolution_add_fusion.13
  865.5 7.2 bitcast_add_fusion.3
  875.9 9.1 all-reduce.10
  916.5 26.8 %reduce-scatter.5.cloned.1.call-done = bf16[729,288]{0,1:T(8,128)(2,1)} async-done(((bf16[729,1152]{0,1:T(8,128)(2,1)}), bf16[729,288]{0,1:T(8,128)(2,1)}) %reduce-scatter.5.cloned.1.call-update) | async-done | bytes 419920 | tf_op jit(solution)/shard_map/while/body/eval_jaxpr/reduce_scatter | solution.py:140
  944.8 9.1 all-reduce.8
  955.7 31.7 %all-gather.3.cloned.1.call-done = bf16[729,1152]{0,1:T(8,128)(2,1)} async-done(((bf16[729,288]{0,1:T(8,128)(2,1)}), bf16[729,1152]{0,1:T(8,128)(2,1)}) %all-gather.3.cloned.1.call-update) | async-done | bytes 1679632 | tf_op jit(solution)/shard_map/while/body/eval_jaxpr/all_gather | solution.py:154
  992.2 7.7 convert_reduce_fusion.11
  1008.6 29.0 %reduce-scatter.9.cloned.1.call-done = bf16[729,288]{0,1:T(8,128)(2,1)} async-done(((bf16[729,1152]{0,1:T(8,128)(2,1)}), bf16[729,288]{0,1:T(8,128)(2,1)}) %reduce-scatter.9.cloned.1.call-update) | async-done | bytes 419920 | tf_op jit(solution)/shard_map/while/body/eval_jaxpr/reduce_scatter | solution.py:176
  1039.6 9.1 all-reduce.9
  1059.1 6.1 convolution_convert_fusion.17
  1065.3 19.2 %all-gather.5.cloned.1.call-done = bf16[729,1152]{0,1:T(8,128)(2,1)} async-done(((bf16[729,288]{0,1:T(8,128)(2,1)}), bf16[729,1152]{0,1:T(8,128)(2,1)}) %all-gather.5.cloned.1.call-update) | async-done | bytes 1679632 | tf_op jit(solution)/shard_map/while/body/eval_jaxpr/all_gather | solution.py:191
  1086.9 7.6 multiply_reduce_fusion.9
  1094.5 10.3 multiply_convert_fusion.9
  1121.4 8.2 convolution_add_fusion.12
  1130.3 8.4 convolution_add_fusion.13
  1146.8 7.2 bitcast_add_fusion.3
  1157.2 9.1 all-reduce.10
  1184.1 27.8 %all-reduce.3 = (bf16[288]{0:T(512)(128)(2,1)S(1)}, bf16[288]{0:T(512)(128)(2,1)S(1)}, bf16[2,288]{1,0:T(2,128)(2,1)S(1)}, bf16[288]{0:T(512)(128)(2,1)S(1)}, bf...) all-reduce(bf16[288]{0:T(512)(128)(2,1)S(1)} %convert_element_type., ...), channel_id=1, replica_groups=mesh['tensor'=4,'dp'=8] {'dp'}, use_global_device_ids=true, to_apply=%region_31.32 | all-reduce | flops 3380 | bytes 13520 | tf_op jit(solution)/shard_map/psum | solution.py:294
  1216.5 127.7 %all-reduce.13.cloned.1.call-done = (bf16[3,1152,288]{1,2,0:T(8,128)(2,1)}, bf16[288,1152]{1,0:T(8,128)(2,1)}, bf16[1152,1076]{0,1:T(8,128)(2,1)}, bf16[1076,1152]{1,0:T(8,128)(2,1)}) async-done(((bf16[3,1152,288]{1,2,0:T(8,128)(2,1)}, bf16[288,1152]{1,0:T(8,128)(2,1)}, bf16[1152,1076]{0,1:T(8,128)(2,1)}, bf16[1076,1152]{1,0:T(8,128)(2,1)}), (bf16[3,1152,288]{1,2,0:T(8,128)(2,1)}, ...) | async-done | bytes 7612432 | tf_op jit(solution)/shard_map/psum | solution.py:296
  (640 shorter events, 382.3 us)
Async XLA Ops:
  42.1 9.8 copy-start.41
  42.1 166.6 %copy-start.18 = (f32[1152]{0:T(1024)}, f32[1152]{0:T(1024)S(1)}, u32[]{:S(2)}) copy-start(f32[1152]{0:T(1024)S(1)} %get-tuple-element.1334) | copy-start | bytes 13828 | tf_op jit(solution)/shard_map/while
  42.1 57.8 %reduce-scatter.5.cloned.1.call-start = ((), (), s32[]{:S(2)}) async-start(), calls=%async_computation.5 | async-start | bytes 2211840 | tf_op jit(solution)/shard_map/while/body/eval_jaxpr/reduce_scatter | solution.py:140
  44.0 167.6 %copy-start.15 = (f32[729]{0:T(1024)}, f32[729]{0:T(1024)S(1)}, u32[]{:S(2)}) copy-start(f32[729]{0:T(1024)S(1)} %broadcast_multiply_fusion.11) | copy-start | bytes 8752 | tf_op jit(solution)/shard_map/while
  64.6 79.6 %all-gather.3.cloned.1.call-start = ((), (), s32[]{:S(2)}) async-start(), calls=%async_computation.6 | async-start | bytes 2211840 | tf_op jit(solution)/shard_map/while/body/eval_jaxpr/all_gather | solution.py:154
  111.6 82.7 %reduce-scatter.9.cloned.1.call-start = ((), (), s32[]{:S(2)}) async-start(), calls=%async_computation.8 | async-start | bytes 2211840 | tf_op jit(solution)/shard_map/while/body/eval_jaxpr/reduce_scatter | solution.py:176
  161.7 79.5 %all-gather.5.cloned.1.call-start = ((), (), s32[]{:S(2)}) async-start(), calls=%async_computation.9 | async-start | bytes 2211840 | tf_op jit(solution)/shard_map/while/body/eval_jaxpr/all_gather | solution.py:191
  208.7 84.9 %reduce-scatter.7.cloned.1.call-start = ((), (), s32[]{:S(2)}) async-start(), calls=%async_computation.7 | async-start | bytes 2211840 | tf_op jit(solution)/shard_map/while/body/eval_jaxpr/reduce_scatter | solution.py:162
  221.3 90.8 %reduce-scatter.11.cloned.1.call-start = ((), (), s32[]{:S(2)}) async-start(), calls=%async_computation.10 | async-start | bytes 2211840 | tf_op jit(solution)/shard_map/while/body/eval_jaxpr/reduce_scatter | solution.py:227
  299.2 12.9 copy-start.17
  299.2 23.7 %copy-start.30 = (f32[288]{0:T(512)S(1)}, f32[288]{0:T(512)}, u32[]{:S(2)}) copy-start(f32[288]{0:T(512)} %get-tuple-element.1286) | copy-start | bytes 3460 | tf_op jit(solution)/shard_map/while
  299.2 23.7 %copy-start.33 = (f32[288]{0:T(512)S(1)}, f32[288]{0:T(512)}, u32[]{:S(2)}) copy-start(f32[288]{0:T(512)} %get-tuple-element.1285) | copy-start | bytes 3460 | tf_op jit(solution)/shard_map/while
  312.1 13.4 copy-start.19
  312.1 13.4 copy-start.21
  312.1 13.4 copy-start.40
  312.1 13.4 copy-start.42
  325.9 9.8 copy-start.41
  325.9 163.9 %copy-start.18 = (f32[1152]{0:T(1024)}, f32[1152]{0:T(1024)S(1)}, u32[]{:S(2)}) copy-start(f32[1152]{0:T(1024)S(1)} %get-tuple-element.1334) | copy-start | bytes 13828 | tf_op jit(solution)/shard_map/while
  325.9 55.1 %reduce-scatter.5.cloned.1.call-start = ((), (), s32[]{:S(2)}) async-start(), calls=%async_computation.5 | async-start | bytes 2211840 | tf_op jit(solution)/shard_map/while/body/eval_jaxpr/reduce_scatter | solution.py:140
  327.8 165.5 %copy-start.15 = (f32[729]{0:T(1024)}, f32[729]{0:T(1024)S(1)}, u32[]{:S(2)}) copy-start(f32[729]{0:T(1024)S(1)} %broadcast_multiply_fusion.11) | copy-start | bytes 8752 | tf_op jit(solution)/shard_map/while
  348.4 76.9 %all-gather.3.cloned.1.call-start = ((), (), s32[]{:S(2)}) async-start(), calls=%async_computation.6 | async-start | bytes 2211840 | tf_op jit(solution)/shard_map/while/body/eval_jaxpr/all_gather | solution.py:154
  392.7 82.7 %reduce-scatter.9.cloned.1.call-start = ((), (), s32[]{:S(2)}) async-start(), calls=%async_computation.8 | async-start | bytes 2211840 | tf_op jit(solution)/shard_map/while/body/eval_jaxpr/reduce_scatter | solution.py:176
  442.8 79.6 %all-gather.5.cloned.1.call-start = ((), (), s32[]{:S(2)}) async-start(), calls=%async_computation.9 | async-start | bytes 2211840 | tf_op jit(solution)/shard_map/while/body/eval_jaxpr/all_gather | solution.py:191
  489.8 88.6 %reduce-scatter.7.cloned.1.call-start = ((), (), s32[]{:S(2)}) async-start(), calls=%async_computation.7 | async-start | bytes 2211840 | tf_op jit(solution)/shard_map/while/body/eval_jaxpr/reduce_scatter | solution.py:162
  503.1 90.2 %reduce-scatter.11.cloned.1.call-start = ((), (), s32[]{:S(2)}) async-start(), calls=%async_computation.10 | async-start | bytes 2211840 | tf_op jit(solution)/shard_map/while/body/eval_jaxpr/reduce_scatter | solution.py:227
  568.1 9.0 copy-start.25
  584.6 19.5 %copy-start.30 = (f32[288]{0:T(512)S(1)}, f32[288]{0:T(512)}, u32[]{:S(2)}) copy-start(f32[288]{0:T(512)} %get-tuple-element.1286) | copy-start | bytes 3460 | tf_op jit(solution)/shard_map/while
  584.6 19.5 %copy-start.33 = (f32[288]{0:T(512)S(1)}, f32[288]{0:T(512)}, u32[]{:S(2)}) copy-start(f32[288]{0:T(512)} %get-tuple-element.1285) | copy-start | bytes 3460 | tf_op jit(solution)/shard_map/while
  593.3 13.4 copy-start.19
  593.3 13.4 copy-start.21
  593.3 13.4 copy-start.40
  593.4 13.4 copy-start.42
  607.0 9.8 copy-start.41
  607.0 163.9 %copy-start.18 = (f32[1152]{0:T(1024)}, f32[1152]{0:T(1024)S(1)}, u32[]{:S(2)}) copy-start(f32[1152]{0:T(1024)S(1)} %get-tuple-element.1334) | copy-start | bytes 13828 | tf_op jit(solution)/shard_map/while
  607.0 55.1 %reduce-scatter.5.cloned.1.call-start = ((), (), s32[]{:S(2)}) async-start(), calls=%async_computation.5 | async-start | bytes 2211840 | tf_op jit(solution)/shard_map/while/body/eval_jaxpr/reduce_scatter | solution.py:140
  608.9 165.5 %copy-start.15 = (f32[729]{0:T(1024)}, f32[729]{0:T(1024)S(1)}, u32[]{:S(2)}) copy-start(f32[729]{0:T(1024)S(1)} %broadcast_multiply_fusion.11) | copy-start | bytes 8752 | tf_op jit(solution)/shard_map/while
  629.5 76.9 %all-gather.3.cloned.1.call-start = ((), (), s32[]{:S(2)}) async-start(), calls=%async_computation.6 | async-start | bytes 2211840 | tf_op jit(solution)/shard_map/while/body/eval_jaxpr/all_gather | solution.py:154
  673.8 82.7 %reduce-scatter.9.cloned.1.call-start = ((), (), s32[]{:S(2)}) async-start(), calls=%async_computation.8 | async-start | bytes 2211840 | tf_op jit(solution)/shard_map/while/body/eval_jaxpr/reduce_scatter | solution.py:176
  723.9 79.6 %all-gather.5.cloned.1.call-start = ((), (), s32[]{:S(2)}) async-start(), calls=%async_computation.9 | async-start | bytes 2211840 | tf_op jit(solution)/shard_map/while/body/eval_jaxpr/all_gather | solution.py:191
  770.8 88.4 %reduce-scatter.7.cloned.1.call-start = ((), (), s32[]{:S(2)}) async-start(), calls=%async_computation.7 | async-start | bytes 2211840 | tf_op jit(solution)/shard_map/while/body/eval_jaxpr/reduce_scatter | solution.py:162
  784.1 90.1 %reduce-scatter.11.cloned.1.call-start = ((), (), s32[]{:S(2)}) async-start(), calls=%async_computation.10 | async-start | bytes 2211840 | tf_op jit(solution)/shard_map/while/body/eval_jaxpr/reduce_scatter | solution.py:227
  865.5 19.6 %copy-start.30 = (f32[288]{0:T(512)S(1)}, f32[288]{0:T(512)}, u32[]{:S(2)}) copy-start(f32[288]{0:T(512)} %get-tuple-element.1286) | copy-start | bytes 3460 | tf_op jit(solution)/shard_map/while
  865.5 19.6 %copy-start.33 = (f32[288]{0:T(512)S(1)}, f32[288]{0:T(512)}, u32[]{:S(2)}) copy-start(f32[288]{0:T(512)} %get-tuple-element.1285) | copy-start | bytes 3460 | tf_op jit(solution)/shard_map/while
  874.2 13.4 copy-start.19
  874.2 13.4 copy-start.21
  874.2 13.4 copy-start.40
  874.2 13.4 copy-start.42
  888.1 9.8 copy-start.41
  888.1 163.9 %copy-start.18 = (f32[1152]{0:T(1024)}, f32[1152]{0:T(1024)S(1)}, u32[]{:S(2)}) copy-start(f32[1152]{0:T(1024)S(1)} %get-tuple-element.1334) | copy-start | bytes 13828 | tf_op jit(solution)/shard_map/while
  888.1 55.1 %reduce-scatter.5.cloned.1.call-start = ((), (), s32[]{:S(2)}) async-start(), calls=%async_computation.5 | async-start | bytes 2211840 | tf_op jit(solution)/shard_map/while/body/eval_jaxpr/reduce_scatter | solution.py:140
  890.0 165.5 %copy-start.15 = (f32[729]{0:T(1024)}, f32[729]{0:T(1024)S(1)}, u32[]{:S(2)}) copy-start(f32[729]{0:T(1024)S(1)} %broadcast_multiply_fusion.11) | copy-start | bytes 8752 | tf_op jit(solution)/shard_map/while
  910.6 76.9 %all-gather.3.cloned.1.call-start = ((), (), s32[]{:S(2)}) async-start(), calls=%async_computation.6 | async-start | bytes 2211840 | tf_op jit(solution)/shard_map/while/body/eval_jaxpr/all_gather | solution.py:154
  954.9 82.7 %reduce-scatter.9.cloned.1.call-start = ((), (), s32[]{:S(2)}) async-start(), calls=%async_computation.8 | async-start | bytes 2211840 | tf_op jit(solution)/shard_map/while/body/eval_jaxpr/reduce_scatter | solution.py:176
  1005.0 79.6 %all-gather.5.cloned.1.call-start = ((), (), s32[]{:S(2)}) async-start(), calls=%async_computation.9 | async-start | bytes 2211840 | tf_op jit(solution)/shard_map/while/body/eval_jaxpr/all_gather | solution.py:191
  1051.9 88.6 %reduce-scatter.7.cloned.1.call-start = ((), (), s32[]{:S(2)}) async-start(), calls=%async_computation.7 | async-start | bytes 2211840 | tf_op jit(solution)/shard_map/while/body/eval_jaxpr/reduce_scatter | solution.py:162
  1065.2 90.2 %reduce-scatter.11.cloned.1.call-start = ((), (), s32[]{:S(2)}) async-start(), calls=%async_computation.10 | async-start | bytes 2211840 | tf_op jit(solution)/shard_map/while/body/eval_jaxpr/reduce_scatter | solution.py:227
  1130.2 9.0 copy-start.25
  1146.8 19.5 %copy-start.30 = (f32[288]{0:T(512)S(1)}, f32[288]{0:T(512)}, u32[]{:S(2)}) copy-start(f32[288]{0:T(512)} %get-tuple-element.1286) | copy-start | bytes 3460 | tf_op jit(solution)/shard_map/while
  1146.8 19.5 %copy-start.33 = (f32[288]{0:T(512)S(1)}, f32[288]{0:T(512)}, u32[]{:S(2)}) copy-start(f32[288]{0:T(512)} %get-tuple-element.1285) | copy-start | bytes 3460 | tf_op jit(solution)/shard_map/while
  1155.5 13.4 copy-start.19
  1155.5 13.4 copy-start.21
  1155.5 13.4 copy-start.40
  1155.5 13.4 copy-start.42
  1171.6 172.7 %all-reduce.13.cloned.1.call-start = ((), (), s32[]{:S(2)}) async-start(), calls=%async_computation.4 | async-start | bytes 15261696 | tf_op jit(solution)/shard_map/psum | solution.py:296
  (132 other events, 667.1 us)
Sparse Core Ops, SparseCore 0:
  64.7 35.1 reduce-scatter.4
  111.8 32.4 all-gather.2
  161.9 32.4 reduce-scatter.8
  208.8 32.4 all-gather.4
  244.2 32.4 reduce-scatter.6
  279.6 32.4 reduce-scatter.10
  348.6 32.4 reduce-scatter.4
  392.9 32.4 all-gather.2
  443.0 32.4 reduce-scatter.8
  489.9 32.4 all-gather.4
  525.4 32.4 reduce-scatter.6
  560.8 32.4 reduce-scatter.10
  629.6 32.4 reduce-scatter.4
  673.9 32.4 all-gather.2
  724.0 32.4 reduce-scatter.8
  770.9 32.4 all-gather.4
  806.3 32.4 reduce-scatter.6
  841.7 32.4 reduce-scatter.10
  910.7 32.4 reduce-scatter.4
  955.0 32.4 all-gather.2
  1005.1 32.4 reduce-scatter.8
  1052.0 32.4 all-gather.4
  1087.6 32.4 reduce-scatter.6
  1123.0 32.4 reduce-scatter.10
Sparse Core Ops, SparseCore 1:
  1182.1 162.1 all-reduce.12
where the time goes:
time: 1370 us; the launch traced here: 1360 us
  waiting for transfers between devices  569 us (42%)
  matrix products  335 us (24%)
  other arithmetic  226 us (16%)
  blocking collectives  137 us (10%)
  local copies, waits for them, and re-layouts  69.1 us (5%)
  between operations  15.9 us (1%)
    psum x1, waiting for transfers between devices, local(): lax.psum(grad_qkv.astype(jnp.bfloat16), 'dp').astype(jnp.float32)  128 us
    all_gather x4, waiting for transfers between devices, layer_step(): normed_two = lax.all_gather(own_normed, 'tensor', axis=1, tiled=True)  126 us
    reduce_scatter x4, waiting for transfers between devices, layer_step(): lax.psum_scatter(back_mlp.astype(jnp.bfloat16), 'tensor', scatter_dimensi...  116 us
    reduce_scatter x4, waiting for transfers between devices, layer_step(): lax.psum_scatter(partial_out, 'tensor', scatter_dimension=1, tiled=True)  110 us
    psum x12, blocking collectives, group_stats(): return lax.psum((first, second), 'tensor')  109 us
    all_gather x4, waiting for transfers between devices, layer_step(): lax.all_gather(d_residual.astype(jnp.bfloat16), 'tensor', axis=1, tiled=T...  77.6 us
    dot_general x12, matrix products, contract_rows(): lax.dot_general(left, right, (((0,), (0,)), ((), ())), preferred_element_...  67.7 us
    dot_general x12, matrix products, contract_cols(): lax.dot_general(left, right, (((1,), (1,)), ((), ())), preferred_element_...  55.6 us
  transfers between devices with their start and end apart: 25, of which 21 were waited for; matrix products, arithmetic and copies ran while one was open for 26% of the time, Pallas kernels for 0%

commit v1 on v0

--- a/solution.py
+++ b/solution.py
@@ -3,6 +3,8 @@
 import jax
 import jax.numpy as jnp
 from jax import lax
+from jax.experimental import pallas as pl
+from jax.experimental.pallas import tpu as pltpu
 from jax.sharding import PartitionSpec as P
 
 HD = 72
@@ -322,9 +324,1136 @@
     )
 
 
+LOG2E = math.log2(math.e)
+LN2 = math.log(2.0)
+GELU_A = math.sqrt(2.0 / math.pi)
+GELU_B = 0.044715
+BF = jnp.bfloat16
+F32 = jnp.float32
+QUERY_BLOCK = 256
+MESH = pl.DeviceIdType.MESH
+TURN = {"x": 1, "y": 2}
+OTHER = {"x": "y", "y": "x"}
+SIDE = {"x": 0, "y": 1}
+LANES = ("x", "y")
+ANYWHERE = pl.BlockSpec(memory_space=pl.ANY)
+
+
+def dot_nn(left, right):
+    return lax.dot_general(left, right, (((1,), (0,)), ((), ())), preferred_element_type=F32)
+
+
+def place(bit):
+    if bit == "core":
+        return {"dp": lax.axis_index("dp") ^ 1}
+    return {"tensor": lax.axis_index("tensor") ^ TURN[bit]}
+
+
+def hop(source, target, sems, index, to):
+    return pltpu.make_async_remote_copy(
+        src_ref=source,
+        dst_ref=target,
+        send_sem=sems.at[0, index],
+        recv_sem=sems.at[1, index],
+        device_id=place(to) if isinstance(to, str) else to,
+        device_id_type=MESH,
+    )
+
+
+def line_place():
+    dp = lax.axis_index("dp")
+    return dp // 2, {"dp": lax.rem(dp + 2, 8)}, {"dp": lax.rem(dp + 6, 8)}
+
+
+class GatherRide:
+    partners = ("x", "y", "core")
+
+    def __init__(self, own, steps):
+        _, count, rows, width = own.shape
+        self.inputs = [own]
+        shape = lambda *lead: jax.ShapeDtypeStruct((*lead, count, rows, width), own.dtype)
+        self.outputs = [shape(2), shape(2), shape(), shape()]
+        self.scratch = [pltpu.SemaphoreType.DMA((2, 6 * count))]
+        self.steps = steps
+
+    def events(self, refs):
+        own, near, near_part, far, far_part, sems = refs
+        count = len(LANES)
+        near_hop, far_hop, swap_near, swap_far = {}, [], {}, []
+        for lane, first in enumerate(LANES):
+            for bit in LANES:
+                k = SIDE[bit]
+                near_hop[bit, lane] = hop(
+                    own.at[0, lane], near.at[k, lane], sems, 2 * lane + k, bit
+                )
+                swap_near[bit, lane] = hop(
+                    near.at[k, lane], near_part.at[k, lane], sems, 3 * count + 2 * lane + k, "core"
+                )
+            far_hop.append(
+                hop(near.at[SIDE[first], lane], far.at[lane], sems, 2 * count + lane, OTHER[first])
+            )
+            swap_far.append(hop(far.at[lane], far_part.at[lane], sems, 5 * count + lane, "core"))
+
+        def start():
+            for bit in LANES:
+                for lane in sorted(range(count), key=lambda lane: LANES[lane] != bit):
+                    near_hop[bit, lane].start()
+
+        def forward():
+            for lane, first in enumerate(LANES):
+                near_hop[first, lane].wait_recv()
+                far_hop[lane].start()
+                swap_near[first, lane].start()
+
+        def finish():
+            for lane, first in enumerate(LANES):
+                near_hop[OTHER[first], lane].wait_recv()
+                swap_near[OTHER[first], lane].start()
+            for lane in range(count):
+                far_hop[lane].wait_recv()
+                swap_far[lane].start()
+            for each in near_hop.values():
+                each.wait_send()
+            for each in far_hop:
+                each.wait_send()
+            for each in [*swap_near.values(), *swap_far]:
+                each.wait()
+
+        return [(self.steps[0], start), (self.steps[1], forward), ("end", finish)]
+
+
+class SwapRide:
+    partners = ("core",)
+
+    def __init__(self, *arrays):
+        self.inputs = list(arrays)
+        self.outputs = [jax.ShapeDtypeStruct(a.shape, a.dtype) for a in arrays]
+        self.scratch = [pltpu.SemaphoreType.DMA((2, len(arrays)))]
+
+    def events(self, refs):
+        count = len(self.inputs)
+        hops = [hop(refs[k], refs[count + k], refs[-1], k, "core") for k in range(count)]
+
+        def start():
+            for each in hops:
+                each.start()
+
+        def finish():
+            for each in hops:
+                each.wait()
+
+        return [(0, start), ("end", finish)]
+
+
+class PlaneRide:
+    partners = LANES
+
+    def __init__(self, rows, step):
+        _, count, unit, width = rows.shape
+        self.inputs = [rows]
+        self.outputs = [jax.ShapeDtypeStruct((count, unit, width), rows.dtype)]
+        tile = lambda *lead: pltpu.VMEM((*lead, unit, width), rows.dtype)
+        self.scratch = [
+            tile(count, 2),
+            tile(count, 2),
+            tile(count),
+            pltpu.SemaphoreType.DMA((2, 3 * count)),
+            pltpu.SemaphoreType.DMA((3 * count,)),
+        ]
+        self.step = step
+
+    def events(self, refs):
+        rows, total, base, got, last, sems, local = refs
+        kept = {"x": (0, 2), "y": (0, 1)}
+        gone = {"x": (1, 3), "y": (2, 3)}
+        first_hop, loads, next_hop, stores = {}, {}, [], []
+        for lane, first in enumerate(LANES):
+            for k in range(2):
+                index = 2 * lane + k
+                first_hop[lane, k] = hop(
+                    rows.at[gone[first][k], lane], got.at[lane, k], sems, index, first
+                )
+                loads[lane, k] = pltpu.make_async_copy(
+                    rows.at[kept[first][k], lane], base.at[lane, k], local.at[index]
+                )
+            next_hop.append(hop(base.at[lane, 1], last.at[lane], sems, 4 + lane, OTHER[first]))
+            stores.append(
+                pltpu.make_async_copy(base.at[lane, 0], total.at[lane], local.at[4 + lane])
+            )
+
+        def start():
+            for k in (1, 0):
+                for lane in range(2):
+                    first_hop[lane, k].start()
+                    loads[lane, k].start()
+
+        def forward():
+            for k in (1, 0):
+                for lane in range(2):
+                    loads[lane, k].wait()
+                    first_hop[lane, k].wait_recv()
+                    base[lane, k] += got[lane, k]
+                    if k == 1:
+                        next_hop[lane].start()
+
+        def finish():
+            for lane in range(2):
+                next_hop[lane].wait_recv()
+                base[lane, 0] += last[lane]
+                stores[lane].start()
+            for lane in range(2):
+                next_hop[lane].wait_send()
+                stores[lane].wait()
+            for each in first_hop.values():
+                each.wait_send()
+
+        return [(0, start), (self.step, forward), ("end", finish)]
+
+
+class LineRide:
+    partners = ("line", "core")
+
+    def __init__(self, rows, steps):
+        count, unit, width = rows.shape
+        self.inputs = [rows]
+        self.outputs = [jax.ShapeDtypeStruct(rows.shape, rows.dtype)] * 2
+        tile = pltpu.VMEM((count, unit, width), rows.dtype)
+        self.scratch = [
+            tile,
+            tile,
+            tile,
+            pltpu.SemaphoreType.DMA((2, 4 * count)),
+            pltpu.SemaphoreType.DMA((2 * count,)),
+        ]
+        self.steps = steps
+
+    def events(self, refs):
+        rows, total, other, held, outer, middle, sems, local = refs
+        count = self.inputs[0].shape[0]
+        z, up, down = line_place()
+        is_outer = jnp.logical_or(z == 0, z == 3)
+        is_inner = jnp.logical_not(is_outer)
+        low = z < 2
+        to = {True: (up, up, down), False: (down, down, up)}
+
+        def both(action):
+            pl.when(low)(lambda: action(*to[True]))
+            pl.when(jnp.logical_not(low))(lambda: action(*to[False]))
+
+        load = [pltpu.make_async_copy(rows.at[k], held.at[k], local.at[k]) for k in range(count)]
+        store = [
+            pltpu.make_async_copy(held.at[k], total.at[k], local.at[count + k])
+            for k in range(count)
+        ]
+        inward = lambda k, at: hop(held.at[k], outer.at[k], sems, k, at)
+        across = lambda k, at: hop(held.at[k], middle.at[k], sems, count + k, at)
+        back = lambda k, at: hop(held.at[k], outer.at[k], sems, 2 * count + k, at)
+        swap = [hop(held.at[k], other.at[k], sems, 3 * count + k, "core") for k in range(count)]
+        every = range(count)
+
+        def start():
+            for k in every:
+                load[k].start()
+            for k in every:
+                load[k].wait()
+
+            @pl.when(is_outer)
+            def _():
+                for k in every:
+                    both(lambda a, b, c, k=k: inward(k, a).start())
+
+        def meet():
+            @pl.when(is_inner)
+            def _():
+                for k in every:
+                    inward(k, up).wait_recv()
+                    held[k] += outer[k]
+                    both(lambda a, b, c, k=k: across(k, b).start())
+
+        def leave():
+            @pl.when(is_inner)
+            def _():
+                for k in every:
+                    across(k, up).wait_recv()
+                    across(k, up).wait_send()
+                    held[k] += middle[k]
+                    both(lambda a, b, c, k=k: back(k, c).start())
+                    swap[k].start()
+                    store[k].start()
+
+        def finish():
+            @pl.when(is_outer)
+            def _():
+                for k in every:
+                    inward(k, up).wait_send()
+                    back(k, up).wait_recv()
+                    held[k] = outer[k]
+                    swap[k].start()
+                    store[k].start()
+
+            @pl.when(is_inner)
+            def _():
+                for k in every:
+                    back(k, up).wait_send()
+
+            for k in every:
+                store[k].wait()
+                swap[k].wait()
+
+        return [(0, start), (self.steps[0], meet), (self.steps[1], leave), ("end", finish)]
+
+
+class SpreadRide:
+    partners = ("x", "y", "xy")
+
+    def __init__(self, rows):
+        self.inputs = [rows]
+        self.outputs = [jax.ShapeDtypeStruct((3, *rows.shape[1:]), rows.dtype)]
+        self.scratch = [pltpu.SemaphoreType.DMA((2, 3))]
+
+    def events(self, refs):
+        rows, landed, sems = refs
+        t = lax.axis_index("tensor")
+        hops = [
+            hop(rows.at[t ^ r], landed.at[r - 1], sems, r - 1, {"tensor": t ^ r}) for r in (3, 1, 2)
+        ]
+
+        def start():
+            for each in hops:
+                each.start()
+
+        def finish():
+            for each in hops:
+                each.wait()
+
+        return [(0, start), ("end", finish)]
+
+
+class VectorRide:
+    partners = ("x", "y", "core", "line")
+
+    def __init__(self, rows):
+        self.inputs = [rows]
+        self.outputs = [jax.ShapeDtypeStruct(rows.shape, rows.dtype)]
+        self.scratch = [
+            pltpu.VMEM(rows.shape, rows.dtype),
+            pltpu.VMEM((6, *rows.shape), rows.dtype),
+            pltpu.SemaphoreType.DMA((2, 6)),
+            pltpu.SemaphoreType.DMA((2,)),
+        ]
+
+    def events(self, refs):
+        rows, total, held, got, sems, local = refs
+        z, up, down = line_place()
+        is_outer = jnp.logical_or(z == 0, z == 3)
+        low = z < 2
+        step = lambda k, at: hop(held, got.at[k], sems, k, at)
+
+        def towards(k, first, second):
+            pl.when(low)(lambda: step(k, first).start())
+            pl.when(jnp.logical_not(low))(lambda: step(k, second).start())
+
+        def finish():
+            load = pltpu.make_async_copy(rows, held, local.at[0])
+            load.start()
+            load.wait()
+            for k, bit in enumerate(("core", "x", "y")):
+                step(k, bit).start()
+                step(k, bit).wait()
+                held[...] += got[k]
+
+            @pl.when(is_outer)
+            def _():
+                towards(3, up, down)
+                step(3, up).wait_send()
+                step(5, up).wait_recv()
+                held[...] = got[5]
+
+            @pl.when(jnp.logical_not(is_outer))
+            def _():
+                step(3, up).wait_recv()
+                held[...] += got[3]
+                towards(4, up, down)
+                step(4, up).wait()
+                held[...] += got[4]
+                towards(5, down, up)
+                step(5, up).wait_send()
+
+            store = pltpu.make_async_copy(held, total, local.at[1])
+            store.start()
+            store.wait()
+
+        return [("end", finish)]
+
+
+def carry(body, inputs, in_specs, out_shape, out_specs, steps, name, rides=(), scratch=(), cost=0):
+    ride_in = [array for ride in rides for array in ride.inputs]
+    ride_out = [shape for ride in rides for shape in ride.outputs]
+    ride_scratch = [each for ride in rides for each in ride.scratch]
+    partners = sorted({bit for ride in rides for bit in ride.partners})
+
+    def kernel(*refs):
+        refs = list(refs)
+        take = lambda count: [refs.pop(0) for _ in range(count)]
+        ins, r_ins = take(len(inputs)), take(len(ride_in))
+        outs, r_outs = take(len(out_shape)), take(len(ride_out))
+        own, r_scratch = take(len(scratch)), take(len(ride_scratch))
+        step = pl.program_id(0)
+        events = []
+        for ride in rides:
+            mine = []
+            for pool, kind in ((r_ins, ride.inputs), (r_outs, ride.outputs), (r_scratch, ride.scratch)):
+                mine += [pool.pop(0) for _ in range(len(kind))]
+            events += ride.events(mine)
+
+        if rides:
+
+            @pl.when(step == 0)
+            def _():
+                barrier = pltpu.get_barrier_semaphore()
+                signal = lambda at: pl.semaphore_signal(
+                    barrier, inc=1, device_id=at, device_id_type=MESH
+                )
+                for bit in partners:
+                    if bit == "xy":
+                        signal({"tensor": lax.axis_index("tensor") ^ 3})
+                    elif bit != "line":
+                        signal(place(bit))
+                singles = len([bit for bit in partners if bit != "line"])
+                if "line" in partners:
+                    z, up, down = line_place()
+                    pl.when(z < 3)(lambda: signal(up))
+                    pl.when(z > 0)(lambda: signal(down))
+                    inner = jnp.logical_and(z > 0, z < 3)
+                    pl.when(inner)(lambda: pl.semaphore_wait(barrier, singles + 2))
+                    pl.when(jnp.logical_not(inner))(
+                        lambda: pl.semaphore_wait(barrier, singles + 1)
+                    )
+                else:
+                    pl.semaphore_wait(barrier, singles)
+
+        for when, event in events:
+            if when != "end":
+                pl.when(step == min(when, steps - 1))(event)
+        body(*ins, *outs, *own)
+        for when, event in events:
+            if when == "end":
+                pl.when(step == steps - 1)(event)
+
+    params = {"vmem_limit_bytes": 60 << 20}
+    if rides:
+        carry.count += 1
+        params.update(collective_id=carry.count, has_side_effects=True)
+    results = pl.pallas_call(
+        kernel,
+        grid=(steps,),
+        in_specs=list(in_specs) + [ANYWHERE] * len(ride_in),
+        out_specs=list(out_specs) + [ANYWHERE] * len(ride_out),
+        out_shape=list(out_shape) + ride_out,
+        scratch_shapes=list(scratch) + ride_scratch,
+        compiler_params=pltpu.CompilerParams(**params),
+        cost_estimate=pl.CostEstimate(flops=int(cost), bytes_accessed=1 << 24, transcendentals=0),
+        name=name,
+    )(*inputs, *ride_in)
+    results = list(results)
+    groups = [results[: len(out_shape)]]
+    results = results[len(out_shape) :]
+    for ride in rides:
+        groups.append(results[: len(ride.outputs)])
+        results = results[len(ride.outputs) :]
+    return groups
+
+
+carry.count = 0
+
+
+def whole(array):
+    zeros = (0,) * array.ndim
+    return pl.BlockSpec(array.shape, lambda i: zeros)
+
+
+def shaped(shape, dtype=BF):
+    return jax.ShapeDtypeStruct(shape, dtype)
+
+
+def prepare_body(slot_ref, live_ref, im_ref, go_ref, gain_ref, bias_ref, x_ref, g_ref, n_ref, s_ref):
+    slot = slot_ref[0]
+
+    def pick(ref):
+        values = ref[...].astype(F32)
+        chosen = values[:, 0]
+        for index in range(1, values.shape[1]):
+            chosen = jnp.where(slot == index, values[:, index], chosen)
+        return chosen
+
+    picture = pick(im_ref)
+    centered = picture - row_mean(picture)
+    inverse = lax.rsqrt(row_mean(centered * centered) + EPS)
+    normed = centered * inverse * gain_ref[...] + bias_ref[...]
+    x_ref[...] = picture.T.astype(BF)
+    g_ref[...] = (pick(go_ref) * live_ref[0].astype(F32)).T.astype(BF)
+    n_ref[...] = normed.T.astype(BF)
+    s_ref[0:1, :] = row_mean(picture).T
+    s_ref[1:2, :] = inverse.T
+
+
+def prepare(images, grad_out, slot, live, gain, bias, rides):
+    slots, length, width = images.shape
+    rows = 128
+    scalar = pl.BlockSpec(memory_space=pltpu.SMEM)
+    tokens = pl.BlockSpec((rows, slots, width), lambda i: (i, 0, 0))
+    vector = pl.BlockSpec((1, width), lambda i: (0, 0))
+    return carry(
+        prepare_body,
+        [slot, live, images.transpose(1, 0, 2), grad_out.transpose(1, 0, 2), gain, bias],
+        [scalar, scalar, tokens, tokens, vector, vector],
+        [shaped((width, length))] * 3 + [shaped((2, length), F32)],
+        [pl.BlockSpec((width, rows), lambda i: (0, i))] * 3
+        + [pl.BlockSpec((2, rows), lambda i: (0, i))],
+        pl.cdiv(length, rows),
+        "prepare",
+        rides,
+    )
+
+
+def attend_head(weight, normed, bias, scale, qkv_ref, o_ref, lse_ref):
+    length = normed.shape[1]
+    rows = (dot_nn(weight, normed) + bias) * scale
+    rows = rows.reshape(3, HD, length).astype(BF)
+    qkv_ref[0] = rows
+    queries, keys, values = rows[0], rows[1].T, rows[2]
+    for start in range(0, length, QUERY_BLOCK):
+        block = slice(start, min(start + QUERY_BLOCK, length))
+        scores = dot_nn(keys, queries[:, block])
+        top = jnp.max(scores, axis=0, keepdims=True)
+        weights = jnp.exp2(scores - top)
+        total = jnp.sum(weights, axis=0, keepdims=True)
+        mixed = dot_nn(values, weights.astype(BF))
+        o_ref[0, :, block] = (mixed * (1.0 / total)).astype(BF)
+        lse_ref[0, :, block] = top + jnp.log2(total)
+
+
+def attend(pieces, normed, bias, scale, rides):
+    own, near, near_part, far, far_part = pieces
+    width, length = normed.shape
+    chunk = own.shape[2]
+    rows = 3 * HD
+    heads = 16
+    lane = lambda i: lax.rem(i, 2)
+    half = lambda i: lax.rem(i // 2, 2)
+    clip = lambda i, low, high: jnp.minimum(jnp.maximum(i, low), high)
+
+    def body(own_ref, near_ref, near_part_ref, far_ref, far_part_ref, n_ref, b_ref, s_ref, *outs):
+        step = pl.program_id(0)
+        shard, which = step // 4, half(step)
+        weight = jnp.where(which == 0, near_ref[0, 0, :rows], near_part_ref[0, 0, :rows])
+        last = jnp.where(which == 0, far_ref[0, :rows], far_part_ref[0, :rows])
+        weight = jnp.where(shard == 0, own_ref[0, 0, :rows], jnp.where(shard == 3, last, weight))
+        attend_head(weight, n_ref[...], b_ref[0], s_ref[...], *outs)
+
+    near_spec = pl.BlockSpec(
+        (1, 1, chunk, width), lambda i: (clip(i // 4 - 1, 0, 1), lane(i), 0, 0)
+    )
+    far_spec = pl.BlockSpec((1, chunk, width), lambda i: (lane(i), 0, 0))
+    return carry(
+        body,
+        [own, near, near_part, far, far_part, normed, bias, scale],
+        [
+            pl.BlockSpec((1, 1, chunk, width), lambda i: (half(i), lane(i), 0, 0)),
+            near_spec,
+            near_spec,
+            far_spec,
+            far_spec,
+            whole(normed),
+            pl.BlockSpec((1, rows, 1), lambda i: (i, 0, 0)),
+            whole(scale),
+        ],
+        [
+            shaped((heads, 3, HD, length)),
+            shaped((heads, HD, length)),
+            shaped((heads, 1, length), F32),
+        ],
+        [
+            pl.BlockSpec((1, 3, HD, length), lambda i: (i, 0, 0, 0)),
+            pl.BlockSpec((1, HD, length), lambda i: (i, 0, 0)),
+            pl.BlockSpec((1, 1, length), lambda i: (i, 0, 0)),
+        ],
+        heads,
+        "attend",
+        rides,
+        cost=3e10,
+    )
+
+
+def piece_refs(own, near, near_part, far, far_part):
+    return [
+        own.at[0],
+        own.at[1],
+        near.at[0],
+        near_part.at[0],
+        near.at[1],
+        near_part.at[1],
+        far,
+        far_part,
+    ]
+
+
+def project_out(pieces, mixed, picture, vectors, rides=()):
+    width, length = picture.shape
+    skip = 3 * HD
+
+    def body(own, near, near_part, far, far_part, o_ref, x_ref, v_ref, h_ref, n_ref, s_ref, w_ref, held, sems):
+        refs = piece_refs(own, near, near_part, far, far_part)
+        copies = [
+            pltpu.make_async_copy(
+                ref.at[j, pl.ds(skip, HD)], held.at[2 * p + j], sems.at[2 * p + j]
+            )
+            for p, ref in enumerate(refs)
+            for j in range(2)
+        ]
+        for each in copies:
+            each.start()
+        for each in copies:
+            each.wait()
+        weight = held[...].reshape(width, width)
+        w_ref[...] = weight
+        residual = x_ref[...].astype(F32) + contract_rows(weight, o_ref[...].reshape(width, length))
+        residual = residual + v_ref[:, 2:3]
+        average = jnp.mean(residual, axis=0, keepdims=True)
+        centered = residual - average
+        inverse = lax.rsqrt(jnp.mean(centered * centered, axis=0, keepdims=True) + EPS)
+        h_ref[...] = residual
+        n_ref[...] = (centered * inverse * v_ref[:, 3:4] + v_ref[:, 4:5]).astype(BF)
+        s_ref[0:1, :] = average
+        s_ref[1:2, :] = inverse
+
+    outs = [
+        shaped((width, length), F32),
+        shaped((width, length)),
+        shaped((2, length), F32),
+        shaped((width, width)),
+    ]
+    return carry(
+        body,
+        [*pieces, mixed, picture, vectors],
+        [ANYWHERE] * 5 + [whole(mixed), whole(picture), whole(vectors)],
+        outs,
+        [whole(each) for each in outs],
+        1,
+        "project_out",
+        rides,
+        scratch=[pltpu.VMEM((16, HD, width), BF), pltpu.SemaphoreType.DMA((16,))],
+        cost=2e9,
+    )
+
+
+class Stream:
+    def __init__(self, pieces, pair, rows=None):
+        _, count, unit, width = pieces[0].shape
+        self.pieces = list(pieces)
+        self.group = 2 if pair else 1
+        self.count = count
+        self.rows = unit if rows is None else rows
+        self.steps = 8 // self.group
+        self.scratch = [
+            pltpu.VMEM((2, self.group, count, self.rows, width), BF),
+            pltpu.SemaphoreType.DMA((2, self.group * count)),
+        ]
+
+    def bring(self, refs, held, sems):
+        step = pl.program_id(0)
+        refs = piece_refs(*refs)
+
+        def copies(piece, slot):
+            return [
+                pltpu.make_async_copy(
+                    refs[piece * self.group + g].at[c, pl.ds(0, self.rows)],
+                    held.at[slot, g, c],
+                    sems.at[slot, g * self.count + c],
+                )
+                for g in range(self.group)
+                for c in range(self.count)
+            ]
+
+        def start(piece):
+            for each in copies(piece, piece % 2):
+                each.start()
+
+        pl.when(step == 0)(lambda: start(0))
+        for piece in range(1, self.steps):
+            pl.when(step == piece - 1)(lambda piece=piece: start(piece))
+        slot = lax.rem(step, 2)
+        for each in copies(0, slot):
+            each.wait()
+        return held[slot].reshape(-1, held.shape[-1])
+
+
+def hidden_act(pieces, normed, bias, rides=()):
+    width, length = normed.shape
+    stream = Stream(pieces, False)
+    rows = stream.count * stream.rows
+
+    def body(p0, p1, p2, p3, p4, n_ref, b_ref, act_ref, slope_ref, held, sems):
+        weight = stream.bring((p0, p1, p2, p3, p4), held, sems)
+        preact = dot_nn(weight, n_ref[...]) + b_ref[0]
+        square = preact * preact
+        curve = jnp.tanh(preact * (GELU_A + (GELU_A * GELU_B) * square))
+        rise = 0.5 * (1.0 + curve)
+        act_ref[0] = (preact * rise).astype(BF)
+        inner = GELU_A + (3.0 * GELU_A * GELU_B) * square
+        slope_ref[0] = (rise + (0.5 * preact) * (1.0 - curve * curve) * inner).astype(BF)
+
+    out = shaped((8, rows, length))
+    spec = pl.BlockSpec((1, rows, length), lambda i: (i, 0, 0))
+    return carry(
+        body,
+        [*pieces, normed, bias],
+        [ANYWHERE] * 5 + [whole(normed), pl.BlockSpec((1, rows, 1), lambda i: (i, 0, 0))],
+        [out, out],
+        [spec, spec],
+        8,
+        "hidden_act",
+        rides,
+        scratch=stream.scratch,
+        cost=8e9,
+    )
+
+
+def hidden_back(pieces, upstream, slope, rides=()):
+    width, length = upstream.shape
+    stream = Stream(pieces, False)
+    rows = stream.count * stream.rows
+
+    def body(p0, p1, p2, p3, p4, g_ref, slope_ref, d_ref, sum_ref, held, sems):
+        weight = stream.bring((p0, p1, p2, p3, p4), held, sems)
+        d_pre = (dot_nn(weight, g_ref[...]) * slope_ref[0].astype(F32)).astype(BF)
+        d_ref[0] = d_pre
+        sum_ref[0] = jnp.sum(d_pre.astype(F32), axis=1, keepdims=True)
+
+    spec = pl.BlockSpec((1, rows, length), lambda i: (i, 0, 0))
+    return carry(
+        body,
+        [*pieces, upstream, slope],
+        [ANYWHERE] * 5 + [whole(upstream), spec],
+        [shaped((8, rows, length)), shaped((8, rows, 1), F32)],
+        [spec, pl.BlockSpec((1, rows, 1), lambda i: (i, 0, 0))],
+        8,
+        "hidden_back",
+        rides,
+        scratch=stream.scratch,
+        cost=8e9,
+    )
+
+
+def weight_rows(rows, other, half, lanes, plus=None, rides=(), name="weight_rows"):
+    _, count, length = rows.shape
+    width = other.shape[0]
+    unit = count // lanes
+
+    def body(a_ref, b_ref, *refs):
+        sums = contract_cols(a_ref[0], b_ref[...])
+        if plus is not None:
+            sums = sums + refs[0][0].reshape(count, width).astype(F32)
+        refs[-1][0] = sums.astype(BF).reshape(lanes, unit, width)
+
+    spec = pl.BlockSpec((1, lanes, unit, width), lambda i: (i, 0, 0, 0))
+    extra = [] if plus is None else [plus]
+    return carry(
+        body,
+        [rows, other] + extra,
+        [pl.BlockSpec((1, count, length), lambda i: (2 * i + half, 0, 0)), whole(other)]
+        + [spec] * len(extra),
+        [shaped((4, lanes, unit, width))],
+        [spec],
+        4,
+        name,
+        rides,
+        cost=2 * 4 * count * length * width,
+    )
+
+
+def norm_back(grad, unit_values, inverse, gain):
+    scaled = grad * gain
+    mean = lambda values: jnp.mean(values, axis=0, keepdims=True)
+    return inverse * (scaled - mean(scaled) - unit_values * mean(scaled * unit_values))
+
+
+def stream_back(pieces, values, rows, name, more, more_specs, outs, finish, rides):
+    width = pieces[0].shape[-1]
+    length = values.shape[-1]
+    stream = Stream(pieces, True, rows)
+    depth = 2 * stream.count * stream.rows
+    count_more = len(more)
+
+    def body(p0, p1, p2, p3, p4, d_ref, *refs):
+        step = pl.program_id(0)
+        more_refs, refs = refs[:count_more], refs[count_more:]
+        out_refs, (acc, held, sems) = refs[: len(outs)], refs[len(outs) :]
+        weight = stream.bring((p0, p1, p2, p3, p4), held, sems)
+        part = contract_rows(weight, d_ref[...].reshape(depth, length))
+
+        @pl.when(step == 0)
+        def _():
+            acc[...] = part
+
+        @pl.when(step > 0)
+        def _():
+            acc[...] += part
+
+        @pl.when(step == stream.steps - 1)
+        def _():
+            finish(acc[...], more_refs, out_refs)
+
+    lead = values.shape[0] // stream.steps
+    tail = (0,) * (values.ndim - 1)
+    return carry(
+        body,
+        [*pieces, values, *more],
+        [ANYWHERE] * 5
+        + [pl.BlockSpec((lead, *values.shape[1:]), lambda i: (i, *tail))]
+        + list(more_specs),
+        outs,
+        [whole(each) for each in outs],
+        stream.steps,
+        name,
+        rides,
+        scratch=[pltpu.VMEM((width, length), F32)] + stream.scratch,
+        cost=2 * 4 * depth * width * length,
+    )
+
+
+def attend_back_body(qkv_ref, do_ref, o_ref, lse_ref, d_ref, sum_ref, dk_acc, dv_acc):
+    queries_all, keys_t, values_t = qkv_ref[0, 0], qkv_ref[0, 1], qkv_ref[0, 2]
+    keys = keys_t.T
+    values = values_t.T
+    length = queries_all.shape[1]
+    scale = 1.0 / math.sqrt(HD)
+    for start in range(0, length, QUERY_BLOCK):
+        block = slice(start, min(start + QUERY_BLOCK, length))
+        queries_t = qkv_ref[0, 0, :, block]
+        pull_t = do_ref[0, :, block]
+        delta = jnp.sum(
+            pull_t.astype(F32) * o_ref[0, :, block].astype(F32), axis=0, keepdims=True
+        )
+        probs = jnp.exp2(dot_nn(keys, queries_t) - lse_ref[0, :, block])
+        probs_low = probs.astype(BF)
+        d_probs = dot_nn(values, pull_t)
+        d_scores = (probs * (d_probs - delta)).astype(BF)
+        d_ref[0, 0, :, block] = (dot_nn(keys_t, d_scores) * scale).astype(BF)
+        d_keys = dot_nn(d_scores, queries_t.T)
+        d_values = dot_nn(probs_low, pull_t.T)
+        if start == 0:
+            dk_acc[...] = d_keys
+            dv_acc[...] = d_values
+        else:
+            dk_acc[...] += d_keys
+            dv_acc[...] += d_values
+    d_ref[0, 1] = (dk_acc[...].T * LN2).astype(BF)
+    d_ref[0, 2] = dv_acc[...].T.astype(BF)
+    for k in (0, 2):
+        sum_ref[0, k // 2] = jnp.sum(d_ref[0, k].astype(F32), axis=1, keepdims=True)
+
+
+def attend_back(qkv, pull, mixed, lse, first, heads, rides=()):
+    _, _, _, length = qkv.shape
+    flat = pl.BlockSpec((1, HD, length), lambda n: (n + first, 0, 0))
+    return carry(
+        attend_back_body,
+        [qkv, pull, mixed, lse],
+        [
+            pl.BlockSpec((1, 3, HD, length), lambda n: (n + first, 0, 0, 0)),
+            flat,
+            flat,
+            pl.BlockSpec((1, 1, length), lambda n: (n + first, 0, 0)),
+        ],
+        [shaped((heads, 3, HD, length)), shaped((heads, 2, HD, 1), F32)],
+        [
+            pl.BlockSpec((1, 3, HD, length), lambda n: (n, 0, 0, 0)),
+            pl.BlockSpec((1, 2, HD, 1), lambda n: (n, 0, 0, 0)),
+        ],
+        heads,
+        "attend_back",
+        rides,
+        scratch=[pltpu.VMEM((length, HD), F32), pltpu.VMEM((length, HD), F32)],
+        cost=heads * 2.5e9,
+    )
+
+
+def head_pull(weight, values, rides=()):
+    width, length = values.shape
+    rows = width // 4
+
+    def body(w_ref, d_ref, o_ref):
+        o_ref[...] = dot_nn(w_ref[...], d_ref[...]).reshape(4, HD, length).astype(BF)
+
+    return carry(
+        body,
+        [weight, values],
+        [pl.BlockSpec((rows, width), lambda i: (i, 0)), whole(values)],
+        [shaped((16, HD, length))],
+        [pl.BlockSpec((4, HD, length), lambda i: (i, 0, 0))],
+        4,
+        "head_pull",
+        rides,
+        cost=2e9,
+    )
+
+
+def turned(values, axis, bit):
+    return jnp.where(bit == 1, lax.rev(values, (axis,)), values)
+
+
+def whole_image(
+    images,
+    counts,
+    ln1_gain,
+    ln1_bias,
+    qkv_weight,
+    qv_bias,
+    out_weight,
+    out_bias,
+    ln2_gain,
+    ln2_bias,
+    fc1_weight,
+    fc1_bias,
+    fc2_weight,
+    fc2_bias,
+    grad_out,
+):
+    carry.count = 0
+    slot_count, length, width = images.shape
+    share = width // 4
+    hidden = fc1_weight.shape[1]
+    unit = -(-hidden // 64) * 16
+    half_hidden = 2 * unit
+    place_t = lax.axis_index("tensor")
+    place_d = lax.axis_index("dp")
+    core = lax.rem(place_d, 2)
+    bit_x = lax.rem(place_t, 2)
+    bit_y = place_t // 2
+    block = 3 * HD
+
+    def own_halves(rows):
+        return turned(rows, 0, core)
+
+    qkv_rows = qkv_weight.reshape(3, width, 2, 2, HD).transpose(2, 3, 0, 4, 1)
+    attn_own = own_halves(
+        jnp.concatenate(
+            [qkv_rows.reshape(2, 2, block, width), out_weight.reshape(2, 2, HD, width)], axis=2
+        )
+    )
+    pad = 4 * unit - hidden
+    fc1_own, fc2_own = (
+        own_halves(jnp.pad(rows, ((0, pad), (0, 0))).reshape(2, 2, unit, width))
+        for rows in (fc1_weight.T, fc2_weight)
+    )
+
+    bias_row = jnp.concatenate(
+        [
+            qv_bias.reshape(2, 2, 2, HD).transpose(1, 2, 0, 3).reshape(1, -1),
+            jnp.zeros((1, 2 * half_hidden - 2 * share), BF),
+            fc1_bias[None],
+            jnp.zeros((1, pad), BF),
+        ],
+        axis=1,
+    ).reshape(2, 2 * half_hidden)
+    bias_all = jnp.stack(
+        [bias_row]
+        + [
+            lax.ppermute(bias_row, "tensor", [(i, i ^ turn) for i in range(4)])
+            for turn in (1, 2, 3)
+        ]
+    ).astype(F32)
+    qv_all = turned(bias_all[:, 0, : 2 * share].reshape(4, 2, 2, 2, HD), 1, core)
+    qv_all = qv_all.reshape(16, 2, HD)
+    qkv_bias = jnp.stack([qv_all[:, 0], jnp.zeros_like(qv_all[:, 0]), qv_all[:, 1]], axis=1)
+    qkv_bias = qkv_bias.reshape(16, block, 1)
+    qkv_scale = jnp.repeat(
+        jnp.array([LOG2E / math.sqrt(HD), 1.0, 1.0], F32), HD, total_repeat_length=block
+    )[:, None]
+    hidden_bias = turned(bias_all[:, 1].reshape(4, 2, half_hidden), 1, core)
+    hidden_bias = hidden_bias.reshape(8, half_hidden, 1)
+    vectors = jnp.stack(
+        [ln1_gain, ln1_bias, out_bias, ln2_gain, ln2_bias, fc2_bias, fc2_bias, fc2_bias], axis=1
+    ).astype(F32)
+
+    live = (place_t < counts[0]).astype(jnp.int32)
+    live_scale = live.astype(F32).reshape(1, 1)
+
+    (picture, upstream, normed_one, stats_one), attn_far = prepare(
+        images,
+        grad_out,
+        place_t[None].astype(jnp.int32),
+        live[None],
+        ln1_gain.astype(F32)[None],
+        ln1_bias.astype(F32)[None],
+        [GatherRide(attn_own, (0, 5))],
+    )
+    attn = [attn_own, *attn_far]
+    (qkv, mixed, lse), fc1_far = attend(
+        attn, normed_one, qkv_bias, qkv_scale, [GatherRide(fc1_own, (0, 6))]
+    )
+    fc1 = [fc1_own, *fc1_far]
+    ((residual, normed_two, stats_two, out_all),) = project_out(attn, mixed, picture, vectors)
+    (activated, slope), fc2_far = hidden_act(
+        fc1, normed_two, hidden_bias, [GatherRide(fc2_own, (0, 6))]
+    )
+    fc2 = [fc2_own, *fc2_far]
+
+    ((fc2_part,),) = weight_rows(activated, upstream, 1, 2)
+    (d_pre, hidden_sums), (fc2_got,) = hidden_back(fc2, upstream, slope, [SwapRide(fc2_part)])
+    ((fc2_mine,),) = weight_rows(activated, upstream, 0, 2, fc2_got)
+    (fc1_part,), (fc2_plane,) = weight_rows(d_pre, normed_two, 1, 2, rides=[PlaneRide(fc2_mine, 3)])
+
+    def finish_two(grad, more, outs):
+        h_ref, s_ref, g_ref, v_ref = more
+        d_ref, low_ref, sum_ref = outs
+        units = (h_ref[...] - s_ref[0:1, :]) * s_ref[1:2, :]
+        d_residual = g_ref[...].astype(F32) + norm_back(grad, units, s_ref[1:2, :], v_ref[:, 3:4])
+        d_ref[...] = d_residual
+        low_ref[...] = d_residual.astype(BF)
+        total = lambda values: jnp.sum(values, axis=1, keepdims=True)
+        sum_ref[:, 0:1] = total(d_residual)
+        sum_ref[:, 1:2] = total(grad * units)
+        sum_ref[:, 2:3] = total(grad)
+        sum_ref[:, 3:4] = total(g_ref[...].astype(F32))
+
+    more = [residual, stats_two, upstream, vectors]
+    (d_residual, d_low, sums_two), (fc1_got,), (fc2_mine_sum, fc2_other_sum) = stream_back(
+        fc1,
+        d_pre,
+        None,
+        "back_fc1",
+        more,
+        [whole(each) for each in more],
+        [shaped((width, length), F32), shaped((width, length)), shaped((width, 4), F32)],
+        finish_two,
+        [SwapRide(fc1_part), LineRide(fc2_plane, (2, 3))],
+    )
+    ((fc1_mine,),) = weight_rows(d_pre, normed_two, 0, 2, fc1_got)
+    ((pull,),) = head_pull(out_all, d_low)
+    mixed_rows = mixed.reshape(8, 2 * HD, length)
+    ((out_part,),) = weight_rows(mixed_rows, d_low, 1, 2)
+    (d_qkv_a, qv_sums_a), (fc1_plane,), (out_got,) = attend_back(
+        qkv, pull, mixed, lse, 0, 8, [PlaneRide(fc1_mine, 4), SwapRide(out_part)]
+    )
+    ((out_mine,),) = weight_rows(mixed_rows, d_low, 0, 2, out_got)
+    (d_qkv_b, qv_sums_b), (fc1_mine_sum, fc1_other_sum), (out_plane,) = attend_back(
+        qkv, pull, mixed, lse, 8, 8, [LineRide(fc1_plane, (3, 6)), PlaneRide(out_mine, 4)]
+    )
+    d_qkv = jnp.concatenate([d_qkv_a, d_qkv_b])
+    d_rows = d_qkv.reshape(8, 2 * block, length)
+    ((qkv_part,),) = weight_rows(d_rows, normed_one, 1, 2)
+
+    def finish_block(total, more, outs):
+        h_ref, v_ref, live_ref = more
+        rows = (h_ref[...] + total + v_ref[:, 5:6]) * live_ref[...]
+        outs[0][...] = rows.astype(BF).reshape(4, share, length)
+
+    more = [residual, vectors, live_scale]
+    (block_rows,), (qkv_got,), (out_mine_sum, out_other_sum) = stream_back(
+        fc2,
+        activated,
+        None,
+        "block_out",
+        more,
+        [whole(each) for each in more],
+        [shaped((4, share, length))],
+        finish_block,
+        [SwapRide(qkv_part), LineRide(out_plane, (2, 3))],
+    )
+    ((qkv_mine,),) = weight_rows(d_rows, normed_one, 0, 2, qkv_got)
+
+    def finish_one(grad, more, outs):
+        x_ref, s_ref, d_ref, v_ref = more
+        units = (x_ref[...].astype(F32) - s_ref[0:1, :]) * s_ref[1:2, :]
+        d_input = d_ref[...] + norm_back(grad, units, s_ref[1:2, :], v_ref[:, 0:1])
+        outs[0][...] = d_input.astype(BF).reshape(4, share, length)
+        outs[1][:, 0:1] = jnp.sum(grad * units, axis=1, keepdims=True)
+        outs[1][:, 1:2] = jnp.sum(grad, axis=1, keepdims=True)
+
+    more = [picture, stats_one, d_residual, vectors]
+    (input_rows, sums_one), (qkv_plane,), (block_far,) = stream_back(
+        attn,
+        d_qkv,
+        block,
+        "back_one",
+        more,
+        [whole(each) for each in more],
+        [shaped((4, share, length)), shaped((width, 2), F32)],
+        finish_one,
+        [PlaneRide(qkv_mine, 3), SpreadRide(block_rows)],
+    )
+
+    def absolute(values):
+        values = values.reshape(2, 2, 2, *values.shape[2:])
+        values = turned(turned(turned(values, 2, core), 0, bit_y), 1, bit_x)
+        return values.reshape(4, -1)
+
+    qv_sums = jnp.concatenate([qv_sums_a, qv_sums_b]).reshape(4, 2, -1)
+    wide = jnp.concatenate([sums_one, sums_two], axis=1).reshape(4, share, 6)
+    wide = wide.transpose(0, 2, 1).reshape(4, 6 * share)
+    sums = jnp.concatenate(
+        [wide, absolute(qv_sums), absolute(hidden_sums.reshape(4, 2, half_hidden))], axis=1
+    )
+    sums = jnp.pad(sums, ((0, 0), (0, -sums.shape[1] % 128)))
+
+    def nothing(*refs):
+        refs[-1][...] = jnp.zeros(refs[-1].shape, F32)
+
+    _, (qkv_mine_sum, qkv_other_sum), (input_far,), (sums,) = carry(
+        nothing,
+        [live_scale],
+        [whole(live_scale)],
+        [shaped((8, 128), F32)],
+        [whole(shaped((8, 128), F32))],
+        1,
+        "last",
+        [LineRide(qkv_plane, (0, 0)), SpreadRide(input_rows), VectorRide(sums)],
+    )
+    own = lax.dynamic_index_in_dim(sums, place_t, 0, keepdims=False)
+    own_wide = own[: 6 * share].reshape(6, share)
+    own_qv = own[6 * share : 8 * share].reshape(4, 2, HD).transpose(1, 0, 2).reshape(2, share)
+    own_hidden = own[8 * share : 8 * share + hidden]
+
+    def columns(rows, far):
+        result = jnp.zeros((slot_count, share, length), F32)
+        pieces = [lax.dynamic_index_in_dim(rows, place_t, 0, keepdims=False)]
+        pieces += [far[r] for r in range(3)]
+        for r, piece in enumerate(pieces):
+            result = lax.dynamic_update_index_in_dim(result, piece.astype(F32), place_t ^ r, 0)
+        return result.transpose(0, 2, 1)
+
+    def ordered(mine, other):
+        return jnp.stack([jnp.where(core == 0, mine, other), jnp.where(core == 0, other, mine)])
+
+    fc2_result = ordered(fc2_mine_sum, fc2_other_sum).reshape(-1, width)[:hidden].astype(F32)
+    fc1_result = ordered(fc1_mine_sum, fc1_other_sum).reshape(-1, width)[:hidden].T.astype(F32)
+    out_result = ordered(out_mine_sum, out_other_sum).reshape(share, width).astype(F32)
+    qkv_result = ordered(qkv_mine_sum, qkv_other_sum).reshape(2, 2, 3, HD, width)
+    qkv_result = qkv_result.transpose(2, 4, 0, 1, 3).reshape(3, width, share).astype(F32)
+    return (
+        columns(block_rows, block_far),
+        columns(input_rows, input_far),
+        own_wide[0],
+        own_wide[1],
+        qkv_result,
+        own_qv,
+        out_result,
+        own_wide[2],
+        own_wide[3],
+        own_wide[4],
+        fc1_result,
+        own_hidden,
+        fc2_result,
+        own_wide[5],
+    )
+
+
 def solution(mesh):
+    whole_fits = mesh.shape["tensor"] == 4 and mesh.shape["dp"] == 8
     return jax.shard_map(
-        local,
+        whole_image if whole_fits else local,
         mesh=mesh,
         in_specs=(
             P("dp", None, None),

time: 1370 us -> 706 us (0.52)
  Pallas kernels: 0 us -> 638 us
  waiting for transfers between devices: 569 us -> 0.01 us
  matrix products: 335 us -> 0 us
  other arithmetic: 226 us -> 24.1 us
  blocking collectives: 137 us -> 0 us
  local copies, waits for them, and re-layouts: 69.1 us -> 31.9 us
  between operations: 15.9 us -> 2.11 us
    pallas_call x0 -> x20, Pallas kernels: none -> 638 us  [carry(): pl.pallas_call(kernel, grid=(steps,), in_specs=list(in_specs) + [ANYWHERE...]
    dot_general x80 -> x0, matrix products: 335 us -> none  [the longest x12 67.7 us: contract_rows(): lax.dot_general(left, right, (((0,), (0,)), ((), ())), preferred_element_...]
    reduce_scatter x16 -> x0, waiting for transfers between devices: 237 us -> none  [the longest x4 116 us: layer_step(): lax.psum_scatter(back_mlp.astype(jnp.bfloat16), 'tensor', scatter_dimensi...]
    all_gather x8 -> x0, waiting for transfers between devices: 204 us -> none  [the longest x4 126 us: layer_step(): normed_two = lax.all_gather(own_normed, 'tensor', axis=1, tiled=True)]
    psum x13 -> x0, blocking collectives: 137 us -> none  [the longest x12 109 us: group_stats(): return lax.psum((first, second), 'tensor')]
    psum x1 -> x0, waiting for transfers between devices: 128 us -> none  [local(): lax.psum(grad_qkv.astype(jnp.bfloat16), 'dp').astype(jnp.float32)]
    convert_element_type x52 -> x5, other arithmetic: 107 us -> 7.56 us  [the longest x1 2.59 us: whole_image(): ordered(fc2_mine_sum, fc2_other_sum).reshape(-1, width)[:hidden].astype(F32)]
    reduce_sum x36 -> x0, other arithmetic: 72.3 us -> none  [the longest x8 15.3 us: row_mean(): return jnp.mean(values, axis=-1, keepdims=True)]
  transfers between devices with their start and end apart: 25 -> 3, of which waited for: 21 -> 0; matrix products, arithmetic and copies ran while one was open for 26% -> 2% of each run, Pallas kernels for 0% -> 8%
where the time goes in v1:
time: 706 us; the launch traced here: 701 us
  Pallas kernels  638 us (90%)
  local copies, waits for them, and re-layouts  31.9 us (5%)
  other arithmetic  24.1 us (3%)
    pallas_call x20, Pallas kernels, carry(): pl.pallas_call(kernel, grid=(steps,), in_specs=list(in_specs) + [ANYWHERE...  638 us
  transfers between devices with their start and end apart: 3, of which 0 were waited for; matrix products, arithmetic and copies ran while one was open for 2% of the time, Pallas kernels for 8%

profile of v1, /device:TPU:0, one launch (start us, length us, event | category | flops | bytes accessed | tf_op | source)
XLA Modules:
  0.0 700.9 jit_solution(10296139246150195362)
XLA Ops:
  0.7 0.9 reshape.173
  1.7 0.7 broadcast_in_dim.51
  2.6 3.0 collective-permute-start
  5.6 1.5 collective-permute-start.1
  7.2 1.3 reshape.190.refs_4_
  8.5 0.7 stack.79
  9.2 1.7 copy.52
  11.2 1.5 copy-done.5
  13.1 2.0 reverse_select_fusion.refs_6_.refs_0_
  15.1 3.2 reverse_select_fusion.1
  18.3 0.6 reshape.191.refs_5_
  19.6 0.8 copy.55.refs_7_
  20.7 0.9 convert_element_type.77.refs_7_.refs_9_
  21.7 52.8 %prepare.1 = (bf16[1152,729]{1,0:T(8,128)(2,1)}, bf16[1152,729]{1,0:T(8,128)(2,1)}, bf16[1152,729]{1,0:T(8,128)(2,1)}, f32[2,729]{1,0:T(2,128)}, bf16[2,2,288,11...) custom-call(s32[1]{0:T(128)} %bitcast.7.refs_0_, ...), custom_call_target="tpu_custom_call" | custom-call | bytes 16777216 | tf_op jit(solution)/shard_map/prepare/pallas_call | solution.py:747
  74.8 1.8 reshape.205.refs_6_
  76.9 3.5 reshape.206.refs_6_
  80.4 51.1 %attend.1 = (bf16[16,3,72,729]{3,2,1,0:T(8,128)(2,1)}, bf16[16,72,729]{2,1,0:T(8,128)(2,1)}, f32[16,1,729]{2,1,0:T(1,128)}, bf16[2,2,272,1152]{3,2,1,0:T(8,128)(...) custom-call(bf16[2,2,288,1152]{3,2,1,0:T(8,128)(2,1)} %reverse_select_fusion.r, ...), custom_call_target="tpu_custom_call" | custom-call | flops 30000001024 | bytes 16777216 | tf_op jit(solution)/shard_map/attend/pallas_call | solution.py:747
  131.4 10.2 %project_out.1 = (f32[1152,729]{1,0:T(8,128)}, bf16[1152,729]{1,0:T(8,128)(2,1)}, f32[2,729]{1,0:T(2,128)}, bf16[1152,1152]{1,0:T(8,128)(2,1)}) custom-call(bf16[2,2,288,1152]{3,2,1,0:T(8,128)(2,1)} %reverse_select_fusion.refs_6_.refs_0_, bf16[2,2,288,1152]{3,2,1,0:T(8,128)(2,1)} %get-tuple-element.83.refs_1_, ...), custom_call_target="tpu_custom_call" | custom-call | flops 2000000000 | bytes 16777216 | tf_op jit(solution)/shard_map/project_out/pallas_call | solution.py:747
  141.7 49.6 %hidden_act.1 = (bf16[8,544,729]{2,1,0:T(8,128)(2,1)}, bf16[8,544,729]{2,1,0:T(8,128)(2,1)}, bf16[2,2,272,1152]{3,2,1,0:T(8,128)(2,1)}, bf16[2,2,272,1152]{3,2,1...) custom-call(bf16[2,2,272,1152]{3,2,1,0:T(8,128)(2,1)} %get-tuple-element.156.refs_8_.refs_0_, ...), custom_call_target="tpu_custom_call" | custom-call | flops 8000000000 | bytes 16777216 | tf_op jit(solution)/shard_map/hidden_act/pallas_call | solution.py:747
  191.3 8.5 %weight_rows.8.refs_7_ = bf16[4,2,272,1152]{3,2,1,0:T(8,128)(2,1)} custom-call(bf16[8,544,729]{2,1,0:T(8,128)(2,1)} %get-tuple-element.99.refs_0_.refs_5_, bf16[1152,729]{1,0:T(8,128)(2,1)} %get-tuple-element.103.refs_1_.refs_5_.refs_8_), custom_call_target="tpu_custom_call" | custom-call | flops 3654844416 | bytes 16777216 | tf_op jit(solution)/shard_map/weight_rows/pallas_call | solution.py:747
  199.8 17.4 %hidden_back.1 = (bf16[8,544,729]{2,1,0:T(8,128)(2,1)}, f32[8,544,1]{2,1,0:T(8,128)}, bf16[4,2,272,1152]{3,2,1,0:T(8,128)(2,1)}) custom-call(bf16[2,2,272,1152]{3,2,1,0:T(8,128)(2,1)} %get-tuple-element.157.refs_7_.refs_0_, bf16[2,2,272,1152]{3,2,1,0:T(8,128)(2,1)} %get-tuple-element.95.refs_1_, bf16[2,2,272,1152]{3,2,1,0:T(8,128)(2,1)} %get-tuple-element.96.refs_2_, ...), custom_call_target="tpu_custom_call" | custom-call | flops 8000000000 | bytes 16777216 | tf_op jit(solution)/shard_map/hidden_back/pallas_call | solution.py:747
  217.2 9.2 %weight_rows.9.refs_2_ = bf16[4,2,272,1152]{3,2,1,0:T(8,128)(2,1)} custom-call(bf16[8,544,729]{2,1,0:T(8,128)(2,1)} %get-tuple-element.99.refs_0_.refs_5_, bf16[1152,729]{1,0:T(8,128)(2,1)} %get-tuple-element.103.refs_1_.refs_5_.refs_8_, bf16[4,2,272,1152]{3,2,1,0:T(8,128)(2,1)} %get-tuple-element.107.refs_2_), custom_call_target="tpu_custom_call" | custom-call | flops 3654844416 | bytes 16777216 | tf_op jit(solution)/shard_map/weight_rows/pallas_call | solution.py:747
  226.5 47.4 %weight_rows.10 = (bf16[4,2,272,1152]{3,2,1,0:T(8,128)(2,1)}, bf16[2,272,1152]{2,1,0:T(8,128)(2,1)}) custom-call(bf16[8,544,729]{2,1,0:T(8,128)(2,1)} %get-tuple-element.105.refs_0_.refs_5_, bf16[1152,729]{1,0:T(8,128)(2,1)} %get-tuple-element.94.refs_5_.refs_1_, bf16[4,2,272,1152]{3,2,1,0:T(8,128)(2,1)} %weight_rows.9.refs_2_), custom_call_target="tpu_custom_call" | custom-call | flops 3654844416 | bytes 16777216 | tf_op jit(solution)/shard_map/weight_rows/pallas_call | solution.py:747
  273.9 69.1 %back_fc1.1 = (f32[1152,729]{1,0:T(8,128)}, bf16[1152,729]{1,0:T(8,128)(2,1)}, f32[1152,4]{1,0:T(8,128)}, bf16[4,2,272,1152]{3,2,1,0:T(8,128)(2,1)}, bf16[2,272,...) custom-call(bf16[2,2,272,1152]{3,2,1,0:T(8,128)(2,1)} %get-tuple-element.156.refs_8_.refs_0_, ...), custom_call_target="tpu_custom_call" | custom-call | flops 7309688832 | bytes 16777216 | tf_op jit(solution)/shard_map/back_fc1/pallas_call | solution.py:747
  343.0 1.9 select_bitcast_fusion.1
  344.9 0.3 pad_maximum_fusion.2
  345.1 2.6 slice_convert_fusion
  347.7 9.5 %weight_rows.11.refs_4_ = bf16[4,2,272,1152]{3,2,1,0:T(8,128)(2,1)} custom-call(bf16[8,544,729]{2,1,0:T(8,128)(2,1)} %get-tuple-element.105.refs_0_.refs_5_, bf16[1152,729]{1,0:T(8,128)(2,1)} %get-tuple-element.94.refs_5_.refs_1_, bf16[4,2,272,1152]{3,2,1,0:T(8,128)(2,1)} %get-tuple-element.112.refs_2_), custom_call_target="tpu_custom_call" | custom-call | flops 3654844416 | bytes 16777216 | tf_op jit(solution)/shard_map/weight_rows/pallas_call | solution.py:747
  357.2 5.6 weight_rows.12.refs_5_
  362.8 6.0 head_pull.1.refs_1_
  368.8 46.6 %attend_back.2 = (bf16[8,3,72,729]{3,2,1,0:T(8,128)(2,1)}, f32[8,2,72,1]{3,2,1,0:T(8,128)}, bf16[2,272,1152]{2,1,0:T(8,128)(2,1)}, bf16[4,2,72,1152]{3,2,1,0:T(8,128)(2,1)}) custom-call(bf16[16,3,72,729]{3,2,1,0:T(8,128)(2,1)} %get-tuple-element.101.refs_0_, bf16[16,72,729]{2,1,0:T(8,128)(2,1)} %head_pull.1.refs_1_, ...), custom_call_target="tpu_custom_call" | custom-call | flops 20000000000 | bytes 16777216 | tf_op jit(solution)/shard_map/attend_back/pallas_call | solution.py:747
  415.4 5.8 weight_rows.13.refs_5_
  421.2 69.8 %attend_back.3 = (bf16[8,3,72,729]{3,2,1,0:T(8,128)(2,1)}, f32[8,2,72,1]{3,2,1,0:T(8,128)}, bf16[2,272,1152]{2,1,0:T(8,128)(2,1)}, bf16[2,272,1152]{2,1,0:T(8,128)(2,1)}, bf16[2,72,1152]{2,1,0:T(8,128)(2,1)}) custom-call(bf16[16,3,72,729]{3,2,1,0:T(8,128)(2,1)} %get-tuple-element.101.refs_0_, bf16[16,72,729]{2,1,0:T(8,128)(2,1)} %head_pull.1.refs_1_, ...), custom_call_target="tpu_custom_call" | custom-call | flops 20000000000 | bytes 16777216 | tf_op jit(solution)/shard_map/attend_back/pallas_call | solution.py:747
  491.0 1.9 select_bitcast_fusion.3
  492.9 0.3 pad_maximum_fusion.1
  493.2 2.6 convert_bitcast_fusion
  495.8 0.3 copy-done.2
  496.1 1.7 constant_dynamic-update-slice_fusion.1
  497.8 1.0 copy-done.3
  498.8 1.7 constant_dynamic-update-slice_fusion.refs_5_
  500.4 7.4 %weight_rows.14.refs_9_ = bf16[4,2,216,1152]{3,2,1,0:T(8,128)(2,1)} custom-call(bf16[8,432,729]{2,1,0:T(8,128)(2,1)} %bitcast.21.refs_0_, bf16[1152,729]{1,0:T(8,128)(2,1)} %get-tuple-element.87.refs_5_.refs_1_), custom_call_target="tpu_custom_call" | custom-call | flops 2902376448 | bytes 16777216 | tf_op jit(solution)/shard_map/weight_rows/pallas_call | solution.py:747
  507.8 31.4 %block_out.1 = (bf16[4,288,729]{2,1,0:T(8,128)(2,1)}, bf16[4,2,216,1152]{3,2,1,0:T(8,128)(2,1)}, bf16[2,72,1152]{2,1,0:T(8,128)(2,1)}, bf16[2,72,1152]{2,1,0:T(8,128)(2,1)}) custom-call(bf16[2,2,272,1152]{3,2,1,0:T(8,128)(2,1)} %get-tuple-element.157.refs_7_.refs_0_, bf16[2,2,272,1152]{3,2,1,0:T(8,128)(2,1)} %get-tuple-element.95.refs_1_, ...), custom_call_target="tpu_custom_call" | custom-call | flops 7309688832 | bytes 16777216 | tf_op jit(solution)/shard_map/block_out/pallas_call | solution.py:747
  539.2 1.3 select_bitcast_fusion.5
  540.6 1.2 bitcast_convert_fusion
  541.8 0.7 reduce.6
  543.2 0.2 copy.61
  543.8 8.1 %weight_rows.15.refs_10_ = bf16[4,2,216,1152]{3,2,1,0:T(8,128)(2,1)} custom-call(bf16[8,432,729]{2,1,0:T(8,128)(2,1)} %bitcast.21.refs_0_, bf16[1152,729]{1,0:T(8,128)(2,1)} %get-tuple-element.87.refs_5_.refs_1_, bf16[4,2,216,1152]{3,2,1,0:T(8,128)(2,1)} %get-tuple-element.121.refs_2_), custom_call_target="tpu_custom_call" | custom-call | flops 2902376448 | bytes 16777216 | tf_op jit(solution)/shard_map/weight_rows/pallas_call | solution.py:747
  551.9 61.5 %back_one.1 = (bf16[4,288,729]{2,1,0:T(8,128)(2,1)}, f32[1152,2]{1,0:T(8,128)}, bf16[2,216,1152]{2,1,0:T(8,128)(2,1)}, bf16[3,288,729]{2,1,0:T(8,128)(2,1)}) custom-call(bf16[2,2,288,1152]{3,2,1,0:T(8,128)(2,1)} %reverse_select_fusion.refs_6_.refs_0_, bf16[2,2,288,1152]{3,2,1,0:T(8,128)(2,1)} %get-tuple-element.83.refs_1_, ...), custom_call_target="tpu_custom_call" | custom-call | flops 5804752896 | bytes 16777216 | tf_op jit(solution)/shard_map/back_one/pallas_call | solution.py:747
  613.4 1.3 copy.58
  614.7 0.2 copy.59
  615.3 0.6 pad.17.refs_3_
  615.9 71.3 %last.1 = (f32[8,128]{1,0:T(8,128)}, bf16[2,216,1152]{2,1,0:T(8,128)(2,1)}, bf16[2,216,1152]{2,1,0:T(8,128)(2,1)}, bf16[3,288,729]{2,1,0:T(8,128)(2,1)}, f32[4,3456]{1,0:T(4,128)}) custom-call(f32[1,1]{1,0:T(1,128)} %bitcast.19.refs_8_.refs_0_, bf16[2,216,1152]{2,1,0:T(8,128)(2,1)} %get-tuple-element.124.refs_1_, ...), custom_call_target="tpu_custom_call" | custom-call | bytes 16777216 | tf_op jit(solution)/shard_map/last/pallas_call | solution.py:747
  687.2 1.7 broadcast_select_fusion.1
  688.9 0.3 convert_bitcast_fusion.1
  689.2 2.2 copy.64
  691.4 0.3 broadcast.52.clone.1
  691.6 1.1 convert_dynamic-update-slice_fusion.3
  692.7 0.8 dynamic-slice_reduce_fusion.1
  693.6 0.7 reshape.187
  694.3 1.5 dynamic-slice_reduce_fusion
  695.8 0.3 broadcast.52.clone
  696.1 1.2 convert_dynamic-update-slice_fusion.7
  697.8 2.2 dynamic-slice_reduce_fusion.2
  700.0 0.7 copy-done
  (98 shorter events, 4.1 us)
Async XLA Ops:
  0.6 10.3 %copy-start.4 = (bf16[1076,1152]{1,0:T(8,128)(2,1)S(1)}, bf16[1076,1152]{1,0:T(8,128)(2,1)}, u32[]{:S(2)}) copy-start(bf16[1076,1152]{1,0:T(8,128)(2,1)} %param.30) | copy-start | bytes 7437316
  2.6 71.8 %collective-permute-start = (bf16[2,1088]{1,0:T(2,128)(2,1)S(1)}, bf16[2,1088]{1,0:T(2,128)(2,1)S(1)}, u32[]{:S(2)}, u32[]{:S(2)}) collective-permute-start(bf16[2,1088]{1,0:T(2,128)(2,1)S(1)} %reshape.175), channel_id=1, source_target_pairs={{0,8},{8,0},{16,24},{24,16},{1,9},{9,1},{17,25},{25,17},{2,10},{10... | collective-permute-start | bytes 13064 | tf_op jit(solution)/shard_map/ppermute | solution.py:1263
  5.6 68.9 %collective-permute-start.1 = (bf16[2,1088]{1,0:T(2,128)(2,1)S(1)}, bf16[2,1088]{1,0:T(2,128)(2,1)S(1)}, u32[]{:S(2)}, u32[]{:S(2)}) collective-permute-start(bf16[2,1088]{1,0:T(2,128)(2,1)S(1)} %reshape.175), channel_id=1, source_target_pairs={{0,16},{8,24},{16,0},{24,8},{1,17},{9,25},{17,1},{25,9},{2,18},{10... | collective-permute-start | bytes 13064 | tf_op jit(solution)/shard_map/ppermute | solution.py:1263
  7.1 67.4 %collective-permute-start.2 = (bf16[2,1088]{1,0:T(2,128)(2,1)S(1)}, bf16[2,1088]{1,0:T(2,128)(2,1)S(1)}, u32[]{:S(2)}, u32[]{:S(2)}) collective-permute-start(bf16[2,1088]{1,0:T(2,128)(2,1)S(1)} %reshape.175), channel_id=1, source_target_pairs={{0,24},{8,16},{16,8},{24,0},{1,25},{9,17},{17,9},{25,1},{2,26},{10... | collective-permute-start | bytes 13064 | tf_op jit(solution)/shard_map/ppermute | solution.py:1263
  10.9 1.7 copy-start.5
  11.1 1.7 copy-start.18
  11.1 1.8 copy-start.9
  15.1 3.2 copy-start.13
  15.1 5.2 copy-start.14
  15.1 5.2 copy-start.15
  15.1 5.3 copy-start.16
  15.1 5.3 copy-start.17
  493.2 2.9 copy-start.2
  496.1 2.7 copy-start.3
  539.2 2.6 copy-start.6
  540.6 2.4 copy-start.12
  540.6 2.6 copy-start.11
  551.9 62.8 %copy-start.10 = (f32[1152,4]{1,0:T(8,128)S(1)}, f32[1152,4]{1,0:T(8,128)}, u32[]{:S(2)}) copy-start(f32[1152,4]{1,0:T(8,128)} %get-tuple-element.126) | copy-start | bytes 55300
  694.3 3.0 copy-start.8
  696.1 1.5 copy-start.7
  697.7 2.3 copy-start.1
  697.8 2.9 copy-start

commit v2 on v0

--- a/solution.py
+++ b/solution.py
@@ -3,6 +3,8 @@
 import jax
 import jax.numpy as jnp
 from jax import lax
+from jax.experimental import pallas as pl
+from jax.experimental.pallas import tpu as pltpu
 from jax.sharding import PartitionSpec as P
 
 HD = 72
@@ -12,7 +14,7 @@
 
 
 def own_columns(values, share_width):
-    start = lax.axis_index("tensor") * share_width
+    start = lax.axis_index(TENSOR) * share_width
     return lax.dynamic_slice_in_dim(values, start, share_width, values.ndim - 1)
 
 
@@ -21,7 +23,7 @@
 
 
 def group_stats(first, second):
-    return lax.psum((first, second), "tensor")
+    return lax.psum((first, second), TENSOR)
 
 
 def contract_rows(left, right):
@@ -58,7 +60,7 @@
     grad_out,
 ):
     slot_count, length, full_width = images.shape
-    share_width = full_width // lax.axis_size("tensor")
+    share_width = full_width // lax.axis_size(TENSOR)
     local_width = qkv_weight.shape[2]
     local_heads = local_width // HD
     hidden_width = fc1_weight.shape[1]
@@ -137,7 +139,7 @@
         )
         residual = (
             own_columns(picture, share_width)
-            + lax.psum_scatter(partial_out, "tensor", scatter_dimension=1, tiled=True).astype(
+            + lax.psum_scatter(partial_out, TENSOR, scatter_dimension=1, tiled=True).astype(
                 jnp.float32
             )
             + own_columns(bias_out, share_width)
@@ -151,7 +153,7 @@
         own_normed = (
             unit_two * own_columns(gain_two, share_width) + own_columns(shift_two, share_width)
         ).astype(jnp.bfloat16)
-        normed_two = lax.all_gather(own_normed, "tensor", axis=1, tiled=True)
+        normed_two = lax.all_gather(own_normed, TENSOR, axis=1, tiled=True)
         preact = jnp.dot(normed_two, fc1_weight, preferred_element_type=jnp.float32) + bias_fc1
         activated = gelu_tanh(preact).astype(jnp.bfloat16)
         partial_mlp = jnp.dot(activated, fc2_weight, preferred_element_type=jnp.float32).astype(
@@ -159,7 +161,7 @@
         )
         block_rows = (
             residual
-            + lax.psum_scatter(partial_mlp, "tensor", scatter_dimension=1, tiled=True).astype(
+            + lax.psum_scatter(partial_mlp, TENSOR, scatter_dimension=1, tiled=True).astype(
                 jnp.float32
             )
             + own_columns(bias_fc2, share_width)
@@ -174,7 +176,7 @@
         grad_fc1_w = grad_fc1_w + contract_rows(normed_two, d_pre)
         back_mlp = contract_cols(d_pre, fc1_weight)
         d_norm_two = lax.psum_scatter(
-            back_mlp.astype(jnp.bfloat16), "tensor", scatter_dimension=1, tiled=True
+            back_mlp.astype(jnp.bfloat16), TENSOR, scatter_dimension=1, tiled=True
         ).astype(jnp.float32)
         scaled_two = d_norm_two * own_columns(gain_two, share_width)
         sum_plain, sum_cross = group_stats(
@@ -189,7 +191,7 @@
         grad_shift_two = grad_shift_two + jnp.sum(d_norm_two, axis=0)
         grad_out_b = grad_out_b + jnp.sum(d_residual, axis=0)
         d_residual_low = lax.all_gather(
-            d_residual.astype(jnp.bfloat16), "tensor", axis=1, tiled=True
+            d_residual.astype(jnp.bfloat16), TENSOR, axis=1, tiled=True
         )
         grad_out_w = grad_out_w + contract_rows(mixed, d_residual_low)
         d_mixed_heads = to_heads(contract_cols(d_residual_low, out_weight).astype(jnp.bfloat16))
@@ -225,7 +227,7 @@
             "lje,jde->ld", d_stack, qkv_weight, preferred_element_type=jnp.float32
         )
         d_norm_one = lax.psum_scatter(
-            back_attn.astype(jnp.bfloat16), "tensor", scatter_dimension=1, tiled=True
+            back_attn.astype(jnp.bfloat16), TENSOR, scatter_dimension=1, tiled=True
         ).astype(jnp.float32)
         own_unit = own_columns(unit_one, share_width)
         scaled_one = d_norm_one * own_columns(gain_one, share_width)
@@ -291,18 +293,18 @@
         grad_fc2_b,
     ) = grads
     summed = (
-        lax.psum(grad_gain_one.astype(jnp.bfloat16), "dp").astype(jnp.float32),
-        lax.psum(grad_shift_one.astype(jnp.bfloat16), "dp").astype(jnp.float32),
-        lax.psum(grad_qkv.astype(jnp.bfloat16), "dp").astype(jnp.float32),
-        lax.psum(grad_qv.astype(jnp.bfloat16), "dp").astype(jnp.float32),
-        lax.psum(grad_out_w.astype(jnp.bfloat16), "dp").astype(jnp.float32),
-        lax.psum(grad_out_b.astype(jnp.bfloat16), "dp").astype(jnp.float32),
-        lax.psum(grad_gain_two.astype(jnp.bfloat16), "dp").astype(jnp.float32),
-        lax.psum(grad_shift_two.astype(jnp.bfloat16), "dp").astype(jnp.float32),
-        lax.psum(grad_fc1_w.astype(jnp.bfloat16), "dp").astype(jnp.float32),
-        lax.psum(grad_fc1_b.astype(jnp.bfloat16), "dp").astype(jnp.float32),
-        lax.psum(grad_fc2_w.astype(jnp.bfloat16), "dp").astype(jnp.float32),
-        lax.psum(grad_fc2_b.astype(jnp.bfloat16), "dp").astype(jnp.float32),
+        lax.psum(grad_gain_one.astype(jnp.bfloat16), DP).astype(jnp.float32),
+        lax.psum(grad_shift_one.astype(jnp.bfloat16), DP).astype(jnp.float32),
+        lax.psum(grad_qkv.astype(jnp.bfloat16), DP).astype(jnp.float32),
+        lax.psum(grad_qv.astype(jnp.bfloat16), DP).astype(jnp.float32),
+        lax.psum(grad_out_w.astype(jnp.bfloat16), DP).astype(jnp.float32),
+        lax.psum(grad_out_b.astype(jnp.bfloat16), DP).astype(jnp.float32),
+        lax.psum(grad_gain_two.astype(jnp.bfloat16), DP).astype(jnp.float32),
+        lax.psum(grad_shift_two.astype(jnp.bfloat16), DP).astype(jnp.float32),
+        lax.psum(grad_fc1_w.astype(jnp.bfloat16), DP).astype(jnp.float32),
+        lax.psum(grad_fc1_b.astype(jnp.bfloat16), DP).astype(jnp.float32),
+        lax.psum(grad_fc2_w.astype(jnp.bfloat16), DP).astype(jnp.float32),
+        lax.psum(grad_fc2_b.astype(jnp.bfloat16), DP).astype(jnp.float32),
     )
     return (
         block_acc,
@@ -322,42 +324,1424 @@
     )
 
 
+LOG2E = math.log2(math.e)
+LN2 = math.log(2.0)
+GELU_A = math.sqrt(2.0 / math.pi)
+GELU_B = 0.044715
+BF = jnp.bfloat16
+F32 = jnp.float32
+QUERY_BLOCK = 256
+MESH = pl.DeviceIdType.MESH
+TENSOR, DP = "tensor", "dp"
+X, Y, XY, CORE, LINE = range(5)
+TURN = {X: 1, Y: 2, XY: 3}
+OTHER = {X: Y, Y: X}
+SIDE = {X: 0, Y: 1}
+LANES = (X, Y)
+FC2, FC1, OUT, QKV = range(4)
+INWARD, ACROSS, BACK, SWAP = range(4)
+
+
+class Bag:
+    def __init__(self, **things):
+        self.__dict__.update(things)
+
+    def each(self, action):
+        return Bag(**{name: action(thing) for name, thing in self.__dict__.items()})
+ANYWHERE = pl.BlockSpec(memory_space=pl.ANY)
+
+
+def dot_nn(left, right):
+    return lax.dot_general(left, right, (((1,), (0,)), ((), ())), preferred_element_type=F32)
+
+
+def place(bit):
+    if bit == CORE:
+        return {DP: lax.axis_index(DP) ^ 1}
+    return {TENSOR: lax.axis_index(TENSOR) ^ TURN[bit]}
+
+
+def hop(source, target, sems, index, to):
+    return pltpu.make_async_remote_copy(
+        src_ref=source,
+        dst_ref=target,
+        send_sem=sems.at[0, index],
+        recv_sem=sems.at[1, index],
+        device_id=place(to) if isinstance(to, int) else to,
+        device_id_type=MESH,
+    )
+
+
+def line_place():
+    dp = lax.axis_index(DP)
+    return dp // 2, {DP: lax.rem(dp + 2, 8)}, {DP: lax.rem(dp + 6, 8)}
+
+
+class Program:
+    def __init__(self, name, partners):
+        self.name = name
+        self.partners = partners
+        self.arrays, self.specs, self.shapes, self.scratches = [], [], [], []
+
+    def input(self, array, spec=ANYWHERE):
+        self.arrays.append(array)
+        self.specs.append(spec)
+        return (0, len(self.arrays) - 1)
+
+    def output(self, *shape, dtype=BF):
+        self.shapes.append(jax.ShapeDtypeStruct(shape, dtype))
+        return (1, len(self.shapes) - 1)
+
+    def scratch(self, spec):
+        self.scratches.append(spec)
+        return (2, len(self.scratches) - 1)
+
+    def tile(self, *shape, dtype=BF):
+        return self.scratch(pltpu.VMEM(shape, dtype))
+
+    def sems(self, *shape):
+        return self.scratch(pltpu.SemaphoreType.DMA(shape))
+
+    def call(self, script, collective_id, cost):
+        count_in, count_out = len(self.arrays), len(self.shapes)
+
+        def kernel(*refs):
+            pools = (
+                refs[:count_in],
+                refs[count_in : count_in + count_out],
+                refs[count_in + count_out :],
+            )
+            meet(self.partners)
+            script(lambda handle: pools[handle[0]][handle[1]])
+
+        results = pl.pallas_call(
+            kernel,
+            in_specs=self.specs,
+            out_specs=[ANYWHERE] * count_out,
+            out_shape=self.shapes,
+            scratch_shapes=self.scratches,
+            compiler_params=pltpu.CompilerParams(
+                vmem_limit_bytes=63 << 20, collective_id=collective_id, has_side_effects=True
+            ),
+            cost_estimate=pl.CostEstimate(
+                flops=int(cost), bytes_accessed=1 << 26, transcendentals=0
+            ),
+            name=self.name,
+        )(*self.arrays)
+        return lambda handle: results[handle[1]]
+
+
+def meet(partners):
+    barrier = pltpu.get_barrier_semaphore()
+    signal = lambda at: pl.semaphore_signal(barrier, inc=1, device_id=at, device_id_type=MESH)
+    for bit in partners:
+        if bit == XY:
+            signal({TENSOR: lax.axis_index(TENSOR) ^ 3})
+        elif bit != LINE:
+            signal(place(bit))
+    singles = len([bit for bit in partners if bit != LINE])
+    if LINE in partners:
+        z, up, down = line_place()
+        pl.when(z < 3)(lambda: signal(up))
+        pl.when(z > 0)(lambda: signal(down))
+        inner = jnp.logical_and(z > 0, z < 3)
+        pl.when(inner)(lambda: pl.semaphore_wait(barrier, singles + 2))
+        pl.when(jnp.logical_not(inner))(lambda: pl.semaphore_wait(barrier, singles + 1))
+    else:
+        pl.semaphore_wait(barrier, singles)
+
+
+def phase(steps, body, ins, in_specs, outs, out_specs, events=()):
+    def inner(at, *refs):
+        step = at.index[0]
+        for when, event in events:
+            pl.when(step == when)(event)
+        body(step, *refs)
+
+    pltpu.emit_pipeline(
+        inner, grid=(steps,), in_specs=in_specs, out_specs=out_specs, _explicit_indices=True
+    )(*ins, *outs)
+
+
+def fetch(source, target, sem):
+    copy = pltpu.make_async_copy(source, target, sem)
+    copy.start()
+    return copy
+
+
+def spec(shape, index):
+    return pl.BlockSpec(shape, index)
+
+
+class Gather:
+    def __init__(self, program, own, shape, early=None):
+        _, count, unit, width = shape
+        self.own = own
+        self.early = early
+        self.near = program.output(2, count, unit, width)
+        self.near_part = program.output(2, count, unit, width)
+        self.far = program.output(count, unit, width)
+        self.far_part = program.output(count, unit, width)
+        self.sems = program.sems(2, 12)
+
+    def bind(self, ref):
+        self.refs = Bag(
+            own=ref(self.own),
+            near=ref(self.near),
+            near_part=ref(self.near_part),
+            far=ref(self.far),
+            far_part=ref(self.far_part),
+            sems=ref(self.sems),
+            early=None if self.early is None else ref(self.early),
+        )
+        return self
+
+    def piece(self, shard, part, lane):
+        r = self.refs
+        if shard == 0:
+            return r.own.at[lax.rem(lax.axis_index(DP) + part, 2), lane]
+        if shard == 3:
+            return (r.far_part if part else r.far).at[lane]
+        if self.early is not None and part == 0 and LANES[lane] == LANES[shard - 1]:
+            return r.early.at[lane]
+        return (r.near_part if part else r.near).at[shard - 1, lane]
+
+    def _near(self, bit, lane):
+        r = self.refs
+        k = SIDE[bit]
+        own = self.piece(0, 0, lane)
+        return hop(own, r.near.at[k, lane], r.sems, 2 * lane + k, bit)
+
+    def _far(self, lane):
+        first = LANES[lane]
+        source = self.piece(1 + SIDE[first], 0, lane)
+        return hop(source, self.refs.far.at[lane], self.refs.sems, 4 + lane, OTHER[first])
+
+    def _swap(self, shard, lane):
+        target = self.piece(shard, 1, lane)
+        index = 6 + 2 * (shard - 1) + lane
+        return hop(self.piece(shard, 0, lane), target, self.refs.sems, index, CORE)
+
+    def start(self):
+        for first in (True, False):
+            for lane, bit in enumerate(LANES):
+                if first and self.early is None:
+                    self._near(bit, lane).start()
+                if not first:
+                    self._near(OTHER[bit], lane).start()
+
+    def forward(self):
+        for lane, first in enumerate(LANES):
+            if self.early is None:
+                self._near(first, lane).wait_recv()
+            self._far(lane).start()
+            self._swap(1 + SIDE[first], lane).start()
+
+    def near_here(self):
+        for lane, first in enumerate(LANES):
+            self._near(OTHER[first], lane).wait_recv()
+            self._swap(1 + SIDE[OTHER[first]], lane).start()
+
+    def near_whole(self):
+        for lane in range(2):
+            for shard in (1, 2):
+                self._swap(shard, lane).wait_recv()
+
+    def far_here(self):
+        for lane in range(2):
+            self._far(lane).wait_recv()
+            self._swap(3, lane).start()
+
+    def far_whole(self):
+        for lane in range(2):
+            self._swap(3, lane).wait_recv()
+
+    def drain(self):
+        for lane, first in enumerate(LANES):
+            if self.early is None:
+                self._near(first, lane).wait_send()
+            self._near(OTHER[first], lane).wait_send()
+            self._far(lane).wait_send()
+            for shard in (1, 2, 3):
+                self._swap(shard, lane).wait_send()
+
+
+class Swap:
+    def __init__(self, program, source, shape):
+        self.source = source
+        self.got = program.output(*shape)
+        self.sems = program.sems(2, shape[0])
+
+    def bind(self, ref):
+        self.refs = ref(self.source), ref(self.got), ref(self.sems)
+        return self
+
+    def _hop(self, k):
+        source, got, sems = self.refs
+        return hop(source.at[k], got.at[k], sems, k, CORE)
+
+    def start(self, *parts):
+        for k in parts:
+            self._hop(k).start()
+
+    def wait(self, *parts):
+        for k in parts:
+            self._hop(k).wait()
+
+
+class Plane:
+    KEPT = {X: (0, 2), Y: (0, 1)}
+    GONE = {X: (1, 3), Y: (2, 3)}
+
+    def __init__(self, program, rows, shape):
+        _, count, unit, width = shape
+        self.rows = rows
+        self.base = program.tile(count, 2, unit, width)
+        self.got = program.tile(count, 2, unit, width)
+        self.last = program.tile(count, unit, width)
+        self.sems = program.sems(2, 6)
+        self.local = program.sems(4)
+
+    def bind(self, ref):
+        self.refs = [ref(h) for h in (self.rows, self.base, self.got, self.last, self.sems)]
+        self.loads = ref(self.local)
+        return self
+
+    def _first(self, lane, k):
+        rows, base, got, last, sems = self.refs
+        first = LANES[lane]
+        return hop(
+            rows.at[self.GONE[first][k], lane], got.at[lane, k], sems, 2 * lane + k, first
+        )
+
+    def _load(self, lane, k):
+        rows, base = self.refs[:2]
+        return pltpu.make_async_copy(
+            rows.at[self.KEPT[LANES[lane]][k], lane], base.at[lane, k], self.loads.at[2 * lane + k]
+        )
+
+    def _next(self, lane):
+        rows, base, got, last, sems = self.refs
+        return hop(base.at[lane, 1], last.at[lane], sems, 4 + lane, OTHER[LANES[lane]])
+
+    def send(self, shard):
+        for lane, first in enumerate(LANES):
+            if shard in self.GONE[first]:
+                self._first(lane, self.GONE[first].index(shard)).start()
+            else:
+                self._load(lane, self.KEPT[first].index(shard)).start()
+
+    def start(self):
+        for shard in (3, 1, 2, 0):
+            self.send(shard)
+
+    def forward(self):
+        rows, base, got, last, sems = self.refs
+        for lane in range(2):
+            self._load(lane, 1).wait()
+            self._first(lane, 1).wait_recv()
+            base[lane, 1] += got[lane, 1]
+            self._next(lane).start()
+
+    def settle(self):
+        rows, base, got, last, sems = self.refs
+        for lane in range(2):
+            self._load(lane, 0).wait()
+            self._first(lane, 0).wait_recv()
+            base[lane, 0] += got[lane, 0]
+
+    def finish(self, line):
+        rows, base, got, last, sems = self.refs
+        for lane in range(2):
+            self._next(lane).wait_recv()
+            line.take(lane, base[lane, 0] + last[lane])
+
+    def drain(self):
+        for lane in range(2):
+            self._next(lane).wait_send()
+            for k in range(2):
+                self._first(lane, k).wait_send()
+
+
+class Line:
+    def __init__(self, program, shape):
+        count, unit, width = shape
+        self.total = program.output(*shape)
+        self.other = program.output(*shape)
+        self.held = program.tile(*shape)
+        self.outer = program.tile(*shape)
+        self.middle = program.tile(*shape)
+        self.sems = program.sems(2, 4 * count)
+        self.local = program.sems(count)
+        self.count = count
+
+    def bind(self, ref):
+        self.refs = Bag(
+            total=ref(self.total),
+            other=ref(self.other),
+            held=ref(self.held),
+            outer=ref(self.outer),
+            middle=ref(self.middle),
+            sems=ref(self.sems),
+            local=ref(self.local),
+        )
+        z, up, down = line_place()
+        self.up, self.down = up, down
+        self.is_outer = jnp.logical_or(z == 0, z == 3)
+        self.is_inner = jnp.logical_not(self.is_outer)
+        self.low = z < 2
+        return self
+
+    def _hop(self, kind, k, at):
+        r = self.refs
+        target = (r.outer, r.middle, r.outer, r.other)[kind]
+        return hop(r.held.at[k], target.at[k], r.sems, kind * self.count + k, at)
+
+    def _store(self, k):
+        r = self.refs
+        return pltpu.make_async_copy(r.held.at[k], r.total.at[k], r.local.at[k])
+
+    def _send(self, kind, k):
+        if kind == BACK:
+            low, high = self.down, self.up
+        else:
+            low, high = self.up, self.down
+        pl.when(self.low)(lambda: self._hop(kind, k, low).start())
+        pl.when(jnp.logical_not(self.low))(lambda: self._hop(kind, k, high).start())
+
+    def take(self, k, values):
+        self.refs.held[k] = values
+        pl.when(self.is_outer)(lambda: self._send(INWARD, k))
+
+    def meet(self, k):
+        r = self.refs
+
+        @pl.when(self.is_inner)
+        def _():
+            self._hop(INWARD, k, self.up).wait_recv()
+            r.held[k] += r.outer[k]
+            self._send(ACROSS, k)
+
+    def leave(self, k):
+        r = self.refs
+
+        @pl.when(self.is_inner)
+        def _():
+            self._hop(ACROSS, k, self.up).wait()
+            r.held[k] += r.middle[k]
+            self._send(BACK, k)
+            self._hop(SWAP, k, CORE).start()
+            self._store(k).start()
+
+    def finish(self, k):
+        r = self.refs
+
+        @pl.when(self.is_outer)
+        def _():
+            self._hop(INWARD, k, self.up).wait_send()
+            self._hop(BACK, k, self.up).wait_recv()
+            r.held[k] = r.outer[k]
+            self._hop(SWAP, k, CORE).start()
+            self._store(k).start()
+
+        pl.when(self.is_inner)(lambda: self._hop(BACK, k, self.up).wait_send())
+        self._store(k).wait()
+        self._hop(SWAP, k, CORE).wait()
+
+
+class Spread:
+    def __init__(self, program, rows, shape):
+        self.rows = rows
+        self.landed = program.output(3, *shape[1:])
+        self.sems = program.sems(2, 3)
+
+    def bind(self, ref):
+        self.refs = ref(self.rows), ref(self.landed), ref(self.sems)
+        return self
+
+    def _hop(self, r):
+        rows, landed, sems = self.refs
+        to = lax.axis_index(TENSOR) ^ r
+        return hop(rows.at[to], landed.at[r - 1], sems, r - 1, {TENSOR: to})
+
+    def start(self):
+        for r in (3, 1, 2):
+            self._hop(r).start()
+
+    def finish(self):
+        for r in (1, 2, 3):
+            self._hop(r).wait()
+
+
+class Vectors:
+    def __init__(self, program, shape):
+        self.total = program.output(*shape, dtype=F32)
+        self.held = program.tile(*shape, dtype=F32)
+        self.got = program.tile(6, *shape, dtype=F32)
+        self.sems = program.sems(2, 6)
+        self.local = program.sems(1)
+
+    def bind(self, ref):
+        self.refs = Bag(
+            total=ref(self.total),
+            held=ref(self.held),
+            got=ref(self.got),
+            sems=ref(self.sems),
+            local=ref(self.local),
+        )
+        return self
+
+    def run(self):
+        r = self.refs
+        held, got = r.held, r.got
+        z, up, down = line_place()
+        is_outer = jnp.logical_or(z == 0, z == 3)
+        low = z < 2
+        step = lambda k, at: hop(held, got.at[k], r.sems, k, at)
+
+        def towards(k, first, second):
+            pl.when(low)(lambda: step(k, first).start())
+            pl.when(jnp.logical_not(low))(lambda: step(k, second).start())
+
+        for k, (bit, turn) in enumerate(((CORE, 1), (X, 2), (Y, 4))):
+            step(k, bit).start()
+            step(k, bit).wait()
+            held[0:8] += got[k, 0:8]
+            for p in range(8):
+                held[8 + p] += got[k, 8 + (p ^ turn)]
+
+        @pl.when(is_outer)
+        def _():
+            towards(3, up, down)
+            step(3, up).wait_send()
+            step(5, up).wait_recv()
+            held[...] = got[5]
+
+        @pl.when(jnp.logical_not(is_outer))
+        def _():
+            step(3, up).wait_recv()
+            held[...] += got[3]
+            towards(4, up, down)
+            step(4, up).wait()
+            held[...] += got[4]
+            towards(5, down, up)
+            step(5, up).wait_send()
+
+        fetch(held, r.total, r.local.at[0]).wait()
+
+
+class Stream:
+    def __init__(self, program, group, unit, width):
+        self.group, self.unit = group, unit
+        self.held = program.tile(2, group, 2, unit, width)
+        self.sems = program.sems(2, group * 2)
+
+    def bind(self, ref):
+        self.refs = ref(self.held), ref(self.sems)
+        return self
+
+    def _copies(self, gather, index, slot, size):
+        held, sems = self.refs
+        return [
+            pltpu.make_async_copy(
+                gather.piece((index * self.group + g) // 2, (index * self.group + g) % 2, c).at[
+                    pl.ds(0, size)
+                ],
+                held.at[slot, g, c, pl.ds(0, size)],
+                sems.at[slot, 2 * g + c],
+            )
+            for g in range(self.group)
+            for c in range(2)
+        ]
+
+    def begin(self, gather, index, size=None):
+        for each in self._copies(gather, index, index % 2, size or self.unit):
+            each.start()
+
+    def bring(self, gather, step, first, last, size=None):
+        size = size or self.unit
+        for index in range(first + 1, last):
+            pl.when(step == index - 1 - first)(
+                lambda index=index: self.begin(gather, index, size)
+            )
+        slot = lax.rem(step + first, 2)
+        for each in self._copies(gather, 0, slot, size):
+            each.wait()
+        held = self.refs[0]
+        return held[slot, :, :, 0:size].reshape(-1, held.shape[-1])
+
+
+def prepare_body(
+    slot_ref, live_ref, im_ref, go_ref, gain_ref, shift_ref, own_ref, row_ref,
+    x_ref, g_ref, n_ref, s_ref, early_ref, bias_ref, sems,
+):
+    step = pl.program_id(0)
+    slot = slot_ref[0]
+    hops = [lambda lane=lane: hop(own_ref.at[lax.rem(lax.axis_index(DP), 2), lane], early_ref.at[lane], sems, lane, LANES[lane]) for lane in range(2)]
+    for r in range(1, 4):
+        to = {TENSOR: lax.axis_index(TENSOR) ^ r}
+        hops.append(lambda r=r, to=to: hop(row_ref, bias_ref.at[r - 1], sems, 1 + r, to))
+
+    @pl.when(step == 0)
+    def _():
+        meet((X, Y, XY))
+        for each in hops[2:] + hops[:2]:
+            each().start()
+
+    def pick(ref):
+        values = ref[...].astype(F32)
+        chosen = values[:, 0]
+        for index in range(1, values.shape[1]):
+            chosen = jnp.where(slot == index, values[:, index], chosen)
+        return chosen
+
+    picture = pick(im_ref)
+    centered = picture - row_mean(picture)
+    inverse = lax.rsqrt(row_mean(centered * centered) + EPS)
+    normed = centered * inverse * gain_ref[...] + shift_ref[...]
+    x_ref[...] = picture.T.astype(BF)
+    g_ref[...] = (pick(go_ref) * live_ref[0].astype(F32)).T.astype(BF)
+    n_ref[...] = normed.T.astype(BF)
+    s_ref[0:1, :] = row_mean(picture).T
+    s_ref[1:2, :] = inverse.T
+
+    @pl.when(step == pl.num_programs(0) - 1)
+    def _():
+        for each in hops:
+            each().wait()
+
+
+def prepare(images, grad_out, slot, live, gain, shift, own, bias):
+    slots, length, width = images.shape
+    rows = 128
+    scalar = pl.BlockSpec(memory_space=pltpu.SMEM)
+    tokens = pl.BlockSpec((rows, slots, width), lambda i: (i, 0, 0))
+    vector = pl.BlockSpec((1, width), lambda i: (0, 0))
+    return pl.pallas_call(
+        prepare_body,
+        grid=(pl.cdiv(length, rows),),
+        in_specs=[scalar, scalar, tokens, tokens, vector, vector, ANYWHERE, ANYWHERE],
+        out_specs=[pl.BlockSpec((width, rows), lambda i: (0, i))] * 3
+        + [pl.BlockSpec((2, rows), lambda i: (0, i)), ANYWHERE, ANYWHERE],
+        out_shape=[jax.ShapeDtypeStruct((width, length), BF)] * 3
+        + [
+            jax.ShapeDtypeStruct((2, length), F32),
+            jax.ShapeDtypeStruct(own.shape[1:], BF),
+            jax.ShapeDtypeStruct((3, *bias.shape), F32),
+        ],
+        scratch_shapes=[pltpu.SemaphoreType.DMA((2, 5))],
+        compiler_params=pltpu.CompilerParams(
+            vmem_limit_bytes=50 << 20, collective_id=1, has_side_effects=True
+        ),
+        name="prepare",
+    )(slot, live, images.transpose(1, 0, 2), grad_out.transpose(1, 0, 2), gain, shift, own, bias)
+
+
+def as_column(row):
+    return jnp.broadcast_to(row, (8, row.shape[1])).T[:, 0:1]
+
+
+def as_row(column):
+    return jnp.broadcast_to(column, (column.shape[0], 8)).T[0:1, :]
+
+
+def attend_head(weight, normed, bias, qkv_ref, o_ref, lse_ref):
+    length = normed.shape[1]
+    rows = dot_nn(weight, normed)
+    queries = ((rows[:HD] + bias[0]) * (LOG2E / math.sqrt(HD))).astype(BF)
+    keys_t = rows[HD : 2 * HD].astype(BF)
+    values = (rows[2 * HD :] + bias[1]).astype(BF)
+    qkv_ref[0, 0] = queries
+    qkv_ref[0, 1] = keys_t
+    qkv_ref[0, 2] = values
+    keys = keys_t.T
+    for start in range(0, length, QUERY_BLOCK):
+        block = slice(start, min(start + QUERY_BLOCK, length))
+        scores = dot_nn(keys, queries[:, block])
+        top = jnp.max(scores, axis=0, keepdims=True)
+        weights = jnp.exp2(scores - top)
+        total = jnp.sum(weights, axis=0, keepdims=True)
+        mixed = dot_nn(values, weights.astype(BF))
+        o_ref[0, :, block] = (mixed * (1.0 / total)).astype(BF)
+        lse_ref[0, :, block] = top + jnp.log2(total)
+
+
+def attend_back_head(qkv_ref, do_ref, o_ref, lse_ref, d_ref, dk_acc, dv_acc):
+    keys_t = qkv_ref[0, 1]
+    keys = keys_t.T
+    values = qkv_ref[0, 2].T
+    length = keys_t.shape[1]
+    scale = 1.0 / math.sqrt(HD)
+    for start in range(0, length, QUERY_BLOCK):
+        block = slice(start, min(start + QUERY_BLOCK, length))
+        queries_t = qkv_ref[0, 0, :, block]
+        pull_t = do_ref[0, :, block]
+        delta = jnp.sum(
+            pull_t.astype(F32) * o_ref[0, :, block].astype(F32), axis=0, keepdims=True
+        )
+        probs = jnp.exp2(dot_nn(keys, queries_t) - lse_ref[0, :, block])
+        probs_low = probs.astype(BF)
+        d_probs = dot_nn(values, pull_t)
+        d_scores = (probs * (d_probs - delta)).astype(BF)
+        d_ref[0, 0, :, block] = (dot_nn(keys_t, d_scores) * scale).astype(BF)
+        d_keys = dot_nn(d_scores, queries_t.T)
+        d_values = dot_nn(probs_low, pull_t.T)
+        if start == 0:
+            dk_acc[...] = d_keys
+            dv_acc[...] = d_values
+        else:
+            dk_acc[...] += d_keys
+            dv_acc[...] += d_values
+    d_ref[0, 1] = (dk_acc[...].T * LN2).astype(BF)
+    d_ref[0, 2] = dv_acc[...].T.astype(BF)
+    return [jnp.sum(d_ref[0, k].astype(F32), axis=1, keepdims=True) for k in (0, 2)]
+
+
+def columns_of(length, block=128):
+    return [slice(start, min(start + block, length)) for start in range(0, length, block)]
+
+
+def norm_back(grad, unit_values, inverse, gain):
+    scaled = grad * gain
+    mean = lambda values: jnp.mean(values, axis=0, keepdims=True)
+    return inverse * (scaled - mean(scaled) - unit_values * mean(scaled * unit_values))
+
+
+def turned(values, axis, bit):
+    return jnp.where(bit == 1, lax.rev(values, (axis,)), values)
+
+
+def forward(attn_own, early, fc1_own, bias, bias_far, picture, normed_one, vectors):
+    width, length = picture.shape
+    chunk = attn_own.shape[2]
+    unit = fc1_own.shape[2]
+    rows = 2 * unit
+    heads = 16
+    p = Program("forward", (X, Y, CORE))
+    own, soon, own_fc1 = p.input(attn_own), p.input(early), p.input(fc1_own)
+    bias_in, x_in, n_in, v_in = p.input(bias), p.input(picture), p.input(normed_one), p.input(vectors)
+    bias_far_in = p.input(bias_far)
+    attn = Gather(p, own, attn_own.shape, soon)
+    fc1 = Gather(p, own_fc1, fc1_own.shape)
+    stream = Stream(p, 1, unit, width)
+    qkv, mixed = p.output(heads, 3, HD, length), p.output(heads, HD, length)
+    lse = p.output(heads, 1, length, dtype=F32)
+    residual, normed = p.output(width, length, dtype=F32), p.output(width, length)
+    stats, out_all = p.output(2, length, dtype=F32), p.output(heads, HD, width)
+    act, slope = p.output(8, rows, length), p.output(8, rows, length)
+    held = Bag(
+        bias=p.tile(4, *bias.shape, dtype=F32),
+        x=p.tile(width, length),
+        n=p.tile(width, length),
+        v=p.tile(*vectors.shape, dtype=F32),
+        o=p.tile(heads, HD, length),
+        w=p.tile(heads, HD, width),
+        h=p.tile(width, length, dtype=F32),
+        n2=p.tile(width, length),
+        s=p.tile(2, length, dtype=F32),
+    )
+    sems, wsems = p.sems(8), p.sems(heads)
+
+    def script(ref):
+        hold = held.each(ref)
+        sem, wsem = ref(sems), ref(wsems)
+        attn.bind(ref)
+        fc1.bind(ref)
+        stream.bind(ref)
+        attn.start()
+        attn.forward()
+        fc1.start()
+        copies = [
+            fetch(ref(n_in), hold.n, sem.at[0]),
+            fetch(ref(bias_in), hold.bias.at[0], sem.at[1]),
+            fetch(ref(bias_far_in), hold.bias.at[pl.ds(1, 3)], sem.at[2]),
+            fetch(ref(x_in), hold.x, sem.at[5]),
+            fetch(ref(v_in), hold.v, sem.at[6]),
+        ]
+        for each in copies[:3]:
+            each.wait()
+
+        def heads_of(first, count, part_of, sources, specs, events=()):
+            def body(step, *refs):
+                weights, (qkv_ref, o_ref, lse_ref) = refs[: len(sources)], refs[len(sources) :]
+                shard, half, lane = part_of(step)
+                rows_of = lambda w: w[...].reshape(chunk, width)[: 3 * HD]
+                weight = rows_of(weights[0])
+                if len(weights) > 2:
+                    weight = jnp.where(lane == shard - 1, rows_of(weights[2]), weight)
+                if len(weights) > 1:
+                    weight = jnp.where(half == 0, weight, rows_of(weights[1]))
+                at = 4 * half + 2 * lane
+                shift = [
+                    as_column(hold.bias[shard, at + k, :, 0:HD]) for k in range(2)
+                ]
+                attend_head(weight, hold.n[...], shift, qkv_ref, o_ref, lse_ref)
+                hold.o[first + step] = o_ref[0]
+
+            phase(
+                count,
+                body,
+                sources,
+                specs,
+                [ref(qkv), ref(mixed), ref(lse)],
+                [
+                    spec((1, 3, HD, length), lambda i: (first + i, 0, 0, 0)),
+                    spec((1, HD, length), lambda i: (first + i, 0, 0)),
+                    spec((1, 1, length), lambda i: (first + i, 0, 0)),
+                ],
+                events,
+            )
+
+        def bring_out(shard):
+            return [
+                pltpu.make_async_copy(
+                    attn.piece(shard, half, lane).at[pl.ds(3 * HD, HD)],
+                    hold.w.at[4 * shard + 2 * half + lane],
+                    wsem.at[4 * shard + 2 * half + lane],
+                )
+                for half in range(2)
+                for lane in range(2)
+            ]
+
+        heads_of(
+            0,
+            4,
+            lambda i: (0, i // 2, lax.rem(i, 2)),
+            [ref(own).at[lax.rem(lax.axis_index(DP) + part, 2)] for part in range(2)],
+            [spec((1, chunk, width), lambda i: (lax.rem(i, 2), 0, 0))] * 2,
+        )
+        attn.near_here()
+        attn.near_whole()
+        mine = lambda i: (i // 4, 1 - i // 4, 0, 0)
+        heads_of(
+            4,
+            8,
+            lambda i: (1 + i // 4, lax.rem(i // 2, 2), lax.rem(i, 2)),
+            [ref(attn.near), ref(attn.near_part), ref(soon)],
+            [
+                spec((1, 1, chunk, width), mine),
+                spec((1, 1, chunk, width), lambda i: (i // 4, lax.rem(i, 2), 0, 0)),
+                spec((1, chunk, width), lambda i: (i // 4, 0, 0)),
+            ],
+        )
+        attn.far_here()
+        for shard in range(3):
+            for each in bring_out(shard):
+                each.start()
+        attn.far_whole()
+        for each in bring_out(3):
+            each.start()
+        heads_of(
+            12,
+            4,
+            lambda i: (3, i // 2, lax.rem(i, 2)),
+            [ref(attn.far), ref(attn.far_part)],
+            [spec((1, chunk, width), lambda i: (lax.rem(i, 2), 0, 0))] * 2,
+        )
+        fc1.forward()
+        for each in copies[3:]:
+            each.wait()
+        for shard in range(4):
+            for each in bring_out(shard):
+                each.wait()
+        stream.begin(fc1, 0)
+        store_w = fetch(hold.w, ref(out_all), sem.at[4])
+        weight = hold.w[...].reshape(width, width)
+        for block in columns_of(length, 256):
+            mix = hold.o[:, :, block].reshape(width, -1)
+            values = hold.x[:, block].astype(F32) + contract_rows(weight, mix)
+            values = values + hold.v[:, 2:3]
+            average = jnp.mean(values, axis=0, keepdims=True)
+            centered = values - average
+            inverse = lax.rsqrt(jnp.mean(centered * centered, axis=0, keepdims=True) + EPS)
+            hold.h[:, block] = values
+            hold.n2[:, block] = (
+                centered * inverse * hold.v[:, 3:4] + hold.v[:, 4:5]
+            ).astype(BF)
+            hold.s[0:1, block] = average
+            hold.s[1:2, block] = inverse
+        stores = [store_w] + [
+            fetch(source, ref(target), sem.at[k])
+            for k, (source, target) in enumerate(((hold.h, residual), (hold.n2, normed), (hold.s, stats)))
+        ]
+
+        def hidden(step, act_ref, slope_ref):
+            weight = stream.bring(fc1, step, 0, 8)
+            shard, half = step // 2, lax.rem(step, 2)
+            shift = as_column(hold.bias[shard, half, :, 128 : 128 + rows])
+            preact = dot_nn(weight, hold.n2[...]) + shift
+            square = preact * preact
+            curve = jnp.tanh(preact * (GELU_A + (GELU_A * GELU_B) * square))
+            rise = 0.5 * (1.0 + curve)
+            act_ref[0] = (preact * rise).astype(BF)
+            inner = GELU_A + (3.0 * GELU_A * GELU_B) * square
+            slope_ref[0] = (rise + (0.5 * preact) * (1.0 - curve * curve) * inner).astype(BF)
+
+        block = spec((1, rows, length), lambda i: (i, 0, 0))
+
+        def near_all():
+            fc1.near_here()
+            fc1.near_whole()
+
+        def far_all():
+            fc1.far_here()
+            fc1.far_whole()
+
+        phase(
+            8, hidden, [], [], [ref(act), ref(slope)], [block, block],
+            [(1, near_all), (5, far_all)],
+        )
+        for each in stores:
+            each.wait()
+        attn.drain()
+        fc1.drain()
+
+    result = p.call(script, 2, 3e10)
+    return (
+        gathered(attn).each(result),
+        gathered(fc1).each(result),
+        Bag(
+            qkv=qkv,
+            mixed=mixed,
+            lse=lse,
+            residual=residual,
+            normed_two=normed,
+            stats_two=stats,
+            out_all=out_all,
+            act=act,
+            slope=slope,
+        ).each(result),
+    )
+
+
+def gathered(source):
+    return Bag(
+        near=source.near, near_part=source.near_part, far=source.far, far_part=source.far_part
+    )
+
+
+class Ready:
+    def __init__(self, program, own, parts, early=None):
+        self.handles = parts.each(program.input)
+        self.handles.own = program.input(own)
+        self.handles.early = None if early is None else program.input(early)
+        self.early = early
+
+    def bind(self, ref):
+        self.refs = self.handles.each(lambda h: None if h is None else ref(h))
+        return self
+
+    piece = Gather.piece
+
+
+def backward(arrays, fc1_parts, attn_parts, owns, early, live):
+    width, length = arrays.picture.shape
+    share = width // 4
+    unit = owns.fc2.shape[2]
+    rows = 2 * unit
+    block = 3 * HD
+    p = Program("backward", (X, Y, XY, CORE, LINE))
+    into = arrays.each(p.input)
+    live_in = p.input(live, pl.BlockSpec(memory_space=pltpu.SMEM))
+    fc1 = Ready(p, owns.fc1, fc1_parts)
+    attn = Ready(p, owns.attn, attn_parts, early)
+    fc2 = Gather(p, p.input(owns.fc2), owns.fc2.shape)
+    stream = Stream(p, 2, unit, width)
+
+    fc_shape, out_shape, qkv_shape = ((4, 2, u, width) for u in (unit, HD, block))
+    shapes = (fc_shape, fc_shape, out_shape, qkv_shape)
+    part = [p.output(*shape) for shape in shapes]
+    mine = [p.output(*shape) for shape in shapes]
+    swap = [Swap(p, source, shape) for source, shape in zip(part, shapes)]
+    plane = [Plane(p, source, shape) for source, shape in zip(mine, shapes)]
+    line = [Line(p, shape[1:]) for shape in shapes]
+    d_pre = p.output(8, rows, length)
+    pull = p.output(16, HD, length)
+    d_qkv = p.output(16, 3, HD, length)
+    block_rows, input_rows = p.output(4, share, length), p.output(4, share, length)
+    spread_block = Spread(p, block_rows, (4, share, length))
+    spread_input = Spread(p, input_rows, (4, share, length))
+    vectors = Vectors(p, (16, 1, width))
+    held = Bag(
+        upstream=p.tile(width, length),
+        normed_two=p.tile(width, length),
+        normed_one=p.tile(width, length),
+        low=p.tile(width, length),
+        residual=p.tile(width, length, dtype=F32),
+        acc=p.tile(width, length, dtype=F32),
+        vectors=p.tile(*arrays.vectors.shape, dtype=F32),
+        cols=p.tile(width, 8, dtype=F32),
+        stats_two=p.tile(2, length, dtype=F32),
+        stats_one=p.tile(2, length, dtype=F32),
+        dk=p.tile(length, HD, dtype=F32),
+        dv=p.tile(length, HD, dtype=F32),
+    )
+    sems = p.sems(12)
+
+    def script(ref):
+        hold = held.each(ref)
+        sem = ref(sems)
+        for each in (fc1, attn, fc2, stream, spread_block, spread_input, vectors):
+            each.bind(ref)
+        for group in (swap, plane, line):
+            for each in group:
+                each.bind(ref)
+        vec = vectors.refs.held
+        array = into.each(ref)
+        live_now = ref(live_in)[0].astype(F32)
+
+        copies = Bag(
+            upstream=fetch(array.upstream, hold.upstream, sem.at[0]),
+            normed_two=fetch(array.normed_two, hold.normed_two, sem.at[1]),
+            residual=fetch(array.residual, hold.residual, sem.at[2]),
+            vectors=fetch(array.vectors, hold.vectors, sem.at[3]),
+            stats_two=fetch(array.stats_two, hold.stats_two, sem.at[4]),
+            normed_one=fetch(array.normed_one, hold.normed_one, sem.at[5]),
+            stats_one=fetch(array.stats_one, hold.stats_one, sem.at[6]),
+        )
+        fc2.start()
+        stream.begin(fc2, 0)
+        vec[...] = jnp.zeros(vec.shape, F32)
+        hold.cols[...] = jnp.zeros(hold.cols.shape, F32)
+        copies.upstream.wait()
+        copies.normed_two.wait()
+
+        def gradient(source, other, name, half, shards, plus=False, events=()):
+            _, lanes, size, _ = shapes[name]
+            count = lanes * size
+            pick = lambda i: jnp.where(i == 0, shards[0], shards[-1]) if len(shards) < 4 else i
+
+            def body(step, *refs):
+                sums = contract_cols(refs[0][...].reshape(count, length), other[...])
+                if plus:
+                    sums = sums + refs[1][0].reshape(count, width).astype(F32)
+                refs[-1][0] = sums.astype(BF).reshape(lanes, size, width)
+
+            lead = source.shape[0] // 8
+            tail = source.shape[1:]
+            out_spec = spec((1, lanes, size, width), lambda i: (pick(i), 0, 0, 0))
+            zeros = (0,) * len(tail)
+            phase(
+                len(shards),
+                body,
+                [source] + ([swap[name].refs[1]] if plus else []),
+                [spec((lead, *tail), lambda i: (2 * pick(i) + half, *zeros))]
+                + ([out_spec] if plus else []),
+                [ref((part, mine)[half == 0][name])],
+                [out_spec],
+                events,
+            )
+
+        every = (0, 1, 2, 3)
+        gradient(array.act, hold.upstream, FC2, 1, every)
+        swap[FC2].start(*every)
+
+        def hidden(first, count, events=()):
+            def body(step, slope_ref, d_ref):
+                weight = stream.bring(fc2, step, first, first + count)
+                values = dot_nn(weight, hold.upstream[...])
+                values = (values * slope_ref[...].reshape(2 * rows, length).astype(F32)).astype(BF)
+                d_ref[...] = values.reshape(2, rows, length)
+                for half in range(2):
+                    sums = jnp.sum(
+                        values[half * rows : (half + 1) * rows].astype(F32), axis=1, keepdims=True
+                    )
+                    vec[8 + 2 * (first + step) + half, :, 0:rows] = as_row(sums)
+
+            pair = spec((2, rows, length), lambda i: (first + i, 0, 0))
+            phase(count, body, [array.slope], [pair], [ref(d_pre)], [pair], events)
+
+        hidden(0, 1)
+        fc2.forward()
+        swap[FC2].wait(*every)
+        gradient(array.act, hold.upstream, FC2, 0, every, True)
+        plane[FC2].start()
+        fc2.near_here()
+        fc2.near_whole()
+        stream.begin(fc2, 1)
+        hidden(1, 2)
+        fc2.far_here()
+        fc2.far_whole()
+        stream.begin(fc2, 3)
+        hidden(3, 1)
+
+        def back(weights, values, lead, size, events=()):
+            def body(step, d_ref):
+                weight = stream.bring(weights, step, 0, 4, size)
+                sums = contract_rows(weight, d_ref[...].reshape(4 * size, length))
+
+                @pl.when(step == 0)
+                def _():
+                    hold.acc[...] = sums
+
+                @pl.when(step > 0)
+                def _():
+                    hold.acc[...] += sums
+
+            tail = values.shape[1:]
+            zeros = (0,) * len(tail)
+            phase(4, body, [values], [spec((lead, *tail), lambda i: (i, *zeros))], [], [], events)
+
+        stream.begin(fc1, 0)
+        back(fc1, ref(d_pre), 2, unit)
+        for each in (copies.residual, copies.vectors, copies.stats_two):
+            each.wait()
+        total = lambda values: jnp.sum(values, axis=1, keepdims=True)
+        for cut in columns_of(length):
+            inverse = hold.stats_two[1:2, cut]
+            grad = hold.acc[:, cut]
+            units = (hold.residual[:, cut] - hold.stats_two[0:1, cut]) * inverse
+            up = hold.upstream[:, cut].astype(F32)
+            d_residual = up + norm_back(grad, units, inverse, hold.vectors[:, 3:4])
+            hold.low[:, cut] = d_residual.astype(BF)
+            hold.cols[:, 2:3] += total(d_residual)
+            hold.cols[:, 3:4] += total(grad * units)
+            hold.cols[:, 4:5] += total(grad)
+            hold.cols[:, 5:6] += total(up)
+
+        gradient(ref(d_pre), hold.normed_two, FC1, 1, every)
+        swap[FC1].start(*every)
+        plane[FC2].forward()
+        plane[FC2].settle()
+        picture_copy = fetch(array.picture, hold.upstream, sem.at[7])
+
+        def pull_body(step, w_ref, o_ref):
+            weight = w_ref[...].reshape(4 * HD, width)
+            o_ref[...] = dot_nn(weight, hold.low[...]).reshape(4, HD, length).astype(BF)
+
+        quarter = lambda *tail: spec((4, *tail), lambda i: (i, *(0 for _ in tail)))
+        phase(
+            4, pull_body, [array.out_all], [quarter(HD, width)], [ref(pull)], [quarter(HD, length)]
+        )
+        gradient(array.mixed, hold.low, OUT, 1, every)
+        swap[OUT].start(*every)
+        swap[FC1].wait(*every)
+        gradient(ref(d_pre), hold.normed_two, FC1, 0, every, True)
+        plane[FC1].start()
+        plane[FC2].finish(line[FC2])
+        swap[OUT].wait(*every)
+        gradient(array.mixed, hold.low, OUT, 0, every, True)
+        plane[OUT].start()
+        copies.normed_one.wait()
+
+        def heads_back(shards, events):
+            shard_of = lambda i: jnp.where(i < 4, shards[0], shards[1])
+            at = lambda i: 4 * shard_of(i) + lax.rem(i, 4)
+
+            def body(step, qkv_ref, do_ref, o_ref, lse_ref, d_ref):
+                sums = attend_back_head(
+                    qkv_ref, do_ref, o_ref, lse_ref, d_ref, hold.dk, hold.dv
+                )
+                row = 8 + 2 * shard_of(step) + lax.rem(step // 2, 2)
+                for k in range(2):
+                    where = pl.multiple_of(640 + 128 * (2 * lax.rem(step, 2) + k), 128)
+                    padded = jnp.concatenate(
+                        [as_row(sums[k]), jnp.zeros((1, 128 - HD), F32)], axis=1
+                    )
+                    vec[row, :, pl.ds(where, 128)] = padded
+
+            flat = spec((1, HD, length), lambda i: (at(i), 0, 0))
+            many = spec((1, 3, HD, length), lambda i: (at(i), 0, 0, 0))
+            phase(
+                8,
+                body,
+                [array.qkv, ref(pull), array.mixed, array.lse],
+                [many, flat, flat, spec((1, 1, length), lambda i: (at(i), 0, 0))],
+                [ref(d_qkv)],
+                [many],
+                events,
+            )
+
+        heads_back((3, 1), [(6, lambda: line[FC2].meet(0))])
+        gradient(ref(d_qkv), hold.normed_one, QKV, 1, (3, 1))
+        swap[QKV].start(3, 1)
+
+        def settle(name):
+            plane[name].forward()
+            plane[name].settle()
+
+        heads_back(
+            (2, 0),
+            [
+                (2, lambda: line[FC2].meet(1)),
+                (2, lambda: settle(FC1)),
+                (3, lambda: line[FC2].leave(0)),
+                (6, lambda: settle(OUT)),
+            ],
+        )
+        swap[QKV].wait(3, 1)
+        gradient(ref(d_qkv), hold.normed_one, QKV, 0, (3, 1), True)
+        plane[QKV].send(3)
+        plane[QKV].send(1)
+        gradient(ref(d_qkv), hold.normed_one, QKV, 1, (2, 0))
+        swap[QKV].start(2, 0)
+        line[FC2].leave(1)
+        plane[FC1].finish(line[FC1])
+        plane[OUT].finish(line[OUT])
+        stream.begin(fc2, 0)
+        swap[QKV].wait(2, 0)
+        gradient(ref(d_qkv), hold.normed_one, QKV, 0, (2, 0), True)
+        plane[QKV].send(2)
+        plane[QKV].send(0)
+        line[FC2].finish(0)
+        back(fc2, array.act, 2, unit, [(3, lambda: line[FC1].meet(0))])
+        line[FC2].finish(1)
+        for cut in columns_of(length):
+            values = hold.residual[:, cut] + hold.acc[:, cut] + hold.vectors[:, 5:6]
+            hold.normed_two[:, cut] = (values * live_now).astype(BF)
+        store_rows(hold.normed_two, ref(block_rows), sem, share)
+        settle(QKV)
+        spread_block.start()
+        line[FC1].meet(1)
+        line[FC1].leave(0)
+        line[OUT].meet(0)
+        line[OUT].meet(1)
+        picture_copy.wait()
+        copies.stats_one.wait()
+        stream.begin(attn, 0, block)
+        back(attn, ref(d_qkv), 4, block, [(2, lambda: line[FC1].leave(1))])
+        line[OUT].leave(0)
+        line[OUT].leave(1)
+        plane[QKV].finish(line[QKV])
+        for cut in columns_of(length):
+            inverse = hold.stats_one[1:2, cut]
+            grad = hold.acc[:, cut]
+            units = hold.upstream[:, cut].astype(F32) - hold.stats_one[0:1, cut]
+            units = units * inverse
+            d_input = hold.low[:, cut].astype(F32) + norm_back(
+                grad, units, inverse, hold.vectors[:, 0:1]
+            )
+            hold.normed_two[:, cut] = d_input.astype(BF)
+            hold.cols[:, 0:1] += total(grad * units)
+            hold.cols[:, 1:2] += total(grad)
+        store_rows(hold.normed_two, ref(input_rows), sem, share)
+        spread_input.start()
+        wide = hold.cols[...].T
+        for k in range(8):
+            vec[k] = wide[k : k + 1]
+        line[QKV].meet(0)
+        vectors.run()
+        line[QKV].meet(1)
+        line[QKV].leave(0)
+        line[FC1].finish(0)
+        line[FC1].finish(1)
+        line[OUT].finish(0)
+        line[OUT].finish(1)
+        line[QKV].leave(1)
+        spread_block.finish()
+        spread_input.finish()
+        line[QKV].finish(0)
+        line[QKV].finish(1)
+        for each in plane:
+            each.drain()
+        fc2.drain()
+
+    result = p.call(script, 3, 8e10)
+    sums = [(result(each.total), result(each.other)) for each in line]
+    spreads = [
+        (result(block_rows), result(spread_block.landed)),
+        (result(input_rows), result(spread_input.landed)),
+    ]
+    return sums, spreads, result(vectors.total)[:, 0]
+
+
+def store_rows(source, target, sem, share):
+    copies = [
+        fetch(source.at[pl.ds(k * share, share)], target.at[k], sem.at[k]) for k in range(4)
+    ]
+    for each in copies:
+        each.wait()
+
+
+def finish(sums, spreads, place_t, core, hidden):
+    width = sums[FC2][0].shape[-1]
+    share, length = spreads[0][0].shape[1:]
+
+    def body(at, *refs):
+        step = pl.program_id(0)
+        same = lax.rem(step // 2 + at[1], 2) == 0
+        ins, outs = refs[:12], refs[12:]
+        for k in range(4):
+            rows = jnp.where(same, ins[2 * k][0], ins[2 * k + 1][0]).astype(F32)
+            outs[k][...] = rows.reshape(outs[k].shape)
+        for k in range(2):
+            rows = jnp.where(step == at[0], ins[8 + 2 * k][0], ins[9 + 2 * k][0])
+            outs[4 + k][0] = rows.astype(F32)
+
+    half = lambda array: pl.BlockSpec((1, *array.shape[1:]), lambda i, at: (lax.rem(i, 2), 0, 0))
+    own = pl.BlockSpec((1, share, length), lambda i, at: (at[0], 0, 0))
+    landed = pl.BlockSpec(
+        (1, share, length), lambda i, at: (jnp.maximum((i ^ at[0]) - 1, 0), 0, 0)
+    )
+    units = [pair[0].shape[1] for pair in sums]
+    rows = lambda unit: pl.BlockSpec((unit, width), lambda i, at: (i, 0))
+    slot = pl.BlockSpec((1, share, length), lambda i, at: (i, 0, 0))
+    shape = lambda *dims: jax.ShapeDtypeStruct(dims, F32)
+    return pl.pallas_call(
+        body,
+        grid_spec=pltpu.PrefetchScalarGridSpec(
+            num_scalar_prefetch=1,
+            grid=(4,),
+            in_specs=[half(array) for pair in sums for array in pair] + [own, landed] * 2,
+            out_specs=[
+                rows(units[FC2]),
+                rows(units[FC1]),
+                rows(units[OUT]),
+                pl.BlockSpec((3, HD, width), lambda i, at: (0, i, 0)),
+                slot,
+                slot,
+            ],
+        ),
+        out_shape=[
+            shape(hidden, width),
+            shape(hidden, width),
+            shape(share, width),
+            shape(3, share, width),
+            shape(4, share, length),
+            shape(4, share, length),
+        ],
+        compiler_params=pltpu.CompilerParams(vmem_limit_bytes=50 << 20),
+        name="finish",
+    )(
+        jnp.stack([place_t, core]).astype(jnp.int32),
+        *[array for pair in sums for array in pair],
+        *spreads[0],
+        *spreads[1],
+    )
+
+
+def whole_image(
+    images,
+    counts,
+    ln1_gain,
+    ln1_bias,
+    qkv_weight,
+    qv_bias,
+    out_weight,
+    out_bias,
+    ln2_gain,
+    ln2_bias,
+    fc1_weight,
+    fc1_bias,
+    fc2_weight,
+    fc2_bias,
+    grad_out,
+):
+    slot_count, length, width = images.shape
+    share = width // 4
+    hidden = fc1_weight.shape[1]
+    unit = -(-hidden // 64) * 16
+    rows = 2 * unit
+    place_t = lax.axis_index(TENSOR)
+    core = lax.rem(lax.axis_index(DP), 2)
+    block = 3 * HD
+
+    qkv_rows = qkv_weight.reshape(3, width, 2, 2, HD).transpose(2, 3, 0, 4, 1)
+    attn_own = jnp.concatenate(
+        [qkv_rows.reshape(2, 2, block, width), out_weight.reshape(2, 2, HD, width)], axis=2
+    )
+    pad = 2 * rows - hidden
+    fc1_own, fc2_own = (
+        jnp.pad(each, ((0, pad), (0, 0))).reshape(2, 2, unit, width)
+        for each in (fc1_weight.T, fc2_weight)
+    )
+    head_bias = qv_bias.reshape(2, 2, 2, HD).transpose(1, 2, 0, 3)
+    head_bias = jnp.pad(turned(head_bias, 0, core).reshape(8, HD), ((0, 0), (0, 128 - HD)))
+    hidden_bias = turned(jnp.pad(fc1_bias, (0, pad)).reshape(2, rows), 0, core)
+    hidden_bias = jnp.pad(hidden_bias, ((0, 6), (0, 640 - rows)))
+    bias = jnp.concatenate([head_bias, hidden_bias], axis=1).astype(F32)[:, None]
+    vectors = jnp.stack(
+        [ln1_gain, ln1_bias, out_bias, ln2_gain, ln2_bias, fc2_bias, fc2_bias, fc2_bias], axis=1
+    ).astype(F32)
+    live = (place_t < counts[0]).astype(jnp.int32)[None]
+
+    picture, upstream, normed_one, stats_one, early, bias_far = prepare(
+        images,
+        grad_out,
+        place_t[None].astype(jnp.int32),
+        live,
+        ln1_gain.astype(F32)[None],
+        ln1_bias.astype(F32)[None],
+        attn_own,
+        bias,
+    )
+    attn_parts, fc1_parts, made = forward(
+        attn_own, early, fc1_own, bias, bias_far, picture, normed_one, vectors
+    )
+    made.__dict__.update(
+        upstream=upstream,
+        picture=picture,
+        normed_one=normed_one,
+        stats_one=stats_one,
+        vectors=vectors,
+    )
+    owns = Bag(attn=attn_own, fc1=fc1_own, fc2=fc2_own)
+    sums, spreads, totals = backward(made, fc1_parts, attn_parts, owns, early, live)
+
+    own_wide = lax.dynamic_slice_in_dim(totals[:6], place_t * share, share, 1)
+    own_rows = turned(totals[8:10], 0, core)
+    own_hidden = own_rows[:, :rows].reshape(-1)[:hidden]
+    own_qv = own_rows[:, 640:].reshape(2, 2, 2, 128)[..., :HD].transpose(2, 0, 1, 3)
+    own_qv = own_qv.reshape(2, share)
+
+    fc2_result, fc1_result, out_result, qkv_result, block_result, input_result = finish(
+        sums, spreads, place_t, core, hidden
+    )
+    return (
+        block_result.transpose(0, 2, 1),
+        input_result.transpose(0, 2, 1),
+        own_wide[0],
+        own_wide[1],
+        qkv_result.transpose(0, 2, 1),
+        own_qv,
+        out_result,
+        own_wide[2],
+        own_wide[3],
+        own_wide[4],
+        fc1_result.T,
+        own_hidden,
+        fc2_result,
+        own_wide[5],
+    )
+
+
 def solution(mesh):
+    whole_fits = mesh.shape[TENSOR] == 4 and mesh.shape[DP] == 8
     return jax.shard_map(
-        local,
+        whole_image if whole_fits else local,
         mesh=mesh,
         in_specs=(
-            P("dp", None, None),
-            P("dp"),
+            P(DP, None, None),
+            P(DP),
             P(),
             P(),
-            P(None, None, "tensor"),
-            P(None, "tensor"),
-            P("tensor", None),
+            P(None, None, TENSOR),
+            P(None, TENSOR),
+            P(TENSOR, None),
             P(),
             P(),
             P(),
-            P(None, "tensor"),
-            P("tensor"),
-            P("tensor", None),
+            P(None, TENSOR),
+            P(TENSOR),
+            P(TENSOR, None),
             P(),
-            P("dp", None, None),
+            P(DP, None, None),
         ),
         out_specs=(
-            P("dp", None, "tensor"),
-            P("dp", None, "tensor"),
-            P("tensor"),
-            P("tensor"),
-            P(None, None, "tensor"),
-            P(None, "tensor"),
-            P("tensor", None),
-            P("tensor"),
-            P("tensor"),
-            P("tensor"),
-            P(None, "tensor"),
-            P("tensor"),
-            P("tensor", None),
-            P("tensor"),
+            P(DP, None, TENSOR),
+            P(DP, None, TENSOR),
+            P(TENSOR),
+            P(TENSOR),
+            P(None, None, TENSOR),
+            P(None, TENSOR),
+            P(TENSOR, None),
+            P(TENSOR),
+            P(TENSOR),
+            P(TENSOR),
+            P(None, TENSOR),
+            P(TENSOR),
+            P(TENSOR, None),
+            P(TENSOR),
         ),
         check_vma=False,
     )

time: 1370 us -> 431 us (0.31)
  waiting for transfers between devices: 569 us -> 0 us
  Pallas kernels: 0 us -> 399 us
  matrix products: 335 us -> 0 us
  other arithmetic: 226 us -> 2.7 us
  blocking collectives: 137 us -> 0 us
  local copies, waits for them, and re-layouts: 69.1 us -> 19 us
  between operations: 15.9 us -> 2.08 us
    pallas_call x0 -> x4, Pallas kernels: none -> 399 us  [the longest x2 363 us: call(): pl.pallas_call(kernel, in_specs=self.specs, out_specs=[ANYWHERE] * count_...]
    dot_general x80 -> x0, matrix products: 335 us -> none  [the longest x12 67.7 us: contract_rows(): lax.dot_general(left, right, (((0,), (0,)), ((), ())), preferred_element_...]
    reduce_scatter x16 -> x0, waiting for transfers between devices: 237 us -> none  [the longest x4 116 us: layer_step(): lax.psum_scatter(back_mlp.astype(jnp.bfloat16), 'tensor', scatter_dimensi...]
    all_gather x8 -> x0, waiting for transfers between devices: 204 us -> none  [the longest x4 126 us: layer_step(): normed_two = lax.all_gather(own_normed, 'tensor', axis=1, tiled=True)]
    psum x13 -> x0, blocking collectives: 137 us -> none  [the longest x12 109 us: group_stats(): return lax.psum((first, second), 'tensor')]
    psum x1 -> x0, waiting for transfers between devices: 128 us -> none  [local(): lax.psum(grad_qkv.astype(jnp.bfloat16), 'dp').astype(jnp.float32)]
    convert_element_type x52 -> x2, other arithmetic: 107 us -> 0.89 us  [the longest x1 0.86 us: whole_image(): vectors = jnp.stack([ln1_gain, ln1_bias, out_bias, ln2_gain, ln2_bias, fc...]
    reduce_sum x36 -> x0, other arithmetic: 72.3 us -> none  [the longest x8 15.3 us: row_mean(): return jnp.mean(values, axis=-1, keepdims=True)]
  transfers between devices with their start and end apart: 25 -> 0, of which waited for: 21 -> 0; matrix products, arithmetic and copies ran while one was open for 26% -> 0% of each run, Pallas kernels for 0% -> 0%
where the time goes in v2:
time: 431 us; the launch traced here: 423 us
  Pallas kernels  399 us (93%)
  local copies, waits for them, and re-layouts  19 us (4%)
    pallas_call x2, Pallas kernels, call(): pl.pallas_call(kernel, in_specs=self.specs, out_specs=[ANYWHERE] * count_...  363 us
    pallas_call x1, Pallas kernels, prepare(): pl.pallas_call(prepare_body, grid=(pl.cdiv(length, rows),), in_specs=[sca...  23.1 us
    pallas_call x1, Pallas kernels, finish(): pl.pallas_call(body, grid_spec=pltpu.PrefetchScalarGridSpec(num_scalar_pr...  12.5 us

profile of v2, /device:TPU:0, one launch (start us, length us, event | category | flops | bytes accessed | tf_op | source)
XLA Modules:
  0.0 422.7 jit_solution(8782351107350390303)
XLA Ops:
  0.6 0.0 copy-start.11
  0.7 0.8 pad.20
  1.4 0.1 reshape.110
  1.5 0.1 rev.10
  1.7 0.8 reshape.108
  2.5 0.0 copy-start.5
  3.2 1.7 copy.45
  4.9 0.0 copy-done.11
  4.9 0.0 copy-start.12
  5.0 0.0 copy-start.13
  5.0 1.7 pad_maximum_fusion.own_ref.refs_0_.refs_24_
  6.7 0.0 copy-done.12
  6.7 0.0 copy-done.13
  6.7 0.0 copy-done.5
  6.7 0.0 copy-start.10
  6.7 23.1 %prepare.1 = (bf16[1152,729]{1,0:T(8,128)(2,1)S(1)}, bf16[1152,729]{1,0:T(8,128)(2,1)}, bf16[1152,729]{1,0:T(8,128)(2,1)}, f32[2,729]{1,0:T(2,128)S(1)}, bf16[2,...) custom-call(s32[1]{0:T(128)} %bitcast.slot_ref, s32[1]{0:T(128)} %bitcast.7.live_ref.refs_14_, ...), custom_call_target="tpu_custom_call" | custom-call | tf_op jit(solution)/shard_map/prepare/pallas_call | solution.py:920
  29.8 0.0 copy-start.6
  29.8 0.0 copy-start.7
  29.8 0.0 copy-start.8
  29.9 0.0 copy-start.9
  29.9 0.0 copy-done.10
  29.9 0.0 copy-start.14
  29.9 0.0 copy-start.15
  29.9 0.0 copy-start.16
  29.9 0.0 copy-start.17
  29.9 1.9 pad.22
  31.8 0.1 copy-done.6
  31.9 0.4 copy-done.7
  32.3 0.0 copy-done.8
  32.3 0.0 copy-done.9
  32.3 0.0 copy-done.14
  32.3 0.0 copy-done.15
  32.4 0.0 copy-done.16
  32.4 0.0 copy-done.17
  32.4 0.1 stack.41
  32.5 0.2 copy.49
  32.7 0.9 convert_element_type.26.refs_6_.refs_13_
  33.6 85.6 %forward.1 = (bf16[2,2,288,1152]{3,2,1,0:T(8,128)(2,1)}, bf16[2,2,288,1152]{3,2,1,0:T(8,128)(2,1)}, bf16[2,288,1152]{2,1,0:T(8,128)(2,1)}, bf16[2,288,1152]{2,1,...) custom-call(bf16[2,2,288,1152]{3,2,1,0:T(8,128)(2,1)} %pad_maximum_f, ...), custom_call_target="tpu_custom_call" | custom-call | flops 30000001024 | bytes 67108864 | tf_op jit(solution)/shard_map/forward/pallas_call | solution.py:417
  119.1 3.4 pad.23
  122.5 277.8 %backward.1 = (bf16[2,2,272,1152]{3,2,1,0:T(8,128)(2,1)}, bf16[2,2,272,1152]{3,2,1,0:T(8,128)(2,1)}, bf16[2,272,1152]{2,1,0:T(8,128)(2,1)}, bf16[2,272,1152]{2,1...) custom-call(bf16[16,3,72,729]{3,2,1,0:T(8,128)(2,1)} %get-tuple-elem, ...), custom_call_target="tpu_custom_call" | custom-call | flops 80000000000 | bytes 67108864 | tf_op jit(solution)/shard_map/backward/pallas_call | solution.py:417
  400.3 0.7 slice.49
  401.0 0.2 rev.11
  401.3 0.7 reshape.114
  401.9 0.7 reshape.115
  402.6 0.1 pad_add_fusion.at
  402.7 0.0 copy-start
  402.7 1.3 copy-done
  404.0 0.0 copy-start.1
  404.0 1.2 copy-done.1
  405.2 0.0 copy-start.2
  405.2 1.2 copy-done.2
  406.4 0.0 copy-start.3
  406.4 1.0 copy-done.3
  407.4 0.0 copy-start.4
  407.4 1.0 copy-done.4
  408.4 12.5 %finish.1 = (f32[1076,1152]{1,0:T(8,128)}, f32[1076,1152]{1,0:T(8,128)}, f32[288,1152]{1,0:T(8,128)}, f32[3,288,1152]{2,1,0:T(8,128)}, f32[4,288,729]{2,1,0:T(8,128)}, /*index=5*/f32[4,288,729]{2,1,0:T(8,128)}) custom-call(s32[2]{0:T(128)S(1)} %pad_add_fusion.at, bf16[2,272,1152]{2,1,0:T(8,128)(2,1)S(1)} %copy-done, ...), custom_call_target="tpu_custom_call" | custom-call | tf_op jit(solution)/shard_map/finish/pallas_call | solution.py:1580
  420.9 0.7 slice.46
  421.6 0.7 dynamic-slice_reduce_fusion
  (23 shorter events, 0.2 us)
Async XLA Ops:
  0.6 4.3 %copy-start.11 = (bf16[288,1152]{1,0:T(8,128)(2,1)S(1)}, bf16[288,1152]{1,0:T(8,128)(2,1)}, u32[]{:S(2)}) copy-start(bf16[288,1152]{1,0:T(8,128)(2,1)} %param.21) | copy-start | bytes 1990660
  2.5 4.2 copy-start.5
  4.9 1.7 copy-start.12
  5.0 1.7 copy-start.13
  6.7 23.2 %copy-start.10 = (bf16[1152,1076]{0,1:T(8,128)(2,1)S(1)}, bf16[1152,1076]{0,1:T(8,128)(2,1)}, u32[]{:S(2)}) copy-start(bf16[1152,1076]{0,1:T(8,128)(2,1)} %param.25) | copy-start | bytes 7437316
  29.8 2.0 copy-start.6
  29.8 2.5 copy-start.7
  29.8 2.5 copy-start.8
  29.9 2.4 copy-start.9
  29.9 2.4 copy-start.14
  29.9 2.4 copy-start.15
  29.9 2.5 copy-start.16
  29.9 2.5 copy-start.17
  402.7 1.3 copy-start
  404.0 1.2 copy-start.1
  405.2 1.2 copy-start.2
  406.4 1.0 copy-start.3
  407.4 1.0 copy-start.4

commit v3 on v2

--- a/solution.py
+++ b/solution.py
@@ -421,7 +421,7 @@
             out_shape=self.shapes,
             scratch_shapes=self.scratches,
             compiler_params=pltpu.CompilerParams(
-                vmem_limit_bytes=63 << 20, collective_id=collective_id, has_side_effects=True
+                vmem_limit_bytes=67_043_328, collective_id=collective_id, has_side_effects=True
             ),
             cost_estimate=pl.CostEstimate(
                 flops=int(cost), bytes_accessed=1 << 26, transcendentals=0
@@ -566,95 +566,85 @@
                 self._swap(shard, lane).wait_send()
 
 
-class Swap:
-    def __init__(self, program, source, shape):
-        self.source = source
-        self.got = program.output(*shape)
-        self.sems = program.sems(2, shape[0])
-
-    def bind(self, ref):
-        self.refs = ref(self.source), ref(self.got), ref(self.sems)
-        return self
-
-    def _hop(self, k):
-        source, got, sems = self.refs
-        return hop(source.at[k], got.at[k], sems, k, CORE)
-
-    def start(self, *parts):
-        for k in parts:
-            self._hop(k).start()
-
-    def wait(self, *parts):
-        for k in parts:
-            self._hop(k).wait()
-
-
 class Plane:
     KEPT = {X: (0, 2), Y: (0, 1)}
     GONE = {X: (1, 3), Y: (2, 3)}
 
-    def __init__(self, program, rows, shape):
+    def __init__(self, program, shape, share=None):
         _, count, unit, width = shape
-        self.rows = rows
-        self.base = program.tile(count, 2, unit, width)
-        self.got = program.tile(count, 2, unit, width)
-        self.last = program.tile(count, unit, width)
+        self.unit = unit
+        if share is None:
+            self.base = program.tile(count, 2, unit, width)
+            self.sent = program.tile(count, 2, unit, width)
+            self.got = program.tile(count, 2, unit, width)
+            self.last = program.tile(count, unit, width)
+        else:
+            self.base, self.sent = share.base, share.sent
+            self.got, self.last = share.got, share.last
         self.sems = program.sems(2, 6)
-        self.local = program.sems(4)
+        self.swap_sems = program.sems(2, 8)
 
     def bind(self, ref):
-        self.refs = [ref(h) for h in (self.rows, self.base, self.got, self.last, self.sems)]
-        self.loads = ref(self.local)
+        self.refs = [ref(h) for h in (self.base, self.sent, self.got, self.last, self.sems)]
+        self.swaps = ref(self.swap_sems)
         return self
 
+    def tile(self, shard, lane):
+        first = LANES[lane]
+        if shard in self.KEPT[first]:
+            return self._part(0, lane, self.KEPT[first].index(shard))
+        return self._part(1, lane, self.GONE[first].index(shard))
+
+    def swap(self, source, shard, lane, static=0):
+        return hop(source, self.tile(static, lane), self.swaps, 2 * shard + lane, CORE)
+
+    def _part(self, which, *at):
+        return self.refs[which].at[*at, pl.ds(0, self.unit)]
+
     def _first(self, lane, k):
-        rows, base, got, last, sems = self.refs
-        first = LANES[lane]
+        at = (lane, k)
         return hop(
-            rows.at[self.GONE[first][k], lane], got.at[lane, k], sems, 2 * lane + k, first
-        )
-
-    def _load(self, lane, k):
-        rows, base = self.refs[:2]
-        return pltpu.make_async_copy(
-            rows.at[self.KEPT[LANES[lane]][k], lane], base.at[lane, k], self.loads.at[2 * lane + k]
+            self._part(1, *at), self._part(2, *at), self.refs[4], 2 * lane + k, LANES[lane]
         )
 
     def _next(self, lane):
-        rows, base, got, last, sems = self.refs
-        return hop(base.at[lane, 1], last.at[lane], sems, 4 + lane, OTHER[LANES[lane]])
-
-    def send(self, shard):
-        for lane, first in enumerate(LANES):
-            if shard in self.GONE[first]:
-                self._first(lane, self.GONE[first].index(shard)).start()
-            else:
-                self._load(lane, self.KEPT[first].index(shard)).start()
-
-    def start(self):
-        for shard in (3, 1, 2, 0):
-            self.send(shard)
+        return hop(
+            self._part(0, lane, 1),
+            self._part(3, lane),
+            self.refs[4],
+            4 + lane,
+            OTHER[LANES[lane]],
+        )
+
+    def add(self, shard, lane, values, go):
+        tile = self.tile(shard, lane)
+        tile[...] = (values + tile[...].astype(F32)).astype(BF)
+        if go and shard in self.GONE[LANES[lane]]:
+            self._first(lane, self.GONE[LANES[lane]].index(shard)).start()
+
+    def launch(self):
+        for k in (1, 0):
+            for lane in range(2):
+                self._first(lane, k).start()
+
+    def _add(self, lane, k):
+        self._first(lane, k).wait_recv()
+        base = self._part(0, lane, k)
+        base[...] = base[...] + self._part(2, lane, k)[...]
 
     def forward(self):
-        rows, base, got, last, sems = self.refs
+        for lane in (1, 0):
+            self._add(lane, 1)
+            self._next(lane).start()
+
+    def settle(self):
         for lane in range(2):
-            self._load(lane, 1).wait()
-            self._first(lane, 1).wait_recv()
-            base[lane, 1] += got[lane, 1]
-            self._next(lane).start()
-
-    def settle(self):
-        rows, base, got, last, sems = self.refs
-        for lane in range(2):
-            self._load(lane, 0).wait()
-            self._first(lane, 0).wait_recv()
-            base[lane, 0] += got[lane, 0]
+            self._add(lane, 0)
 
     def finish(self, line):
-        rows, base, got, last, sems = self.refs
         for lane in range(2):
             self._next(lane).wait_recv()
-            line.take(lane, base[lane, 0] + last[lane])
+            line.take(lane, self._part(0, lane, 0)[...] + self._part(3, lane)[...])
 
     def drain(self):
         for lane in range(2):
@@ -664,13 +654,17 @@
 
 
 class Line:
-    def __init__(self, program, shape):
+    def __init__(self, program, shape, share=None):
         count, unit, width = shape
+        self.unit = unit
         self.total = program.output(*shape)
         self.other = program.output(*shape)
-        self.held = program.tile(*shape)
-        self.outer = program.tile(*shape)
-        self.middle = program.tile(*shape)
+        if share is None:
+            self.held = program.tile(*shape)
+            self.outer = program.tile(*shape)
+            self.middle = program.tile(*shape)
+        else:
+            self.held, self.outer, self.middle = share.held, share.outer, share.middle
         self.sems = program.sems(2, 4 * count)
         self.local = program.sems(count)
         self.count = count
@@ -679,9 +673,9 @@
         self.refs = Bag(
             total=ref(self.total),
             other=ref(self.other),
-            held=ref(self.held),
-            outer=ref(self.outer),
-            middle=ref(self.middle),
+            held=ref(self.held).at[:, pl.ds(0, self.unit)],
+            outer=ref(self.outer).at[:, pl.ds(0, self.unit)],
+            middle=ref(self.middle).at[:, pl.ds(0, self.unit)],
             sems=ref(self.sems),
             local=ref(self.local),
         )
@@ -733,7 +727,7 @@
             self._hop(SWAP, k, CORE).start()
             self._store(k).start()
 
-    def finish(self, k):
+    def collect(self, k):
         r = self.refs
 
         @pl.when(self.is_outer)
@@ -744,6 +738,7 @@
             self._hop(SWAP, k, CORE).start()
             self._store(k).start()
 
+    def done(self, k):
         pl.when(self.is_inner)(lambda: self._hop(BACK, k, self.up).wait_send())
         self._store(k).wait()
         self._hop(SWAP, k, CORE).wait()
@@ -1026,7 +1021,7 @@
     stream = Stream(p, 1, unit, width)
     qkv, mixed = p.output(heads, 3, HD, length), p.output(heads, HD, length)
     lse = p.output(heads, 1, length, dtype=F32)
-    residual, normed = p.output(width, length, dtype=F32), p.output(width, length)
+    residual, normed = p.output(2, width, 384, dtype=F32), p.output(width, length)
     stats, out_all = p.output(2, length, dtype=F32), p.output(heads, HD, width)
     act, slope = p.output(8, rows, length), p.output(8, rows, length)
     held = Bag(
@@ -1036,7 +1031,7 @@
         v=p.tile(*vectors.shape, dtype=F32),
         o=p.tile(heads, HD, length),
         w=p.tile(heads, HD, width),
-        h=p.tile(width, length, dtype=F32),
+        h=p.tile(2, width, 384, dtype=F32),
         n2=p.tile(width, length),
         s=p.tile(2, length, dtype=F32),
     )
@@ -1147,14 +1142,14 @@
         stream.begin(fc1, 0)
         store_w = fetch(hold.w, ref(out_all), sem.at[4])
         weight = hold.w[...].reshape(width, width)
-        for block in columns_of(length, 256):
+        for block in columns_of(length, 384):
             mix = hold.o[:, :, block].reshape(width, -1)
             values = hold.x[:, block].astype(F32) + contract_rows(weight, mix)
             values = values + hold.v[:, 2:3]
             average = jnp.mean(values, axis=0, keepdims=True)
             centered = values - average
             inverse = lax.rsqrt(jnp.mean(centered * centered, axis=0, keepdims=True) + EPS)
-            hold.h[:, block] = values
+            hold.h[block.start // 384, :, 0 : block.stop - block.start] = values
             hold.n2[:, block] = (
                 centered * inverse * hold.v[:, 3:4] + hold.v[:, 4:5]
             ).astype(BF)
@@ -1250,11 +1245,10 @@
 
     fc_shape, out_shape, qkv_shape = ((4, 2, u, width) for u in (unit, HD, block))
     shapes = (fc_shape, fc_shape, out_shape, qkv_shape)
-    part = [p.output(*shape) for shape in shapes]
-    mine = [p.output(*shape) for shape in shapes]
-    swap = [Swap(p, source, shape) for source, shape in zip(part, shapes)]
-    plane = [Plane(p, source, shape) for source, shape in zip(mine, shapes)]
-    line = [Line(p, shape[1:]) for shape in shapes]
+    plane = [Plane(p, shape) for shape in shapes[:QKV]]
+    plane.append(Plane(p, shapes[QKV], plane[FC2]))
+    line = [Line(p, shape[1:]) for shape in shapes[:QKV]]
+    line.append(Line(p, shapes[QKV][1:], line[FC2]))
     d_pre = p.output(8, rows, length)
     pull = p.output(16, HD, length)
     d_qkv = p.output(16, 3, HD, length)
@@ -1267,7 +1261,7 @@
         normed_two=p.tile(width, length),
         normed_one=p.tile(width, length),
         low=p.tile(width, length),
-        residual=p.tile(width, length, dtype=F32),
+        residual=p.tile(width, 384, dtype=F32),
         acc=p.tile(width, length, dtype=F32),
         vectors=p.tile(*arrays.vectors.shape, dtype=F32),
         cols=p.tile(width, 8, dtype=F32),
@@ -1275,7 +1269,11 @@
         stats_one=p.tile(2, length, dtype=F32),
         dk=p.tile(length, HD, dtype=F32),
         dv=p.tile(length, HD, dtype=F32),
-    )
+        rows=p.tile(2, rows, length),
+        heads=p.tile(2, 2, 3, HD, length),
+        part=p.tile(2, 2, unit, width),
+    )
+    tile_sems = p.sems(2)
     sems = p.sems(12)
 
     def script(ref):
@@ -1283,7 +1281,7 @@
         sem = ref(sems)
         for each in (fc1, attn, fc2, stream, spread_block, spread_input, vectors):
             each.bind(ref)
-        for group in (swap, plane, line):
+        for group in (plane, line):
             for each in group:
                 each.bind(ref)
         vec = vectors.refs.held
@@ -1293,7 +1291,6 @@
         copies = Bag(
             upstream=fetch(array.upstream, hold.upstream, sem.at[0]),
             normed_two=fetch(array.normed_two, hold.normed_two, sem.at[1]),
-            residual=fetch(array.residual, hold.residual, sem.at[2]),
             vectors=fetch(array.vectors, hold.vectors, sem.at[3]),
             stats_two=fetch(array.stats_two, hold.stats_two, sem.at[4]),
             normed_one=fetch(array.normed_one, hold.normed_one, sem.at[5]),
@@ -1306,56 +1303,121 @@
         copies.upstream.wait()
         copies.normed_two.wait()
 
-        def gradient(source, other, name, half, shards, plus=False, events=()):
-            _, lanes, size, _ = shapes[name]
-            count = lanes * size
-            pick = lambda i: jnp.where(i == 0, shards[0], shards[-1]) if len(shards) < 4 else i
-
-            def body(step, *refs):
-                sums = contract_cols(refs[0][...].reshape(count, length), other[...])
-                if plus:
-                    sums = sums + refs[1][0].reshape(count, width).astype(F32)
-                refs[-1][0] = sums.astype(BF).reshape(lanes, size, width)
-
-            lead = source.shape[0] // 8
-            tail = source.shape[1:]
-            out_spec = spec((1, lanes, size, width), lambda i: (pick(i), 0, 0, 0))
-            zeros = (0,) * len(tail)
-            phase(
-                len(shards),
-                body,
-                [source] + ([swap[name].refs[1]] if plus else []),
-                [spec((lead, *tail), lambda i: (2 * pick(i) + half, *zeros))]
-                + ([out_spec] if plus else []),
-                [ref((part, mine)[half == 0][name])],
-                [out_spec],
-                events,
+        tile_sem = ref(tile_sems)
+
+        def rows_in(source, index, slot):
+            if len(source.shape) == 3 and source.shape[0] == 8:
+                target = hold.rows.at[slot]
+                source = source.at[index]
+            elif len(source.shape) == 3:
+                target = hold.heads.at[slot, :, 0]
+                source = source.at[pl.ds(2 * index, 2)]
+            else:
+                target = hold.heads.at[slot]
+                source = source.at[pl.ds(2 * index, 2)]
+            return pltpu.make_async_copy(source, target, tile_sem.at[slot])
+
+        def rows_of(source, slot, count):
+            if len(source.shape) == 3 and source.shape[0] == 8:
+                return hold.rows[slot]
+            if len(source.shape) == 3:
+                return hold.heads[slot, :, 0].reshape(count, length)
+            return hold.heads[slot].reshape(count, length)
+
+        def gradient(source, other, name, shards, go=True):
+            _, _, size, _ = shapes[name]
+            count = 2 * size
+            total = len(shards)
+
+            def pick(i):
+                if total == 1:
+                    return shards[0]
+                if total == 2:
+                    return jnp.where(i == 0, shards[0], shards[1])
+                return jnp.where(
+                    i < 2,
+                    jnp.where(i == 0, shards[0], shards[1]),
+                    jnp.where(i == 2, shards[2], shards[3]),
+                )
+
+            part_of = lambda slot, lane: hold.part.at[slot, lane, pl.ds(0, size)]
+            sums_of = plane[name]
+            piece = lambda k: jnp.where(
+                k < total, 2 * pick(k) + 1, 2 * pick(jnp.maximum(k - total, 0))
             )
-
-        every = (0, 1, 2, 3)
-        gradient(array.act, hold.upstream, FC2, 1, every)
-        swap[FC2].start(*every)
+            rows_in(source, 2 * shards[0] + 1, 0).start()
+
+            def product(k):
+                slot = lax.rem(k, 2)
+
+                @pl.when(k + 1 < 2 * total)
+                def _():
+                    rows_in(source, piece(k + 1), 1 - slot).start()
+
+                rows_in(source, 0, slot).wait()
+                return contract_cols(rows_of(source, slot, count), other[...])
+
+            def give(i, _):
+                slot = lax.rem(i, 2)
+                sums = product(i).astype(BF).reshape(2, size, width)
+                shard = pick(i)
+
+                @pl.when(i >= 2)
+                def _():
+                    for lane in range(2):
+                        sums_of.swap(
+                            part_of(slot, lane), pick(jnp.maximum(i - 2, 0)), lane
+                        ).wait_send()
+
+                for lane in range(2):
+                    part_of(slot, lane)[...] = sums[lane]
+                for each in shards:
+
+                    @pl.when(shard == each)
+                    def _():
+                        for lane in range(2):
+                            sums_of.swap(part_of(slot, lane), each, lane, each).start()
+
+                return 0
+
+            def keep(i, _):
+                shard = pick(i)
+                sums = product(total + i).reshape(2, size, width)
+                for each in shards:
+
+                    @pl.when(shard == each)
+                    def _():
+                        for lane in range(2):
+                            sums_of.swap(part_of(0, lane), each, lane, each).wait_recv()
+                            sums_of.add(each, lane, sums[lane], go)
+
+                return 0
+
+            lax.fori_loop(0, total, give, 0)
+            lax.fori_loop(0, total, keep, 0)
+            for i in range(max(total - 2, 0), total):
+                for lane in range(2):
+                    sums_of.swap(part_of(i % 2, lane), shards[i], lane).wait_send()
+
+        every = (3, 1, 2, 0)
+        gradient(array.act, hold.upstream, FC2, every, False)
 
         def hidden(first, count, events=()):
             def body(step, slope_ref, d_ref):
                 weight = stream.bring(fc2, step, first, first + count)
-                values = dot_nn(weight, hold.upstream[...])
-                values = (values * slope_ref[...].reshape(2 * rows, length).astype(F32)).astype(BF)
-                d_ref[...] = values.reshape(2, rows, length)
                 for half in range(2):
-                    sums = jnp.sum(
-                        values[half * rows : (half + 1) * rows].astype(F32), axis=1, keepdims=True
-                    )
+                    values = dot_nn(weight[half * rows : (half + 1) * rows], hold.upstream[...])
+                    values = (values * slope_ref[half].astype(F32)).astype(BF)
+                    d_ref[half] = values
+                    sums = jnp.sum(values.astype(F32), axis=1, keepdims=True)
                     vec[8 + 2 * (first + step) + half, :, 0:rows] = as_row(sums)
 
             pair = spec((2, rows, length), lambda i: (first + i, 0, 0))
             phase(count, body, [array.slope], [pair], [ref(d_pre)], [pair], events)
 
+        fc2.forward()
+        plane[FC2].launch()
         hidden(0, 1)
-        fc2.forward()
-        swap[FC2].wait(*every)
-        gradient(array.act, hold.upstream, FC2, 0, every, True)
-        plane[FC2].start()
         fc2.near_here()
         fc2.near_whole()
         stream.begin(fc2, 1)
@@ -1368,7 +1430,8 @@
         def back(weights, values, lead, size, events=()):
             def body(step, d_ref):
                 weight = stream.bring(weights, step, 0, 4, size)
-                sums = contract_rows(weight, d_ref[...].reshape(4 * size, length))
+                values = d_ref[...].reshape(4 * size, length)
+                sums = contract_rows(weight, values)
 
                 @pl.when(step == 0)
                 def _():
@@ -1384,13 +1447,14 @@
 
         stream.begin(fc1, 0)
         back(fc1, ref(d_pre), 2, unit)
-        for each in (copies.residual, copies.vectors, copies.stats_two):
+        for each in (copies.vectors, copies.stats_two):
             each.wait()
         total = lambda values: jnp.sum(values, axis=1, keepdims=True)
+        residual_of = halves_of(array.residual, hold.residual, sem.at[2])
         for cut in columns_of(length):
             inverse = hold.stats_two[1:2, cut]
             grad = hold.acc[:, cut]
-            units = (hold.residual[:, cut] - hold.stats_two[0:1, cut]) * inverse
+            units = (residual_of(cut) - hold.stats_two[0:1, cut]) * inverse
             up = hold.upstream[:, cut].astype(F32)
             d_residual = up + norm_back(grad, units, inverse, hold.vectors[:, 3:4])
             hold.low[:, cut] = d_residual.astype(BF)
@@ -1399,8 +1463,6 @@
             hold.cols[:, 4:5] += total(grad)
             hold.cols[:, 5:6] += total(up)
 
-        gradient(ref(d_pre), hold.normed_two, FC1, 1, every)
-        swap[FC1].start(*every)
         plane[FC2].forward()
         plane[FC2].settle()
         picture_copy = fetch(array.picture, hold.upstream, sem.at[7])
@@ -1413,19 +1475,14 @@
         phase(
             4, pull_body, [array.out_all], [quarter(HD, width)], [ref(pull)], [quarter(HD, length)]
         )
-        gradient(array.mixed, hold.low, OUT, 1, every)
-        swap[OUT].start(*every)
-        swap[FC1].wait(*every)
-        gradient(ref(d_pre), hold.normed_two, FC1, 0, every, True)
-        plane[FC1].start()
+        gradient(ref(d_pre), hold.normed_two, FC1, every)
         plane[FC2].finish(line[FC2])
-        swap[OUT].wait(*every)
-        gradient(array.mixed, hold.low, OUT, 0, every, True)
-        plane[OUT].start()
+        plane[FC2].drain()
+        gradient(array.mixed, hold.low, OUT, every)
         copies.normed_one.wait()
 
         def heads_back(shards, events):
-            shard_of = lambda i: jnp.where(i < 4, shards[0], shards[1])
+            shard_of = lambda i: jnp.where(i < 4, shards[0], shards[-1])
             at = lambda i: 4 * shard_of(i) + lax.rem(i, 4)
 
             def body(step, qkv_ref, do_ref, o_ref, lse_ref, d_ref):
@@ -1443,7 +1500,7 @@
             flat = spec((1, HD, length), lambda i: (at(i), 0, 0))
             many = spec((1, 3, HD, length), lambda i: (at(i), 0, 0, 0))
             phase(
-                8,
+                4 * len(shards),
                 body,
                 [array.qkv, ref(pull), array.mixed, array.lse],
                 [many, flat, flat, spec((1, 1, length), lambda i: (at(i), 0, 0))],
@@ -1452,57 +1509,55 @@
                 events,
             )
 
-        heads_back((3, 1), [(6, lambda: line[FC2].meet(0))])
-        gradient(ref(d_qkv), hold.normed_one, QKV, 1, (3, 1))
-        swap[QKV].start(3, 1)
-
         def settle(name):
             plane[name].forward()
             plane[name].settle()
 
-        heads_back(
-            (2, 0),
-            [
-                (2, lambda: line[FC2].meet(1)),
-                (2, lambda: settle(FC1)),
-                (3, lambda: line[FC2].leave(0)),
-                (6, lambda: settle(OUT)),
-            ],
-        )
-        swap[QKV].wait(3, 1)
-        gradient(ref(d_qkv), hold.normed_one, QKV, 0, (3, 1), True)
-        plane[QKV].send(3)
-        plane[QKV].send(1)
-        gradient(ref(d_qkv), hold.normed_one, QKV, 1, (2, 0))
-        swap[QKV].start(2, 0)
-        line[FC2].leave(1)
+        heads_back((3, 1), [(6, lambda: line[FC2].meet(0))])
+        settle(FC1)
+        gradient(ref(d_qkv), hold.normed_one, QKV, (3, 1))
+        heads_back((2,), [(1, lambda: line[FC2].meet(1)), (3, lambda: line[FC2].leave(0))])
+        gradient(ref(d_qkv), hold.normed_one, QKV, (2,))
+        settle(OUT)
         plane[FC1].finish(line[FC1])
+        heads_back((0,), [(1, lambda: line[FC2].leave(1)), (3, lambda: line[FC2].collect(0))])
+        gradient(ref(d_qkv), hold.normed_one, QKV, (0,))
+        plane[QKV].forward()
+        line[FC1].meet(0)
         plane[OUT].finish(line[OUT])
         stream.begin(fc2, 0)
-        swap[QKV].wait(2, 0)
-        gradient(ref(d_qkv), hold.normed_one, QKV, 0, (2, 0), True)
-        plane[QKV].send(2)
-        plane[QKV].send(0)
-        line[FC2].finish(0)
-        back(fc2, array.act, 2, unit, [(3, lambda: line[FC1].meet(0))])
-        line[FC2].finish(1)
+        back(
+            fc2,
+            array.act,
+            2,
+            unit,
+            [(2, lambda: plane[QKV].settle()), (2, lambda: line[FC2].collect(1)), (3, lambda: line[FC1].meet(1))],
+        )
+        for k in range(2):
+            line[FC2].done(k)
+        plane[QKV].finish(line[QKV])
+        stream.begin(attn, 0, block)
+        residual_of = halves_of(array.residual, hold.residual, sem.at[2])
         for cut in columns_of(length):
-            values = hold.residual[:, cut] + hold.acc[:, cut] + hold.vectors[:, 5:6]
+            values = residual_of(cut) + hold.acc[:, cut] + hold.vectors[:, 5:6]
             hold.normed_two[:, cut] = (values * live_now).astype(BF)
         store_rows(hold.normed_two, ref(block_rows), sem, share)
-        settle(QKV)
         spread_block.start()
-        line[FC1].meet(1)
         line[FC1].leave(0)
         line[OUT].meet(0)
         line[OUT].meet(1)
         picture_copy.wait()
         copies.stats_one.wait()
-        stream.begin(attn, 0, block)
-        back(attn, ref(d_qkv), 4, block, [(2, lambda: line[FC1].leave(1))])
+        back(
+            attn,
+            ref(d_qkv),
+            4,
+            block,
+            [(2, lambda: line[FC1].leave(1)), (3, lambda: line[QKV].meet(0))],
+        )
         line[OUT].leave(0)
         line[OUT].leave(1)
-        plane[QKV].finish(line[QKV])
+        line[FC1].collect(0)
         for cut in columns_of(length):
             inverse = hold.stats_one[1:2, cut]
             grad = hold.acc[:, cut]
@@ -1516,23 +1571,24 @@
             hold.cols[:, 1:2] += total(grad)
         store_rows(hold.normed_two, ref(input_rows), sem, share)
         spread_input.start()
+        line[QKV].meet(1)
+        line[QKV].leave(0)
         wide = hold.cols[...].T
         for k in range(8):
             vec[k] = wide[k : k + 1]
-        line[QKV].meet(0)
         vectors.run()
-        line[QKV].meet(1)
-        line[QKV].leave(0)
-        line[FC1].finish(0)
-        line[FC1].finish(1)
-        line[OUT].finish(0)
-        line[OUT].finish(1)
         line[QKV].leave(1)
+        line[FC1].collect(1)
+        for k in range(2):
+            line[OUT].collect(k)
+        for k in range(2):
+            line[QKV].collect(k)
         spread_block.finish()
         spread_input.finish()
-        line[QKV].finish(0)
-        line[QKV].finish(1)
-        for each in plane:
+        for each in line[1:]:
+            for k in range(2):
+                each.done(k)
+        for each in plane[1:]:
             each.drain()
         fc2.drain()
 
@@ -1543,6 +1599,23 @@
         (result(input_rows), result(spread_input.landed)),
     ]
     return sums, spreads, result(vectors.total)[:, 0]
+
+
+def halves_of(source, held, sem):
+    width = held.shape[1]
+
+    def bring(part):
+        return fetch(source.at[part], held, sem)
+
+    bring(0).wait()
+
+    def columns(cut):
+        if cut.start == width:
+            bring(1).wait()
+        first = cut.start % width
+        return held[:, first : first + cut.stop - cut.start]
+
+    return columns
 
 
 def store_rows(source, target, sem, share):

time: 431 us -> 407 us (0.944)
  Pallas kernels: 399 us -> 376 us
    pallas_call x2, Pallas kernels: 363 us -> 340 us  [call(): pl.pallas_call(kernel, in_specs=self.specs, out_specs=[ANYWHERE] * count_...]
where the time goes in v3:
time: 407 us; the launch traced here: 399 us
  Pallas kernels  376 us (92%)
  local copies, waits for them, and re-layouts  19 us (5%)
    pallas_call x2, Pallas kernels, call(): pl.pallas_call(kernel, in_specs=self.specs, out_specs=[ANYWHERE] * count_...  340 us
    pallas_call x1, Pallas kernels, prepare(): pl.pallas_call(prepare_body, grid=(pl.cdiv(length, rows),), in_specs=[sca...  23 us
    pallas_call x1, Pallas kernels, finish(): pl.pallas_call(body, grid_spec=pltpu.PrefetchScalarGridSpec(num_scalar_pr...  12.5 us

profile of v3, /device:TPU:0, one launch (start us, length us, event | category | flops | bytes accessed | tf_op | source)
XLA Modules:
  0.0 399.1 jit_solution(859717676206740268)
XLA Ops:
  0.6 0.0 copy-start.11
  0.7 0.8 pad.20
  1.4 0.1 reshape.110
  1.5 0.1 rev.10
  1.7 0.8 reshape.108
  2.5 0.0 copy-start.5
  3.2 1.7 copy.45
  4.9 0.0 copy-done.11
  4.9 0.0 copy-start.12
  5.0 0.0 copy-start.13
  5.0 1.7 pad_maximum_fusion.own_ref.refs_0_.refs_24_
  6.7 0.0 copy-done.12
  6.7 0.0 copy-done.13
  6.7 0.0 copy-done.5
  6.7 0.0 copy-start.10
  6.7 23.0 %prepare.1 = (bf16[1152,729]{1,0:T(8,128)(2,1)S(1)}, bf16[1152,729]{1,0:T(8,128)(2,1)}, bf16[1152,729]{1,0:T(8,128)(2,1)}, f32[2,729]{1,0:T(2,128)S(1)}, bf16[2,...) custom-call(s32[1]{0:T(128)} %bitcast.slot_ref, s32[1]{0:T(128)} %bitcast.7.live_ref.refs_14_, ...), custom_call_target="tpu_custom_call" | custom-call | tf_op jit(solution)/shard_map/prepare/pallas_call | solution.py:915
  29.8 0.0 copy-start.6
  29.8 0.0 copy-start.7
  29.8 0.0 copy-start.8
  29.8 0.0 copy-start.9
  29.8 0.0 copy-done.10
  29.8 0.0 copy-start.14
  29.8 0.0 copy-start.15
  29.8 0.0 copy-start.16
  29.9 0.0 copy-start.17
  29.9 1.8 pad.22
  31.7 0.1 copy-done.6
  31.8 0.4 copy-done.7
  32.2 0.0 copy-done.8
  32.2 0.0 copy-done.9
  32.3 0.0 copy-done.14
  32.3 0.0 copy-done.15
  32.3 0.0 copy-done.16
  32.3 0.0 copy-done.17
  32.4 0.1 stack.41
  32.4 0.2 copy.49
  32.6 0.9 convert_element_type.26.refs_6_.refs_13_
  33.5 86.1 %forward.1 = (bf16[2,2,288,1152]{3,2,1,0:T(8,128)(2,1)}, bf16[2,2,288,1152]{3,2,1,0:T(8,128)(2,1)}, bf16[2,288,1152]{2,1,0:T(8,128)(2,1)}, bf16[2,288,1152]{2,1,...) custom-call(bf16[2,2,288,1152]{3,2,1,0:T(8,128)(2,1)} %pad_maximum_f, ...), custom_call_target="tpu_custom_call" | custom-call | flops 30000001024 | bytes 67108864 | tf_op jit(solution)/shard_map/forward/pallas_call | solution.py:417
  119.6 3.4 pad.23
  122.9 253.9 %backward.1 = (bf16[2,2,272,1152]{3,2,1,0:T(8,128)(2,1)}, bf16[2,2,272,1152]{3,2,1,0:T(8,128)(2,1)}, bf16[2,272,1152]{2,1,0:T(8,128)(2,1)}, bf16[2,272,1152]{2,1...) custom-call(bf16[16,3,72,729]{3,2,1,0:T(8,128)(2,1)} %get-tuple-elem, ...), custom_call_target="tpu_custom_call" | custom-call | flops 80000000000 | bytes 67108864 | tf_op jit(solution)/shard_map/backward/pallas_call | solution.py:417
  376.8 0.7 slice.49
  377.5 0.2 rev.11
  377.9 0.7 reshape.114
  378.5 0.7 reshape.115
  379.2 0.1 pad_add_fusion.at
  379.3 0.0 copy-start
  379.3 1.3 copy-done
  380.6 0.0 copy-start.1
  380.6 1.2 copy-done.1
  381.8 0.0 copy-start.2
  381.8 1.2 copy-done.2
  383.0 0.0 copy-start.3
  383.0 1.0 copy-done.3
  384.0 0.0 copy-start.4
  384.0 1.0 copy-done.4
  384.9 12.5 %finish.1 = (f32[1076,1152]{1,0:T(8,128)}, f32[1076,1152]{1,0:T(8,128)}, f32[288,1152]{1,0:T(8,128)}, f32[3,288,1152]{2,1,0:T(8,128)}, f32[4,288,729]{2,1,0:T(8,128)}, /*index=5*/f32[4,288,729]{2,1,0:T(8,128)}) custom-call(s32[2]{0:T(128)S(1)} %pad_add_fusion.at, bf16[2,272,1152]{2,1,0:T(8,128)(2,1)S(1)} %copy-done, ...), custom_call_target="tpu_custom_call" | custom-call | tf_op jit(solution)/shard_map/finish/pallas_call | solution.py:1653
  397.4 0.7 slice.46
  398.2 0.7 dynamic-slice_reduce_fusion
  (23 shorter events, 0.2 us)
Async XLA Ops:
  0.6 4.3 %copy-start.11 = (bf16[288,1152]{1,0:T(8,128)(2,1)S(1)}, bf16[288,1152]{1,0:T(8,128)(2,1)}, u32[]{:S(2)}) copy-start(bf16[288,1152]{1,0:T(8,128)(2,1)} %param.21) | copy-start | bytes 1990660
  2.5 4.2 %copy-start.5 = (f32[8,1,768]{2,1,0:T(1,128)}, f32[8,1,768]{2,1,0:T(1,128)S(1)}, u32[]{:S(2)}) copy-start(f32[8,1,768]{2,1,0:T(1,128)S(1)} %maximum_convert_fusion.row_ref.refs_3_) | copy-start | bytes 73732
  4.9 1.7 copy-start.12
  5.0 1.7 copy-start.13
  6.7 23.1 %copy-start.10 = (bf16[1152,1076]{0,1:T(8,128)(2,1)S(1)}, bf16[1152,1076]{0,1:T(8,128)(2,1)}, u32[]{:S(2)}) copy-start(bf16[1152,1076]{0,1:T(8,128)(2,1)} %param.25) | copy-start | bytes 7437316
  29.8 2.0 copy-start.6
  29.8 2.5 copy-start.7
  29.8 2.5 copy-start.8
  29.8 2.4 copy-start.9
  29.8 2.4 copy-start.14
  29.8 2.4 copy-start.15
  29.8 2.5 copy-start.16
  29.9 2.5 copy-start.17
  379.3 1.3 copy-start
  380.6 1.2 copy-start.1
  381.8 1.2 copy-start.2
  383.0 1.0 copy-start.3
  384.0 1.0 copy-start.4
